TPU v7x, 256 devices: a whole 4x4x8 slice. The times are simulated.
256 devices in a mesh: table: 128 (over x, z, y), dp: 2 (over core).
Axes of the slice: x: 4, y: 4, z: 8, core: 2. Of those that a mesh axis runs over, the one named last changes fastest.
Arguments:
- tables: bfloat16 [4, 524288, 128], P(None, 'table'), may hold values from -6 to 6
- owner_ids: int32 [256, 4, 256, 1], P(('table', 'dp')), may hold values from 0 to 127; in each aligned block of 256 rows (0 to 255, 256 to 511, ..., all dimensions but the last counted through in order) at most 4 rows name the same one
- row_ids: int32 [256, 4, 256], P(('table', 'dp')), may hold values from 0 to 4095
- session_of: int32 [256, 256], P(('table', 'dp')), may hold values from 0 to 1, never falling along the last dimension, each value on 1 to 200 neighbouring positions
- relevance: float32 [256, 256], P(('table', 'dp')), may hold values from 0.1 to 10
- logit_bias: float32 [256, 256], P(('table', 'dp')), may hold values from -400 to 400
- w_hidden: float32 [512, 512], replicated, may hold values from -0.25 to 0.25
- bias_hidden: float32 [512], replicated, may hold values from -3 to 3
- w_score: float32 [512], replicated, may hold values from -0.9 to 0.9
Outputs:
- emb_step: float32 [4, 524288, 128], P(None, ('table', 'dp'))
- step_hidden: float32 [512, 512], replicated
- step_bias: float32 [512], replicated
- step_score: float32 [512], replicated
- loss: float32 [], replicated
Inputs may be any that keep to these rules, and one draw needn't show every extreme that they name: `owner_ids`: among one device's impressions, for one table, at most 4 name the same owner. `session_of`: session numbers never fall along a device's impressions; each of a device's 2 sessions has 1 to 200 impressions.
All inputs are finite; a program needn't handle non-finite values.
Results may differ from a plain program's by a relative error of at most 0.001.
The roundings to bfloat16 on the way count: a program that leaves them out, or rounds other values in their place, can miss the bound.
Values may be sent and summed in bfloat16 or wider, within the bound.
No kernel may reach another device: no remote copies, remote signals or barrier semaphores. Data moves between devices by JAX's collectives and lax.ppermute only.
A program may use at most 64 MiB of HBM per device.

v0:
```python
import jax
import jax.numpy as jnp
from jax import lax
from jax.experimental import pallas as pl
from jax.experimental.pallas import tpu as pltpu
from jax.sharding import Mesh
from jax.sharding import PartitionSpec as P


TABLE = ("x", "z", "y")
ALL = ("x", "z", "y", "dp")
TABLES = 4
CAP = 4
LINES = TABLES * CAP
OWNERS = 128
IMPS = 256
EMB = 128
ROWS = 4096
HID = 512
DENSE = 2 * HID + 128
VMEM = pl.BlockSpec(memory_space=pltpu.VMEM)
ANY = pl.BlockSpec(memory_space=pl.ANY)
BF = jnp.bfloat16
F32 = jnp.float32


def iota(shape, dim):
    return lax.broadcasted_iota(jnp.int32, shape, dim)


def hot_rows(low, block, blocks):
    n = low.shape[0]
    one = jnp.where(iota((n, 128), 1) == low, 1.0, 0.0).astype(BF)
    which = jnp.broadcast_to(block, (n, 128)).astype(F32).astype(BF)
    zero = jnp.zeros((n, 128), BF)
    return jnp.concatenate([jnp.where(which == BF(c), one, zero) for c in range(blocks)], axis=1)


def hot_cols(low, block, blocks):
    n = low.shape[1]
    one = jnp.where(iota((128, n), 0) == low, 1.0, 0.0).astype(BF)
    which = jnp.broadcast_to(block, (128, n)).astype(F32).astype(BF)
    zero = jnp.zeros((128, n), BF)
    return jnp.concatenate([jnp.where(which == BF(c), one, zero) for c in range(blocks)], axis=0)


def slots_kernel(own_ref, row_ref, want_ref, slot_ref, slot_col_ref):
    own = own_ref[...]
    own_rows = [
        jnp.concatenate([own[2 * t : 2 * t + 1], own[2 * t + 1 : 2 * t + 2]], axis=1)
        for t in range(TABLES)
    ]
    own_cols = jnp.transpose(jnp.concatenate(own_rows + own_rows, axis=0))
    row_cols = jnp.transpose(jnp.concatenate([row_ref[...], row_ref[...]], axis=0))
    before = iota((IMPS, IMPS), 0) < iota((IMPS, IMPS), 1)
    slots = []
    for t in range(TABLES):
        same = (own_cols[:, t : t + 1] == own_rows[t]) & before
        rank = jnp.sum(jnp.where(same, 1, 0), axis=0, keepdims=True)
        slots.append(own_rows[t] * LINES + (CAP * t) + rank)
    slot_ref[...] = jnp.concatenate(slots, axis=0)
    slot_cols = jnp.transpose(jnp.concatenate(slots + slots, axis=0))
    slot_col_ref[...] = slot_cols
    lines = []
    for t in range(TABLES):
        slot = jnp.broadcast_to(slot_cols[:, t : t + 1], (IMPS, OWNERS))
        row = jnp.broadcast_to(row_cols[:, t : t + 1], (IMPS, OWNERS))
        for r in range(CAP):
            target = iota((IMPS, OWNERS), 1) * LINES + (CAP * t + r)
            lines.append(jnp.sum(jnp.where(slot == target, row, 0), axis=0, keepdims=True))
    want_ref[...] = jnp.transpose(jnp.concatenate(lines, axis=0))


def serve_kernel(req_ref, far_ref, out_ref, wide_ref, tab_ref, sems):
    copies = [pltpu.make_async_copy(far_ref.at[t], tab_ref.at[t], sems.at[t]) for t in range(TABLES)]
    for copy in copies:
        copy.start()
    req = req_ref[...]
    half = ROWS // 2
    for t in range(TABLES):
        copies[t].wait()
        table = jnp.concatenate([tab_ref[t, :half, :], tab_ref[t, half:, :]], axis=1)
        rows = [req[:, CAP * t + r : CAP * t + r + 1] for r in range(CAP)]
        hot = jnp.concatenate([hot_rows(row & 127, (row >> 7) & 15, 16) for row in rows], axis=0)
        both = jnp.dot(hot, table, preferred_element_type=F32)
        for r in range(CAP):
            upper = jnp.broadcast_to(rows[r], (OWNERS, EMB)) >= half
            mine = both[r * OWNERS : (r + 1) * OWNERS]
            wide_ref[pl.ds(CAP * t + r, OWNERS, stride=LINES), :] = jnp.where(
                upper, mine[:, EMB:], mine[:, :EMB]
            )
    out_ref[...] = wide_ref[...].astype(BF).reshape(OWNERS, LINES, EMB)


def step_kernel(
    core_ref, ret_ref, slot_ref, slot_col_ref, ses_ref, rel_ref, lb_ref, w_ref, b_ref, ws_ref,
    out_ref, keep_ref, send_ref, dense_ref,
):
    back = ret_ref[...].reshape(OWNERS * LINES, EMB)
    half = OWNERS * LINES // 2
    source = jnp.concatenate([back[:half], back[half:]], axis=1)
    slot_cols = slot_col_ref[...]
    pieces = []
    picks = []
    for t in range(TABLES):
        slot = slot_cols[:, t : t + 1]
        picks.append(hot_rows(slot & 127, (slot >> 7) & 7, 8))
    found = jnp.dot(jnp.concatenate(picks, axis=0), source, preferred_element_type=F32)
    for t in range(TABLES):
        both = found[t * IMPS : (t + 1) * IMPS]
        upper = jnp.broadcast_to(slot_cols[:, t : t + 1], (IMPS, EMB)) >= half
        pieces.append(jnp.where(upper, both[:, EMB:], both[:, :EMB]).astype(BF))
    inputs = jnp.concatenate(pieces, axis=1)
    w_bf = w_ref[...].astype(BF)
    w_score = ws_ref[...]
    pre = jnp.dot(inputs, w_bf, preferred_element_type=F32) + b_ref[...]
    sig = jax.nn.sigmoid(pre)
    hidden = pre * sig
    aux = jnp.transpose(
        jnp.concatenate(
            [rel_ref[...], lb_ref[...], ses_ref[...].astype(F32)] + [rel_ref[...]] * 5, axis=0
        )
    )
    relevance, bias_col, session = aux[:, 0:1], aux[:, 1:2], aux[:, 2:3]
    scores = jnp.sum(hidden * w_score, axis=1, keepdims=True) + bias_col
    first = session < 0.5
    low = jnp.float32(-jnp.inf)
    top = [jnp.max(jnp.where(m, scores, low), axis=0, keepdims=True) for m in (first, ~first)]
    shifted = scores - jnp.where(first, top[0], top[1])
    exponent = jnp.exp(shifted)
    total = [jnp.sum(jnp.where(m, exponent, 0.0), axis=0, keepdims=True) for m in (first, ~first)]
    weight = [jnp.sum(jnp.where(m, relevance, 0.0), axis=0, keepdims=True) for m in (first, ~first)]
    probability = exponent / jnp.where(first, total[0], total[1])
    target = relevance / jnp.where(first, weight[0], weight[1])
    loss = jnp.log(total[0]) + jnp.log(total[1]) - jnp.sum(target * shifted, axis=0, keepdims=True)
    score_grad = probability - target
    pre_grad = score_grad * w_score * (sig * (1.0 + pre * (1.0 - sig)))
    pre_grad_bf = pre_grad.astype(BF)
    grad = jnp.dot(pre_grad_bf, w_bf.T, preferred_element_type=F32).astype(BF)
    slots = slot_ref[...]
    values, hots = [], []
    for t in range(TABLES):
        slot = slots[t : t + 1]
        hots.append(hot_cols(slot & 127, (slot >> 7) & 7, 8))
        piece = grad[:, t * EMB : (t + 1) * EMB]
        upper = jnp.broadcast_to(slot_cols[:, t : t + 1], (IMPS, EMB)) >= half
        zero = jnp.zeros((IMPS, EMB), BF)
        values.append(
            jnp.concatenate([jnp.where(upper, zero, piece), jnp.where(upper, piece, zero)], axis=1)
        )
    placed = jnp.dot(
        jnp.concatenate(hots, axis=1), jnp.concatenate(values, axis=0), preferred_element_type=F32
    )
    out_ref[: OWNERS // 2] = placed[:, :EMB].astype(BF).reshape(OWNERS // 2, LINES, EMB)
    out_ref[OWNERS // 2 :] = placed[:, EMB:].astype(BF).reshape(OWNERS // 2, LINES, EMB)
    weight_grad = lax.dot_general(
        inputs, pre_grad_bf, (((0,), (0,)), ((), ())), preferred_element_type=F32
    )
    dense_ref[:, 0:HID] = weight_grad[:256]
    dense_ref[:, HID : 2 * HID] = weight_grad[256:]
    bias_grad = jnp.sum(pre_grad, axis=0, keepdims=True)
    score_w_grad = jnp.sum(score_grad * hidden, axis=0, keepdims=True)
    dense_ref[:, 2 * HID :] = jnp.zeros((256, 128), F32)
    for k in range(4):
        dense_ref[k : k + 1, 2 * HID :] = bias_grad[:, 128 * k : 128 * (k + 1)]
        dense_ref[4 + k : 5 + k, 2 * HID :] = score_w_grad[:, 128 * k : 128 * (k + 1)]
    dense_ref[8:9, 2 * HID :] = jnp.broadcast_to(loss, (1, 128))
    start = pl.multiple_of(core_ref[0] * 128, 128)
    keep_ref[...] = dense_ref[pl.ds(start, 128), :]
    send_ref[...] = dense_ref[pl.ds(128 - start, 128), :]


def place_kernel(
    core_ref, own_ref, other_ref, own_id_ref, other_id_ref, out_ref, wide_ref, buf_ref, sems
):
    core = core_ref[0]
    lines = OWNERS * LINES
    wide_ref[:lines] = own_ref[...].reshape(lines, EMB).astype(F32)
    wide_ref[lines:] = other_ref[...].reshape(lines, EMB).astype(F32)
    cols = [own_id_ref[...], other_id_ref[...]]
    rows = [jnp.transpose(c) for c in cols]
    copies = []
    for t in range(TABLES):
        values, hots = [], []
        for s in range(2):
            for r in range(CAP):
                j = CAP * t + r
                line = wide_ref[pl.ds(s * lines + j, OWNERS, stride=LINES), :]
                quarter = jnp.broadcast_to(cols[s][:, j : j + 1] >> 10, (OWNERS, EMB)) - 2 * core
                values.append(
                    jnp.concatenate(
                        [jnp.where(quarter == 0, line, 0.0), jnp.where(quarter == 1, line, 0.0)],
                        axis=1,
                    ).astype(BF)
                )
                row = rows[s][j : j + 1]
                hots.append(hot_cols(row & 127, (row >> 7) & 7, 8))
        total = jnp.dot(
            jnp.concatenate(hots, axis=1), jnp.concatenate(values, axis=0), preferred_element_type=F32
        )
        for h in range(2):
            x = total[:, h * EMB : (h + 1) * EMB]
            mean = jnp.sum(x * x, axis=1, keepdims=True) * (1.0 / EMB)
            buf_ref[t, 1024 * h : 1024 * (h + 1)] = x * (1.0 / (jnp.sqrt(mean) + 1e-06))
        copy = pltpu.make_async_copy(buf_ref.at[t], out_ref.at[t], sems.at[t])
        copy.start()
        copies.append(copy)
    for copy in copies:
        copy.wait()


def final_kernel(core_ref, own_ref, other_ref, w_ref, b_ref, s_ref, loss_ref, dense_ref):
    start = pl.multiple_of(core_ref[0] * 128, 128)
    dense_ref[pl.ds(start, 128), :] = own_ref[...]
    dense_ref[pl.ds(128 - start, 128), :] = other_ref[...]
    main = dense_ref[:, : 2 * HID]
    small = dense_ref[0:8, 2 * HID :]
    square = jnp.sum(jnp.sum(main * main, axis=0, keepdims=True), axis=1, keepdims=True) + jnp.sum(
        jnp.sum(small * small, axis=0, keepdims=True), axis=1, keepdims=True
    )
    factor = 1.0 / jnp.sqrt(square * (1.0 / (HID * HID + 2 * HID)) + 1e-06)
    w_ref[:256] = main[:, :HID] * factor
    w_ref[256:] = main[:, HID:] * factor
    b_ref[...] = small[0:4] * factor
    s_ref[...] = small[4:8] * factor
    loss_ref[...] = dense_ref[8:9, 2 * HID :] * (1.0 / 512)


def sds(shape, dtype):
    return jax.ShapeDtypeStruct(shape, dtype)


def cost(flops, moved):
    return pl.CostEstimate(flops=flops, bytes_accessed=moved, transcendentals=0)


def whole_step(
    tables, owner_ids, row_ids, session_of, relevance, logit_bias, w_hidden, bias_hidden, w_score
):
    core = lax.axis_index("dp").astype(jnp.int32).reshape(1)
    swap = [(0, 1), (1, 0)]
    smem = pl.BlockSpec(memory_space=pltpu.SMEM)
    wanted, slots, slot_cols = pl.pallas_call(
        slots_kernel,
        out_shape=(
            sds((OWNERS, LINES), jnp.int32),
            sds((TABLES, IMPS), jnp.int32),
            sds((IMPS, 2 * TABLES), jnp.int32),
        ),
        in_specs=[VMEM, VMEM],
        out_specs=(VMEM, VMEM, VMEM),
        cost_estimate=cost(1 << 20, 1 << 16),
        compiler_params=pltpu.CompilerParams(vmem_limit_bytes=8 << 20),
        name="slots",
    )(owner_ids.reshape(8, 128), row_ids.reshape(TABLES, IMPS))
    requested = lax.all_to_all(wanted, TABLE, split_axis=0, concat_axis=0, tiled=True)
    other_ids = lax.ppermute(requested, "dp", swap)
    served = pl.pallas_call(
        serve_kernel,
        out_shape=sds((OWNERS, LINES, EMB), BF),
        in_specs=[VMEM, pl.BlockSpec(memory_space=pltpu.HBM)],
        out_specs=VMEM,
        scratch_shapes=[
            pltpu.VMEM((OWNERS * LINES, EMB), F32),
            pltpu.VMEM((TABLES, ROWS, EMB), BF),
            pltpu.SemaphoreType.DMA((TABLES,)),
        ],
        cost_estimate=cost(4 << 30, 5 << 20),
        compiler_params=pltpu.CompilerParams(vmem_limit_bytes=61 << 20),
        name="serve",
    )(requested, tables)
    returned = lax.all_to_all(served, TABLE, split_axis=0, concat_axis=0, tiled=True)
    outgoing, keep, send = pl.pallas_call(
        step_kernel,
        out_shape=(
            sds((OWNERS, LINES, EMB), BF), sds((128, DENSE), F32), sds((128, DENSE), F32),
        ),
        in_specs=[smem] + [VMEM] * 9,
        out_specs=(VMEM,) * 3,
        scratch_shapes=[pltpu.VMEM((256, DENSE), F32)],
        cost_estimate=cost(3 << 30, 3 << 20),
        compiler_params=pltpu.CompilerParams(vmem_limit_bytes=24 << 20),
        name="step",
    )(
        core, returned, slots, slot_cols, session_of, relevance, logit_bias, w_hidden,
        bias_hidden.reshape(1, HID), w_score.reshape(1, HID),
    )
    incoming = lax.all_to_all(outgoing, TABLE, split_axis=0, concat_axis=0, tiled=True)
    chip = keep + lax.ppermute(send, "dp", swap)
    plane = lax.all_to_all(
        chip.reshape(16, 8, DENSE), ("x", "y"), split_axis=0, concat_axis=0, tiled=True
    ).sum(axis=0)
    total = lax.all_to_all(
        jnp.broadcast_to(plane[None], (8, 8, DENSE)), "z", split_axis=0, concat_axis=0, tiled=True
    ).sum(axis=0)
    mine = lax.all_to_all(
        jnp.broadcast_to(total[None], (16, 8, DENSE)), ("x", "y"),
        split_axis=0, concat_axis=0, tiled=True,
    ).reshape(128, DENSE)
    theirs = lax.ppermute(mine, "dp", swap)
    other = lax.ppermute(incoming, "dp", swap)
    emb_step = pl.pallas_call(
        place_kernel,
        out_shape=sds((TABLES, ROWS // 2, EMB), F32),
        in_specs=[smem] + [VMEM] * 4,
        out_specs=ANY,
        scratch_shapes=[
            pltpu.VMEM((2 * OWNERS * LINES, EMB), F32),
            pltpu.VMEM((TABLES, ROWS // 2, EMB), F32),
            pltpu.SemaphoreType.DMA((TABLES,)),
        ],
        cost_estimate=cost(4 << 30, 5 << 20),
        compiler_params=pltpu.CompilerParams(vmem_limit_bytes=28 << 20),
        name="place",
    )(core, incoming, other, requested, other_ids)
    step_hidden, step_bias, step_score, loss = pl.pallas_call(
        final_kernel,
        out_shape=(
            sds((HID, HID), F32), sds((4, 128), F32), sds((4, 128), F32), sds((1, 128), F32),
        ),
        in_specs=[smem, VMEM, VMEM],
        out_specs=(VMEM,) * 4,
        scratch_shapes=[pltpu.VMEM((256, DENSE), F32)],
        cost_estimate=cost(1 << 20, 2 << 20),
        compiler_params=pltpu.CompilerParams(vmem_limit_bytes=12 << 20),
        name="final",
    )(core, mine, theirs)
    return emb_step, step_hidden, step_bias.reshape(HID), step_score.reshape(HID), loss[0, 0]


def solution(mesh):
    split = Mesh(mesh.devices.reshape(4, 8, 4, mesh.shape["dp"]), ALL)
    return jax.shard_map(
        whole_step,
        mesh=split,
        in_specs=(
            P(None, TABLE, None),
            P(ALL, None, None, None),
            P(ALL, None, None),
            P(ALL, None),
            P(ALL, None),
            P(ALL, None),
            P(),
            P(),
            P(),
        ),
        out_specs=(P(None, ALL, None), P(), P(), P(), P()),
        check_vma=False,
    )
```

profile of v0, /device:TPU:1, one launch (start us, length us, event | category | flops | bytes accessed | tf_op | source)
XLA Modules:
  0.0 151.5 jit_solution(16812675629523278932)
XLA Ops:
  0.6 0.0 copy-start.1
  0.6 0.7 copy-done.1
  1.3 0.0 copy-start.2
  1.3 0.7 copy-done.2
  2.0 1.1 slots.1
  3.1 27.1 %all_to_all.36 = s32[128,1,16]{2,1,0:T(1,128)} all-to-all(s32[128,1,16]{2,1,0:T(1,128)S(1)} %bitcast.21), channel_id=1, replica_groups=mesh['x'=4,'z'=8,'y'=4,'dp'=2] {'x','z','y'}, dimensions={0} | all-to-all | bytes 16384 | tf_op jit(solution)/shard_map/all_to_all | solution.py:256
  30.2 0.0 copy-start.3
  30.2 0.0 copy-start.4
  30.2 0.0 copy-start.5
  30.2 0.0 copy-start.6
  30.2 0.0 copy-start.7
  30.2 0.0 copy-start.8
  30.2 8.2 %serve.1 = bf16[128,16,128]{2,1,0:T(8,128)(2,1)} custom-call(s32[128,16]{1,0:T(8,128)} %bitcast.18, bf16[4,4096,128]{2,1,0:T(8,128)(2,1)} %far_ref.1), custom_call_target="tpu_custom_call" | custom-call | flops 4294967296 | bytes 5242880 | tf_op jit(solution)/shard_map/serve/pallas_call | solution.py:258
  38.4 6.2 %all-to-all-start.1 = ((bf16[128,16,128]{2,1,0:T(8,128)(2,1)}), bf16[128,16,128]{2,1,0:T(8,128)(2,1)S(1)}, u32[]{:S(2)}, u32[]{:S(2)}) async-start(bf16[128,16,128]{2,1,0:T(8,128)(2,1)} %serve.1), calls=%async_computation.1 | async-start | bytes 1048576 | tf_op jit(solution)/shard_map/all_to_all | solution.py:272
  44.6 16.1 %all-to-all-done.1.ret_ref = bf16[128,16,128]{2,1,0:T(8,128)(2,1)S(1)} async-done(((bf16[128,16,128]{2,1,0:T(8,128)(2,1)}), bf16[128,16,128]{2,1,0:T(8,128)(2,1)S(1)}, u32[]{:S(2)}, u32[]{:S(2)}) %all-to-all-start.1) | async-done | bytes 524320 | tf_op jit(solution)/shard_map/all_to_all | solution.py:272
  60.7 0.0 copy-done.3
  60.7 0.0 copy-done.4
  60.7 0.0 copy-done.5
  60.7 0.0 copy-done.6
  60.7 0.0 copy-done.7
  60.7 0.0 copy-done.8
  60.7 4.4 %step.1 = (bf16[128,16,128]{2,1,0:T(8,128)(2,1)}, f32[128,1152]{1,0:T(8,128)S(1)}, f32[128,1152]{1,0:T(8,128)S(1)}) custom-call(s32[1]{0:T(128)} %bitcast.core_ref, bf16[128,16,128]{2,1,0:T(8,128)(2,1)S(1)} %all-to-all-done.1.ret_ref, s32[4,256]{1,0:T(4,128)S(1)} %get-tuple-element.16.slot_ref, s32[256,8]{1,0:T(8,128)S(1)} %get-tuple-element.17.slot_col_ref, ...), custom_call_target="tpu_custom_call" | custom-call | flops 3221225472 | bytes 3145728 | tf_op jit(solution)/shard_map/step/pallas_call | solution.py:273
  65.1 0.0 copy-start
  65.1 4.2 %collective-permute-start.2 = (f32[128,1152]{1,0:T(8,128)S(1)}, f32[128,1152]{1,0:T(8,128)S(1)}, u32[]{:S(2)}, u32[]{:S(2)}) collective-permute-start(f32[128,1152]{1,0:T(8,128)S(1)} %get-tuple-element.20), channel_id=1, source_target_pairs={{0,1},{1,0},{2,3},{3,2},{4,5},{5,4},{6,7},{7,6},{8,9},{9,8},{10,11... | collective-permute-start | bytes 1769480 | tf_op jit(solution)/shard_map/ppermute | solution.py:289
  69.3 1.6 %collective-permute-done.2 = f32[128,1152]{1,0:T(8,128)S(1)} collective-permute-done((f32[128,1152]{1,0:T(8,128)S(1)}, f32[128,1152]{1,0:T(8,128)S(1)}, u32[]{:S(2)}, u32[]{:S(2)}) %collective-permute-start.2) | collective-permute-done | bytes 589856 | tf_op jit(solution)/shard_map/ppermute | solution.py:289
  70.9 0.1 add_bitcast_fusion
  71.0 15.4 %all_to_all.37 = f32[16,8,1152]{2,1,0:T(8,128)S(1)} all-to-all(f32[16,8,1152]{2,1,0:T(8,128)S(1)} %add_bitcast_fusion), channel_id=1, replica_groups=mesh['x'=4,'z'=8,'y'=4,'dp'=2] {'x','y'}, dimensions={0} | all-to-all | bytes 1179648 | tf_op jit(solution)/shard_map/all_to_all | solution.py:290
  86.4 12.8 %all_to_all.38 = f32[8,8,1152]{2,1,0:T(8,128)S(1)} all-to-all(f32[8,8,1152]{2,1,0:T(8,128)S(1)} %broadcast_in_dim.4), channel_id=1, replica_groups=mesh['x'=4,'z'=8,'y'=4,'dp'=2] {'z'}, dimensions={0} | all-to-all | bytes 589824 | tf_op jit(solution)/shard_map/all_to_all | solution.py:293
  99.3 7.2 %all-to-all-start.2 = ((bf16[128,16,128]{2,1,0:T(8,128)(2,1)}), bf16[128,16,128]{2,1,0:T(8,128)(2,1)S(1)}, u32[]{:S(2)}, u32[]{:S(2)}) async-start(bf16[128,16,128]{2,1,0:T(8,128)(2,1)} %get-tuple-element.18), calls=%async_computation.2 | async-start | bytes 1048576 | tf_op jit(solution)/shard_map/all_to_all | solution.py:288
  106.5 15.9 %all-to-all-done.2.own_ref = bf16[128,16,128]{2,1,0:T(8,128)(2,1)S(1)} async-done(((bf16[128,16,128]{2,1,0:T(8,128)(2,1)}), bf16[128,16,128]{2,1,0:T(8,128)(2,1)S(1)}, u32[]{:S(2)}, u32[]{:S(2)}) %all-to-all-start.2) | async-done | bytes 524320 | tf_op jit(solution)/shard_map/all_to_all | solution.py:288
  122.4 0.9 broadcast_in_dim.5
  123.2 4.8 %all-to-all-start.5 = ((f32[16,8,1152]{2,1,0:T(8,128)}), f32[16,8,1152]{2,1,0:T(8,128)S(1)}, u32[]{:S(2)}, u32[]{:S(2)}) async-start(f32[16,8,1152]{2,1,0:T(8,128)} %broadcast_in_dim.5), calls=%async_computation.5 | async-start | bytes 1179648 | tf_op jit(solution)/shard_map/all_to_all | solution.py:296
  128.0 4.0 %collective-permute-start = (bf16[128,16,128]{2,1,0:T(8,128)(2,1)S(1)}, bf16[128,16,128]{2,1,0:T(8,128)(2,1)S(1)}, u32[]{:S(2)}, u32[]{:S(2)}) collective-permute-start(bf16[128,16,128]{2,1,0:T(8,128)(2,1)S(1)} %all-to-all-done.2.own_ref), channel_id=1, source_target_pairs={{0,1},{1,0},{2,3},{3,2},{4,5},{5,4},{6,7},{7,6},{8,9},{9,8},{10,11... | collective-permute-start | bytes 1572872 | tf_op jit(solution)/shard_map/ppermute | solution.py:301
  132.0 5.4 %all-to-all-done.5 = f32[16,8,1152]{2,1,0:T(8,128)S(1)} async-done(((f32[16,8,1152]{2,1,0:T(8,128)}), f32[16,8,1152]{2,1,0:T(8,128)S(1)}, u32[]{:S(2)}, u32[]{:S(2)}) %all-to-all-start.5) | async-done | bytes 589856 | tf_op jit(solution)/shard_map/all_to_all | solution.py:296
  137.4 5.0 %collective-permute-start.3 = (f32[128,1152]{1,0:T(8,128)S(1)}, f32[128,1152]{1,0:T(8,128)S(1)}, u32[]{:S(2)}, u32[]{:S(2)}) collective-permute-start(f32[128,1152]{1,0:T(8,128)S(1)} %bitcast.16), channel_id=1, source_target_pairs={{0,1},{1,0},{2,3},{3,2},{4,5},{5,4},{6,7},{7,6},{8,9},{9,8},{10,11... | collective-permute-start | bytes 1769480 | tf_op jit(solution)/shard_map/ppermute | solution.py:300
  142.4 0.0 copy-done
  142.4 0.0 collective-permute-start.1
  142.4 1.7 %collective-permute-done.1.other_id_ref = s32[128,16]{1,0:T(8,128)S(1)} collective-permute-done((s32[128,16]{1,0:T(8,128)S(1)}, s32[128,16]{1,0:T(8,128)S(1)}, u32[]{:S(2)}, u32[]{:S(2)}) %collective-permute-start.1) | collective-permute-done | bytes 8224 | tf_op jit(solution)/shard_map/ppermute | solution.py:257
  144.1 0.0 collective-permute-done.other_ref
  144.1 6.0 %place.1 = f32[4,2048,128]{2,1,0:T(8,128)} custom-call(s32[1]{0:T(128)} %bitcast.core_ref, bf16[128,16,128]{2,1,0:T(8,128)(2,1)S(1)} %all-to-all-done.2.own_ref, bf16[128,16,128]{2,1,0:T(8,128)(2,1)S(1)} %collective-permute-done.other_ref, s32[128,16]{1,0:T(8,128)S(1)} %bitcast.20, s32[128,16]{1,0:T(8,128)S(1)} %collective-permute-done.1.other_id_ref), custom_call_target="tpu_custom_call" | custom-call | flops 4294967296 | bytes 5242880 | tf_op jit(solution)/shard_map/place/pallas_call | solution.py:302
  150.2 0.0 collective-permute-done.3.other_ref
  150.2 1.3 final.1
  (3 shorter events, 0.1 us)
Async XLA Ops:
  0.6 0.7 copy-start.1
  1.3 0.7 copy-start.2
  30.2 30.5 %copy-start.3 = (f32[512,512]{1,0:T(8,128)S(1)}, f32[512,512]{1,0:T(8,128)}, u32[]{:S(2)}) copy-start(f32[512,512]{1,0:T(8,128)} %w_ref.1) | copy-start | bytes 3145732
  30.2 30.5 %copy-start.4 = (f32[512]{0:T(512)S(1)}, f32[512]{0:T(512)}, u32[]{:S(2)}) copy-start(f32[512]{0:T(512)} %param.16) | copy-start | bytes 6148
  30.2 30.5 %copy-start.5 = (f32[512]{0:T(512)S(1)}, f32[512]{0:T(512)}, u32[]{:S(2)}) copy-start(f32[512]{0:T(512)} %param.17) | copy-start | bytes 6148
  30.2 30.5 %copy-start.6 = (s32[1,256]{1,0:T(1,128)S(1)}, s32[1,256]{1,0:T(1,128)}, u32[]{:S(2)}) copy-start(s32[1,256]{1,0:T(1,128)} %ses_ref.1) | copy-start | bytes 3076
  30.2 30.5 %copy-start.7 = (f32[1,256]{1,0:T(1,128)S(1)}, f32[1,256]{1,0:T(1,128)}, u32[]{:S(2)}) copy-start(f32[1,256]{1,0:T(1,128)} %rel_ref.1) | copy-start | bytes 3076
  30.2 30.5 %copy-start.8 = (f32[1,256]{1,0:T(1,128)S(1)}, f32[1,256]{1,0:T(1,128)}, u32[]{:S(2)}) copy-start(f32[1,256]{1,0:T(1,128)} %lb_ref.1) | copy-start | bytes 3076
  38.4 22.3 %all-to-all-start.1 = ((bf16[128,16,128]{2,1,0:T(8,128)(2,1)}), bf16[128,16,128]{2,1,0:T(8,128)(2,1)S(1)}, u32[]{:S(2)}, u32[]{:S(2)}) async-start(bf16[128,16,128]{2,1,0:T(8,128)(2,1)} %serve.1), calls=%async_computation.1 | async-start | bytes 1048576 | tf_op jit(solution)/shard_map/all_to_all | solution.py:272
  65.1 77.3 %copy-start = (s32[128,1,16]{2,1,0:T(1,128)S(1)}, s32[128,1,16]{2,1,0:T(1,128)}, u32[]{:S(2)}) copy-start(s32[128,1,16]{2,1,0:T(1,128)} %all_to_all.36) | copy-start | bytes 24580
  65.1 5.9 %collective-permute-start.2 = (f32[128,1152]{1,0:T(8,128)S(1)}, f32[128,1152]{1,0:T(8,128)S(1)}, u32[]{:S(2)}, u32[]{:S(2)}) collective-permute-start(f32[128,1152]{1,0:T(8,128)S(1)} %get-tuple-element.20), channel_id=1, source_target_pairs={{0,1},{1,0},{2,3},{3,2},{4,5},{5,4},{6,7},{7,6},{8,9},{9,8},{10,11... | collective-permute-start | bytes 1769480 | tf_op jit(solution)/shard_map/ppermute | solution.py:289
  99.3 23.1 %all-to-all-start.2 = ((bf16[128,16,128]{2,1,0:T(8,128)(2,1)}), bf16[128,16,128]{2,1,0:T(8,128)(2,1)S(1)}, u32[]{:S(2)}, u32[]{:S(2)}) async-start(bf16[128,16,128]{2,1,0:T(8,128)(2,1)} %get-tuple-element.18), calls=%async_computation.2 | async-start | bytes 1048576 | tf_op jit(solution)/shard_map/all_to_all | solution.py:288
  123.2 14.2 %all-to-all-start.5 = ((f32[16,8,1152]{2,1,0:T(8,128)}), f32[16,8,1152]{2,1,0:T(8,128)S(1)}, u32[]{:S(2)}, u32[]{:S(2)}) async-start(f32[16,8,1152]{2,1,0:T(8,128)} %broadcast_in_dim.5), calls=%async_computation.5 | async-start | bytes 1179648 | tf_op jit(solution)/shard_map/all_to_all | solution.py:296
  128.0 16.1 %collective-permute-start = (bf16[128,16,128]{2,1,0:T(8,128)(2,1)S(1)}, bf16[128,16,128]{2,1,0:T(8,128)(2,1)S(1)}, u32[]{:S(2)}, u32[]{:S(2)}) collective-permute-start(bf16[128,16,128]{2,1,0:T(8,128)(2,1)S(1)} %all-to-all-done.2.own_ref), channel_id=1, source_target_pairs={{0,1},{1,0},{2,3},{3,2},{4,5},{5,4},{6,7},{7,6},{8,9},{9,8},{10,11... | collective-permute-start | bytes 1572872 | tf_op jit(solution)/shard_map/ppermute | solution.py:301
  137.4 12.8 %collective-permute-start.3 = (f32[128,1152]{1,0:T(8,128)S(1)}, f32[128,1152]{1,0:T(8,128)S(1)}, u32[]{:S(2)}, u32[]{:S(2)}) collective-permute-start(f32[128,1152]{1,0:T(8,128)S(1)} %bitcast.16), channel_id=1, source_target_pairs={{0,1},{1,0},{2,3},{3,2},{4,5},{5,4},{6,7},{7,6},{8,9},{9,8},{10,11... | collective-permute-start | bytes 1769480 | tf_op jit(solution)/shard_map/ppermute | solution.py:300
  142.4 1.7 %collective-permute-start.1 = (s32[128,16]{1,0:T(8,128)S(1)}, s32[128,16]{1,0:T(8,128)S(1)}, u32[]{:S(2)}, u32[]{:S(2)}) collective-permute-start(s32[128,16]{1,0:T(8,128)S(1)} %bitcast.19), channel_id=1, source_target_pairs={{0,1},{1,0},{2,3},{3,2},{4,5},{5,4},{6,7},{7,6},{8,9},{9,8},{10,11... | collective-permute-start | bytes 24584 | tf_op jit(solution)/shard_map/ppermute | solution.py:257
where the time goes:
time: 152 us; the launch traced here: 151 us
  blocking collectives  55.3 us (36%)
  waiting for transfers between devices  40.6 us (27%)
  starting transfers between devices  31.4 us (21%)
  Pallas kernels  20.9 us (14%)
  local copies, waits for them, and re-layouts  2.27 us (1%)
    all_to_all x1, blocking collectives, whole_step(): lax.all_to_all(wanted, TABLE, split_axis=0, concat_axis=0, tiled=True)  27.1 us
    all_to_all x1, waiting for transfers between devices, whole_step(): lax.all_to_all(served, TABLE, split_axis=0, concat_axis=0, tiled=True)  16.1 us
    all_to_all x1, waiting for transfers between devices, whole_step(): lax.all_to_all(outgoing, TABLE, split_axis=0, concat_axis=0, tiled=True)  15.9 us
    all_to_all x1, blocking collectives, whole_step(): lax.all_to_all(chip.reshape(16, 8, DENSE), ('x', 'y'), split_axis=0, conc...  15.4 us
    all_to_all x1, blocking collectives, whole_step(): lax.all_to_all(jnp.broadcast_to(plane[None], (8, 8, DENSE)), 'z', split_a...  12.8 us
    pallas_call x1, Pallas kernels, whole_step(): pl.pallas_call(serve_kernel, out_shape=sds((OWNERS, LINES, EMB), BF), in_...  8.19 us
    all_to_all x1, starting transfers between devices, whole_step(): lax.all_to_all(outgoing, TABLE, split_axis=0, concat_axis=0, tiled=True)  7.23 us
    all_to_all x1, starting transfers between devices, whole_step(): lax.all_to_all(served, TABLE, split_axis=0, concat_axis=0, tiled=True)  6.19 us
  transfers between devices with their start and end apart: 7, of which 5 were waited for; matrix products, arithmetic and copies ran while one was open for 0% of the time, Pallas kernels for 4%

commit v1 on v0

v1 whole, which is shorter than its diff:
```python
import jax
import jax.numpy as jnp
from jax import lax
from jax.experimental import pallas as pl
from jax.experimental.pallas import tpu as pltpu
from jax.sharding import Mesh
from jax.sharding import PartitionSpec as P


TABLE = ("x", "z", "y")
ALL = ("x", "z", "y", "dp")
TABLES = 4
CAP = 4
LINES = TABLES * CAP
OWNERS = 128
IMPS = 256
EMB = 128
ROWS = 4096
HID = 512
FOLD = 4
SMALL = 16
VMEM = pl.BlockSpec(memory_space=pltpu.VMEM)
ANY = pl.BlockSpec(memory_space=pl.ANY)
BF = jnp.bfloat16
F32 = jnp.float32


HBM = pl.BlockSpec(memory_space=pltpu.HBM)
SMEM = pl.BlockSpec(memory_space=pltpu.SMEM)


def iota(shape, dim):
    return lax.broadcasted_iota(jnp.int32, shape, dim)


def hot_rows(low, block, blocks):
    n = low.shape[0]
    one = jnp.where(iota((n, 128), 1) == low, 1.0, 0.0).astype(BF)
    which = jnp.broadcast_to(block, (n, 128)).astype(F32).astype(BF)
    zero = jnp.zeros((n, 128), BF)
    return jnp.concatenate([jnp.where(which == BF(c), one, zero) for c in range(blocks)], axis=1)


def hot_cols(low, block, blocks):
    n = low.shape[1]
    one = jnp.where(iota((128, n), 0) == low, 1.0, 0.0).astype(BF)
    which = jnp.broadcast_to(block, (128, n)).astype(F32).astype(BF)
    zero = jnp.zeros((128, n), BF)
    return jnp.concatenate([jnp.where(which == BF(c), one, zero) for c in range(blocks)], axis=0)


def chosen(wide, which):
    kept = wide[:, :EMB]
    for f in range(1, FOLD):
        kept = jnp.where(which == f, wide[:, f * EMB : (f + 1) * EMB], kept)
    return kept


def fanned(piece, which):
    zero = jnp.zeros_like(piece)
    return jnp.concatenate([jnp.where(which == f, piece, zero) for f in range(FOLD)], axis=1)


def slots_kernel(own_hbm, row_hbm, want_ref, slot_ref, slot_col_ref, own_ref, row_ref, sems):
    copies = [
        pltpu.make_async_copy(own_hbm, own_ref, sems.at[0]),
        pltpu.make_async_copy(row_hbm, row_ref, sems.at[1]),
    ]
    for copy in copies:
        copy.start()
    for copy in copies:
        copy.wait()
    own = own_ref[...]
    own_rows = [
        jnp.concatenate([own[2 * t : 2 * t + 1], own[2 * t + 1 : 2 * t + 2]], axis=1)
        for t in range(TABLES)
    ]
    own_cols = jnp.transpose(jnp.concatenate(own_rows + own_rows, axis=0))
    row_cols = jnp.transpose(jnp.concatenate([row_ref[...], row_ref[...]], axis=0))
    before = iota((IMPS, IMPS), 0) < iota((IMPS, IMPS), 1)
    slots = []
    for t in range(TABLES):
        same = (own_cols[:, t : t + 1] == own_rows[t]) & before
        rank = jnp.sum(jnp.where(same, 1, 0), axis=0, keepdims=True)
        slots.append(own_rows[t] * LINES + (CAP * t) + rank)
    slot_ref[...] = jnp.concatenate(slots, axis=0)
    slot_cols = jnp.transpose(jnp.concatenate(slots + slots, axis=0))
    slot_col_ref[...] = slot_cols
    lines = []
    for t in range(TABLES):
        slot = jnp.broadcast_to(slot_cols[:, t : t + 1], (IMPS, OWNERS))
        row = jnp.broadcast_to(row_cols[:, t : t + 1], (IMPS, OWNERS))
        for r in range(CAP):
            target = iota((IMPS, OWNERS), 1) * LINES + (CAP * t + r)
            lines.append(jnp.sum(jnp.where(slot == target, row, 0), axis=0, keepdims=True))
    want_ref[...] = jnp.transpose(jnp.concatenate(lines, axis=0))


def serve_kernel(req_ref, far_ref, out_ref, wide_ref, tab_ref, sems):
    copies = [pltpu.make_async_copy(far_ref.at[t], tab_ref.at[t], sems.at[t]) for t in range(TABLES)]
    for copy in copies:
        copy.start()
    req = req_ref[...]
    part = ROWS // FOLD
    for t in range(TABLES):
        rows = [req[:, CAP * t + r : CAP * t + r + 1] for r in range(CAP)]
        hot = jnp.concatenate([hot_rows(row & 127, (row >> 7) & 7, 8) for row in rows], axis=0)
        copies[t].wait()
        table = jnp.concatenate(
            [tab_ref[t, f * part : (f + 1) * part, :] for f in range(FOLD)], axis=1
        )
        wide = jnp.dot(hot, table, preferred_element_type=F32)
        for r in range(CAP):
            which = jnp.broadcast_to(rows[r] >> 10, (OWNERS, EMB))
            wide_ref[pl.ds(CAP * t + r, OWNERS, stride=LINES), :] = chosen(
                wide[r * OWNERS : (r + 1) * OWNERS], which
            )
    out_ref[...] = wide_ref[...].astype(BF).reshape(OWNERS, LINES, EMB)


def step_kernel(
    core_ref, ret_ref, slot_col_ref, ses_ref, rel_ref, lb_ref, w_ref, b_ref, ws_ref,
    pre_grad_ref, keep_ref, send_ref, dense_ref,
):
    back = ret_ref[...].reshape(OWNERS * LINES, EMB)
    half = OWNERS * LINES // 2
    source = jnp.concatenate([back[:half], back[half:]], axis=1)
    slot_cols = slot_col_ref[...]
    pieces = []
    for t in range(TABLES):
        slot = slot_cols[:, t : t + 1]
        both = jnp.dot(hot_rows(slot & 127, (slot >> 7) & 7, 8), source, preferred_element_type=F32)
        upper = jnp.broadcast_to(slot, (IMPS, EMB)) >= half
        pieces.append(jnp.where(upper, both[:, EMB:], both[:, :EMB]).astype(BF))
    inputs = jnp.concatenate(pieces, axis=1)
    w_bf = w_ref[...].astype(BF)
    w_score = ws_ref[...]
    pre = jnp.dot(inputs, w_bf, preferred_element_type=F32) + b_ref[...]
    sig = jax.nn.sigmoid(pre)
    hidden = pre * sig
    aux = jnp.transpose(
        jnp.concatenate(
            [rel_ref[...], lb_ref[...], ses_ref[...].astype(F32)] + [rel_ref[...]] * 5, axis=0
        )
    )
    relevance, bias_col, session = aux[:, 0:1], aux[:, 1:2], aux[:, 2:3]
    scores = jnp.sum(hidden * w_score, axis=1, keepdims=True) + bias_col
    first = session < 0.5
    low = jnp.float32(-jnp.inf)
    top = [jnp.max(jnp.where(m, scores, low), axis=0, keepdims=True) for m in (first, ~first)]
    shifted = scores - jnp.where(first, top[0], top[1])
    exponent = jnp.exp(shifted)
    total = [jnp.sum(jnp.where(m, exponent, 0.0), axis=0, keepdims=True) for m in (first, ~first)]
    weight = [jnp.sum(jnp.where(m, relevance, 0.0), axis=0, keepdims=True) for m in (first, ~first)]
    probability = exponent / jnp.where(first, total[0], total[1])
    target = relevance / jnp.where(first, weight[0], weight[1])
    loss = jnp.log(total[0]) + jnp.log(total[1]) - jnp.sum(target * shifted, axis=0, keepdims=True)
    score_grad = probability - target
    pre_grad = score_grad * w_score * (sig * (1.0 + pre * (1.0 - sig)))
    pre_grad_bf = pre_grad.astype(BF)
    pre_grad_ref[...] = pre_grad_bf
    dense_ref[...] = lax.dot_general(
        inputs, pre_grad_bf, (((0,), (0,)), ((), ())), preferred_element_type=F32
    )
    bias_grad = jnp.sum(pre_grad, axis=0, keepdims=True)
    score_w_grad = jnp.sum(score_grad * hidden, axis=0, keepdims=True)
    start = pl.multiple_of(core_ref[0] * 256, 256)
    for q in range(4):
        columns = slice(EMB * q, EMB * (q + 1))
        keep_ref[256 * q : 256 * (q + 1)] = dense_ref[pl.ds(start, 256), columns]
        send_ref[256 * q : 256 * (q + 1)] = dense_ref[pl.ds(256 - start, 256), columns]
    small = jnp.concatenate(
        [bias_grad[:, EMB * q : EMB * (q + 1)] for q in range(4)]
        + [score_w_grad[:, EMB * q : EMB * (q + 1)] for q in range(4)]
        + [jnp.broadcast_to(loss, (1, EMB))]
        + [jnp.zeros((7, EMB), F32)],
        axis=0,
    )
    keep_ref[1024:] = small
    send_ref[1024:] = small


def back_kernel(pre_grad_ref, slot_ref, slot_col_ref, w_ref, out_ref):
    w_bf = w_ref[...].astype(BF)
    grad = jnp.dot(pre_grad_ref[...], w_bf.T, preferred_element_type=F32).astype(BF).astype(F32)
    slots, slot_cols = slot_ref[...], slot_col_ref[...]
    values, hots = [], []
    for t in range(TABLES):
        which = jnp.broadcast_to(slot_cols[:, t : t + 1] >> 9, (IMPS, EMB))
        values.append(fanned(grad[:, t * EMB : (t + 1) * EMB], which).astype(BF))
        slot = slots[t : t + 1]
        hots.append(hot_cols(slot & 127, (slot >> 7) & 3, 4))
    placed = jnp.dot(
        jnp.concatenate(hots, axis=1), jnp.concatenate(values, axis=0), preferred_element_type=F32
    )
    part = OWNERS // FOLD
    for f in range(FOLD):
        out_ref[f * part : (f + 1) * part] = (
            placed[:, f * EMB : (f + 1) * EMB].astype(BF).reshape(part, LINES, EMB)
        )


def pack_kernel(line_ref, keep_ref, came_ref, out_ref, small_ref):
    out_ref[:, :LINES] = line_ref[...]
    for x in range(4):
        for z in range(8):
            for y in range(4):
                k = 256 * (z % 4) + 8 * (2 * (4 * x + y) + z // 4)
                tile = keep_ref[k : k + 8] + came_ref[k : k + 8]
                high = tile.astype(BF).astype(F32)
                out_ref[(x * 8 + z) * 4 + y, LINES:] = jnp.concatenate(
                    [high, tile - high], axis=0
                ).astype(BF)
    small_ref[...] = keep_ref[1024:] + came_ref[1024:]


def open_kernel(got_ref, small_ref, line_ref, chunk_ref):
    line_ref[...] = got_ref[:, :LINES]
    sums = [jnp.zeros((16, EMB), F32) for _ in range(4)]
    for k in range(OWNERS):
        sums[k % 4] = sums[k % 4] + got_ref[k, LINES:].astype(F32)
    total = (sums[0] + sums[1]) + (sums[2] + sums[3])
    tile = total[:8] + total[8:]
    for k in range(8):
        chunk_ref[k, :8] = tile
        chunk_ref[k, 8:] = small_ref[...]


def column_kernel(got_ref, out_ref):
    small = got_ref[0, 8:]
    for z in range(1, 8):
        small = small + got_ref[z, 8:]
    for p in range(16):
        for z in range(8):
            out_ref[p, 8 * z : 8 * (z + 1)] = got_ref[z, :8]
        out_ref[p, 64:] = small


def place_kernel(
    core_ref, own_ref, other_ref, own_id_ref, other_id_ref, out_ref, wide_ref, buf_ref, sems
):
    core = core_ref[0]
    lines = OWNERS * LINES
    wide_ref[:lines] = own_ref[...].reshape(lines, EMB).astype(F32)
    wide_ref[lines:] = other_ref[...].reshape(lines, EMB).astype(F32)
    cols = [own_id_ref[...], other_id_ref[...]]
    rows = [jnp.transpose(c) for c in cols]
    part = ROWS // 2 // FOLD
    copies = []
    for t in range(TABLES):
        values, hots = [], []
        for s in range(2):
            for r in range(CAP):
                j = CAP * t + r
                line = wide_ref[pl.ds(s * lines + j, OWNERS, stride=LINES), :]
                which = jnp.broadcast_to(cols[s][:, j : j + 1] >> 9, (OWNERS, EMB)) - FOLD * core
                values.append(fanned(line, which).astype(BF))
                row = rows[s][j : j + 1]
                hots.append(hot_cols(row & 127, (row >> 7) & 3, 4))
        total = jnp.dot(
            jnp.concatenate(hots, axis=1), jnp.concatenate(values, axis=0), preferred_element_type=F32
        )
        for f in range(FOLD):
            x = total[:, f * EMB : (f + 1) * EMB]
            mean = jnp.sum(x * x, axis=1, keepdims=True) * (1.0 / EMB)
            buf_ref[t, part * f : part * (f + 1)] = x * (1.0 / (jnp.sqrt(mean) + 1e-06))
        copy = pltpu.make_async_copy(buf_ref.at[t], out_ref.at[t], sems.at[t])
        copy.start()
        copies.append(copy)
    for copy in copies:
        copy.wait()


def final_kernel(core_ref, own_ref, other_ref, w_ref, b_ref, s_ref, loss_ref):
    start = core_ref[0] * 256
    small = own_ref[0, 64:]
    for p in range(1, 16):
        small = small + own_ref[p, 64:]
    kept = small[0:8]
    square = jnp.sum(kept * kept, axis=0, keepdims=True)
    halves = []
    for ref in (own_ref, other_ref):
        sums = [jnp.zeros((8, EMB), F32) for _ in range(4)]
        for p in range(16):
            for z in range(8):
                tile = ref[p, 8 * z : 8 * (z + 1)]
                sums[z % 4] = sums[z % 4] + tile * tile
        halves.append((sums[0] + sums[1]) + (sums[2] + sums[3]))
    main = halves[0] + halves[1]
    square = jnp.sum(square + jnp.sum(main, axis=0, keepdims=True), axis=1, keepdims=True)
    factor = 1.0 / jnp.sqrt(square * (1.0 / (HID * HID + 2 * HID)) + 1e-06)
    for p in range(16):
        for z in range(8):
            row = 8 * (2 * p + z // 4)
            columns = slice(EMB * (z % 4), EMB * (z % 4 + 1))
            w_ref[pl.ds(pl.multiple_of(start + row, 8), 8), columns] = (
                own_ref[p, 8 * z : 8 * (z + 1)] * factor
            )
            w_ref[pl.ds(pl.multiple_of(256 - start + row, 8), 8), columns] = (
                other_ref[p, 8 * z : 8 * (z + 1)] * factor
            )
    b_ref[...] = small[0:4] * factor
    s_ref[...] = small[4:8] * factor
    loss_ref[...] = small[8:9] * (1.0 / 512)


def sds(shape, dtype):
    return jax.ShapeDtypeStruct(shape, dtype)


def call(kernel, mib, outs, ins, scratch=(), out_specs=None, flops=1 << 28):
    return pl.pallas_call(
        kernel,
        out_shape=outs,
        in_specs=ins,
        out_specs=(VMEM,) * len(outs) if out_specs is None else out_specs,
        scratch_shapes=list(scratch),
        cost_estimate=pl.CostEstimate(flops=flops, bytes_accessed=1 << 20, transcendentals=0),
        compiler_params=pltpu.CompilerParams(vmem_limit_bytes=mib << 20),
    )


def exchange(array, axes):
    return lax.all_to_all(array, axes, split_axis=0, concat_axis=0, tiled=True)


def whole_step(
    tables, owner_ids, row_ids, session_of, relevance, logit_bias, w_hidden, bias_hidden, w_score
):
    core = lax.axis_index("dp").astype(jnp.int32).reshape(1)
    swap = [(0, 1), (1, 0)]
    i32 = jnp.int32
    wanted, slots, slot_cols = call(
        slots_kernel, 8,
        (sds((OWNERS, LINES), i32), sds((TABLES, IMPS), i32), sds((IMPS, 2 * TABLES), i32)),
        [HBM, HBM],
        [pltpu.VMEM((8, 128), i32), pltpu.VMEM((TABLES, IMPS), i32), pltpu.SemaphoreType.DMA((2,))],
    )(owner_ids.reshape(8, 128), row_ids.reshape(TABLES, IMPS))
    requested = exchange(wanted, TABLE)
    other_ids = lax.ppermute(requested, "dp", swap)
    (served,) = call(
        serve_kernel, 61,
        (sds((OWNERS, LINES, EMB), BF),),
        [VMEM, HBM],
        [
            pltpu.VMEM((OWNERS * LINES, EMB), F32),
            pltpu.VMEM((TABLES, ROWS, EMB), BF),
            pltpu.SemaphoreType.DMA((TABLES,)),
        ],
    )(requested, tables)
    returned = exchange(served, TABLE)
    half = sds((1024 + SMALL, EMB), F32)
    pre_grad, keep, send = call(
        step_kernel, 24,
        (sds((IMPS, HID), BF), half, half),
        [SMEM] + [VMEM] * 8,
        [pltpu.VMEM((HID, HID), F32)],
    )(
        core, returned, slot_cols, session_of, relevance, logit_bias, w_hidden,
        bias_hidden.reshape(1, HID), w_score.reshape(1, HID),
    )
    came = lax.ppermute(send, "dp", swap)
    (lines,) = call(
        back_kernel, 20, (sds((OWNERS, LINES, EMB), BF),), [VMEM] * 4
    )(pre_grad, slots, slot_cols, w_hidden)
    message, small = call(
        pack_kernel, 12,
        (sds((OWNERS, 2 * LINES, EMB), BF), sds((SMALL, EMB), F32)),
        [VMEM] * 3,
    )(lines, keep, came)
    got = exchange(message, TABLE)
    incoming, chunks = call(
        open_kernel, 12,
        (sds((OWNERS, LINES, EMB), BF), sds((8, 8 + SMALL, EMB), F32)),
        [VMEM] * 2,
    )(got, small)
    other = lax.ppermute(incoming, "dp", swap)
    column = exchange(chunks, "z")
    (emb_step,) = call(
        place_kernel, 28,
        (sds((TABLES, ROWS // 2, EMB), F32),),
        [SMEM] + [VMEM] * 4,
        [
            pltpu.VMEM((2 * OWNERS * LINES, EMB), F32),
            pltpu.VMEM((TABLES, ROWS // 2, EMB), F32),
            pltpu.SemaphoreType.DMA((TABLES,)),
        ],
        out_specs=(ANY,),
    )(core, incoming, other, requested, other_ids)
    (plane,) = call(column_kernel, 12, (sds((16, 64 + SMALL, EMB), F32),), [VMEM])(column)
    mine = exchange(plane, ("x", "y"))
    theirs = lax.ppermute(mine, "dp", swap)
    step_hidden, step_bias, step_score, loss = call(
        final_kernel, 12,
        (sds((HID, HID), F32), sds((4, 128), F32), sds((4, 128), F32), sds((1, 128), F32)),
        [SMEM] + [VMEM] * 2,
    )(core, mine, theirs)
    return emb_step, step_hidden, step_bias.reshape(HID), step_score.reshape(HID), loss[0, 0]


def solution(mesh):
    split = Mesh(mesh.devices.reshape(4, 8, 4, mesh.shape["dp"]), ALL)
    return jax.shard_map(
        whole_step,
        mesh=split,
        in_specs=(
            P(None, TABLE, None),
            P(ALL, None, None, None),
            P(ALL, None, None),
            P(ALL, None),
            P(ALL, None),
            P(ALL, None),
            P(),
            P(),
            P(),
        ),
        out_specs=(P(None, ALL, None), P(), P(), P(), P()),
        check_vma=False,
    )
```

time: 152 us -> 140 us (0.921)
  blocking collectives: 55.3 us -> 86.7 us
  waiting for transfers between devices: 40.6 us -> 18.6 us
  starting transfers between devices: 31.4 us -> 15.3 us
  Pallas kernels: 20.9 us -> 17.2 us
    all_to_all x3 -> x4, blocking collectives: 55.3 us -> 86.7 us  [exchange(): return lax.all_to_all(array, axes, split_axis=0, concat_axis=0, tiled=True)]
    all_to_all x3 -> x1, waiting for transfers between devices: 37.3 us -> 16.1 us  [exchange(): return lax.all_to_all(array, axes, split_axis=0, concat_axis=0, tiled=True)]
    all_to_all x3 -> x1, starting transfers between devices: 18.2 us -> 6.19 us  [exchange(): return lax.all_to_all(array, axes, split_axis=0, concat_axis=0, tiled=True)]
    ppermute x1, starting transfers between devices: 4.01 us -> 0.01 us  [whole_step(): other = lax.ppermute(incoming, 'dp', swap)]
    pallas_call x5 -> x9, Pallas kernels: 20.9 us -> 17.2 us  [the longest x1 5.95 us: whole_step(): call(serve_kernel, 61, (sds((OWNERS, LINES, EMB), BF),), [VMEM, HBM], [pl...]
  transfers between devices with their start and end apart: 7 -> 5, of which waited for: 5 -> 3; matrix products, arithmetic and copies ran while one was open for 0% -> 0% of each run, Pallas kernels for 4% -> 5%
where the time goes in v1:
time: 140 us
  blocking collectives  86.7 us (62%)
  waiting for transfers between devices  18.6 us (13%)
  Pallas kernels  17.2 us (12%)
  starting transfers between devices  15.3 us (11%)
  local copies, waits for them, and re-layouts  1.47 us (1%)
    all_to_all x4, blocking collectives, exchange(): return lax.all_to_all(array, axes, split_axis=0, concat_axis=0, tiled=True)  86.7 us
    all_to_all x1, waiting for transfers between devices, exchange(): return lax.all_to_all(array, axes, split_axis=0, concat_axis=0, tiled=True)  16.1 us
    all_to_all x1, starting transfers between devices, exchange(): return lax.all_to_all(array, axes, split_axis=0, concat_axis=0, tiled=True)  6.19 us
    pallas_call x1, Pallas kernels, whole_step(): call(serve_kernel, 61, (sds((OWNERS, LINES, EMB), BF),), [VMEM, HBM], [pl...  5.95 us
    pallas_call x1, Pallas kernels, whole_step(): call(place_kernel, 28, (sds((TABLES, ROWS // 2, EMB), F32),), [SMEM] + [V...  5.34 us
    ppermute x1, starting transfers between devices, whole_step(): came = lax.ppermute(send, 'dp', swap)  4.31 us
    ppermute x1, starting transfers between devices, whole_step(): theirs = lax.ppermute(mine, 'dp', swap)  4.26 us
  transfers between devices with their start and end apart: 5, of which 3 were waited for; matrix products, arithmetic and copies ran while one was open for 0% of the time, Pallas kernels for 5%

profile of v1, /device:TPU:1, one launch (start us, length us, event | category | flops | bytes accessed | tf_op | source)
XLA Modules:
  0.0 140.1 jit_solution(4417091039933151705)
XLA Ops:
  0.6 0.0 copy-start
  0.6 0.0 copy-start.3
  0.7 0.0 copy-start.2
  0.7 0.0 copy-start.6
  0.7 0.0 copy-start.5
  0.7 0.0 copy-start.4
  0.7 0.0 copy-start.7
  0.7 0.8 copy-done.7
  1.5 0.0 copy-start.8
  1.5 0.7 copy-done.8
  2.1 1.1 shard_map.128
  3.2 27.1 %all_to_all.31 = s32[128,1,16]{2,1,0:T(1,128)} all-to-all(s32[128,1,16]{2,1,0:T(1,128)S(1)} %bitcast.16), channel_id=1, replica_groups=mesh['x'=4,'z'=8,'y'=4,'dp'=2] {'x','z','y'}, dimensions={0} | all-to-all | bytes 16384 | tf_op jit(solution)/shard_map/all_to_all | solution.py:324
  30.4 5.9 %shard_map.129 = bf16[128,16,128]{2,1,0:T(8,128)(2,1)} custom-call(s32[128,16]{1,0:T(8,128)} %bitcast.13, bf16[4,4096,128]{2,1,0:T(8,128)(2,1)} %far_ref.1), custom_call_target="tpu_custom_call" | custom-call | flops 268435456 | bytes 1048576 | tf_op jit(solution)/shard_map/pallas_call | solution.py:341
  36.3 6.2 %all-to-all-start.1 = ((bf16[128,16,128]{2,1,0:T(8,128)(2,1)}), bf16[128,16,128]{2,1,0:T(8,128)(2,1)S(1)}, u32[]{:S(2)}, u32[]{:S(2)}) async-start(bf16[128,16,128]{2,1,0:T(8,128)(2,1)} %shard_map.129), calls=%async_computation.1 | async-start | bytes 1048576 | tf_op jit(solution)/shard_map/all_to_all | solution.py:324
  42.5 16.1 %all-to-all-done.1.ret_ref = bf16[128,16,128]{2,1,0:T(8,128)(2,1)S(1)} async-done(((bf16[128,16,128]{2,1,0:T(8,128)(2,1)}), bf16[128,16,128]{2,1,0:T(8,128)(2,1)S(1)}, u32[]{:S(2)}, u32[]{:S(2)}) %all-to-all-start.1) | async-done | bytes 524320 | tf_op jit(solution)/shard_map/all_to_all | solution.py:324
  58.6 0.0 copy-done
  58.6 0.0 copy-done.3
  58.6 0.0 copy-done.2
  58.6 0.0 copy-done.6
  58.6 0.0 copy-done.5
  58.6 0.0 copy-done.4
  58.6 2.2 %shard_map.130 = (bf16[256,512]{1,0:T(8,128)(2,1)S(1)}, f32[1040,128]{1,0:T(8,128)S(1)}, f32[1040,128]{1,0:T(8,128)S(1)}) custom-call(s32[1]{0:T(128)} %bitcast.core_ref, bf16[128,16,128]{2,1,0:T(8,128)(2,1)S(1)} %all-to-all-done.1.ret_ref, s32[256,8]{1,0:T(8,128)S(1)} %get-tuple-element.20.slot_col_ref, s32[1,256]{1,0:T(1,128)S(1)} %copy-done.4, ...), custom_call_target="tpu_custom_call" | custom-call | flops 268435456 | bytes 1048576 | tf_op jit(solution)/shard_map/pallas_call | solution.py:353
  60.8 4.3 %collective-permute-start = (f32[1040,128]{1,0:T(8,128)S(1)}, f32[1040,128]{1,0:T(8,128)S(1)}, u32[]{:S(2)}, u32[]{:S(2)}) collective-permute-start(f32[1040,128]{1,0:T(8,128)S(1)} %get-tuple-element.24), channel_id=1, source_target_pairs={{0,1},{1,0},{2,3},{3,2},{4,5},{5,4},{6,7},{7,6},{8,9},{9,8},{10,11... | collective-permute-start | bytes 1597448 | tf_op jit(solution)/shard_map/ppermute | solution.py:362
  65.2 0.0 copy-start.1
  65.2 1.0 shard_map.131.line_ref
  66.2 0.5 collective-permute-done.came_ref
  66.7 0.2 shard_map.132
  66.9 33.9 %all_to_all.32.got_ref = bf16[128,32,128]{2,1,0:T(8,128)(2,1)S(1)} all-to-all(bf16[128,32,128]{2,1,0:T(8,128)(2,1)S(1)} %get-tuple-element.25), channel_id=1, replica_groups=mesh['x'=4,'z'=8,'y'=4,'dp'=2] {'x','z','y'}, dimensions={0} | all-to-all | bytes 2097152 | tf_op jit(solution)/shard_map/all_to_all | solution.py:324
  100.8 0.1 shard_map.133
  100.9 13.4 %all_to_all.33.got_ref = f32[8,24,128]{2,1,0:T(8,128)S(1)} all-to-all(f32[8,24,128]{2,1,0:T(8,128)S(1)} %get-tuple-element.28), channel_id=1, replica_groups=mesh['x'=4,'z'=8,'y'=4,'dp'=2] {'z'}, dimensions={0} | all-to-all | bytes 196608 | tf_op jit(solution)/shard_map/all_to_all | solution.py:324
  114.3 12.3 %all_to_all.34.own_ref = f32[16,80,128]{2,1,0:T(8,128)S(1)} all-to-all(f32[16,80,128]{2,1,0:T(8,128)S(1)} %shard_map.135), channel_id=1, replica_groups=mesh['x'=4,'z'=8,'y'=4,'dp'=2] {'x','y'}, dimensions={0} | all-to-all | bytes 1310720 | tf_op jit(solution)/shard_map/all_to_all | solution.py:324
  126.6 4.3 %collective-permute-start.3 = (f32[16,80,128]{2,1,0:T(8,128)S(1)}, f32[16,80,128]{2,1,0:T(8,128)S(1)}, u32[]{:S(2)}, u32[]{:S(2)}) collective-permute-start(f32[16,80,128]{2,1,0:T(8,128)S(1)} %all_to_all.34.own_ref), channel_id=1, source_target_pairs={{0,1},{1,0},{2,3},{3,2},{4,5},{5,4},{6,7},{7,6},{8,9},{9,8},{10,11... | collective-permute-start | bytes 1966088 | tf_op jit(solution)/shard_map/ppermute | solution.py:392
  130.9 0.0 collective-permute-start.1
  130.9 0.0 copy-done.1
  130.9 0.5 collective-permute-start.2
  131.4 2.1 %collective-permute-done.2.other_id_ref = s32[128,16]{1,0:T(8,128)S(1)} collective-permute-done((s32[128,16]{1,0:T(8,128)S(1)}, s32[128,16]{1,0:T(8,128)S(1)}, u32[]{:S(2)}, u32[]{:S(2)}) %collective-permute-start.2) | collective-permute-done | bytes 8224 | tf_op jit(solution)/shard_map/ppermute | solution.py:340
  133.4 0.0 collective-permute-done.1.other_ref
  133.4 5.3 %shard_map.134 = f32[4,2048,128]{2,1,0:T(8,128)} custom-call(s32[1]{0:T(128)} %bitcast.core_ref, bf16[128,16,128]{2,1,0:T(8,128)(2,1)S(1)} %get-tuple-element.27.own_ref, bf16[128,16,128]{2,1,0:T(8,128)(2,1)S(1)} %collective-permute-done.1.other_ref, s32[128,16]{1,0:T(8,128)S(1)} %bitcast.15, s32[128,16]{1,0:T(8,128)S(1)} %collective-permute-done.2.other_id_ref), custom_call_target="tpu_custom_call" | custom-call | flops 268435456 | bytes 1048576 | tf_op jit(solution)/shard_map/pallas_call | solution.py:379
  138.8 0.0 collective-permute-done.3.other_ref
  138.8 1.3 shard_map.136
  (1 shorter events, 0.0 us)
Async XLA Ops:
  0.6 58.0 %copy-start = (f32[512,512]{1,0:T(8,128)S(1)}, f32[512,512]{1,0:T(8,128)}, u32[]{:S(2)}) copy-start(f32[512,512]{1,0:T(8,128)} %w_ref.3) | copy-start | bytes 3145732
  0.6 58.0 %copy-start.3 = (f32[512]{0:T(512)S(1)}, f32[512]{0:T(512)}, u32[]{:S(2)}) copy-start(f32[512]{0:T(512)} %param.17) | copy-start | bytes 6148
  0.7 57.9 %copy-start.2 = (f32[512]{0:T(512)S(1)}, f32[512]{0:T(512)}, u32[]{:S(2)}) copy-start(f32[512]{0:T(512)} %param.16) | copy-start | bytes 6148
  0.7 57.9 %copy-start.6 = (f32[1,256]{1,0:T(1,128)S(1)}, f32[1,256]{1,0:T(1,128)}, u32[]{:S(2)}) copy-start(f32[1,256]{1,0:T(1,128)} %lb_ref.1) | copy-start | bytes 3076
  0.7 57.9 %copy-start.5 = (f32[1,256]{1,0:T(1,128)S(1)}, f32[1,256]{1,0:T(1,128)}, u32[]{:S(2)}) copy-start(f32[1,256]{1,0:T(1,128)} %rel_ref.1) | copy-start | bytes 3076
  0.7 57.9 %copy-start.4 = (s32[1,256]{1,0:T(1,128)S(1)}, s32[1,256]{1,0:T(1,128)}, u32[]{:S(2)}) copy-start(s32[1,256]{1,0:T(1,128)} %ses_ref.1) | copy-start | bytes 3076
  0.7 0.8 copy-start.7
  1.5 0.7 copy-start.8
  36.3 22.3 %all-to-all-start.1 = ((bf16[128,16,128]{2,1,0:T(8,128)(2,1)}), bf16[128,16,128]{2,1,0:T(8,128)(2,1)S(1)}, u32[]{:S(2)}, u32[]{:S(2)}) async-start(bf16[128,16,128]{2,1,0:T(8,128)(2,1)} %shard_map.129), calls=%async_computation.1 | async-start | bytes 1048576 | tf_op jit(solution)/shard_map/all_to_all | solution.py:324
  60.8 5.9 %collective-permute-start = (f32[1040,128]{1,0:T(8,128)S(1)}, f32[1040,128]{1,0:T(8,128)S(1)}, u32[]{:S(2)}, u32[]{:S(2)}) collective-permute-start(f32[1040,128]{1,0:T(8,128)S(1)} %get-tuple-element.24), channel_id=1, source_target_pairs={{0,1},{1,0},{2,3},{3,2},{4,5},{5,4},{6,7},{7,6},{8,9},{9,8},{10,11... | collective-permute-start | bytes 1597448 | tf_op jit(solution)/shard_map/ppermute | solution.py:362
  65.2 65.7 %copy-start.1 = (s32[128,1,16]{2,1,0:T(1,128)S(1)}, s32[128,1,16]{2,1,0:T(1,128)}, u32[]{:S(2)}) copy-start(s32[128,1,16]{2,1,0:T(1,128)} %all_to_all.31) | copy-start | bytes 24580
  126.6 12.2 %collective-permute-start.3 = (f32[16,80,128]{2,1,0:T(8,128)S(1)}, f32[16,80,128]{2,1,0:T(8,128)S(1)}, u32[]{:S(2)}, u32[]{:S(2)}) collective-permute-start(f32[16,80,128]{2,1,0:T(8,128)S(1)} %all_to_all.34.own_ref), channel_id=1, source_target_pairs={{0,1},{1,0},{2,3},{3,2},{4,5},{5,4},{6,7},{7,6},{8,9},{9,8},{10,11... | collective-permute-start | bytes 1966088 | tf_op jit(solution)/shard_map/ppermute | solution.py:392
  130.9 2.6 %collective-permute-start.1 = (bf16[128,16,128]{2,1,0:T(8,128)(2,1)S(1)}, bf16[128,16,128]{2,1,0:T(8,128)(2,1)S(1)}, u32[]{:S(2)}, u32[]{:S(2)}) collective-permute-start(bf16[128,16,128]{2,1,0:T(8,128)(2,1)S(1)} %get-tuple-element.27.own_ref), channel_id=1, source_target_pairs={{0,1},{1,0},{2,3},{3,2},{4,5},{5,4},{6,7},{7,6},{8,9},{9,8},{10,11... | collective-permute-start | bytes 1572872 | tf_op jit(solution)/shard_map/ppermute | solution.py:377
  130.9 2.6 %collective-permute-start.2 = (s32[128,16]{1,0:T(8,128)S(1)}, s32[128,16]{1,0:T(8,128)S(1)}, u32[]{:S(2)}, u32[]{:S(2)}) collective-permute-start(s32[128,16]{1,0:T(8,128)S(1)} %bitcast.14), channel_id=1, source_target_pairs={{0,1},{1,0},{2,3},{3,2},{4,5},{5,4},{6,7},{7,6},{8,9},{9,8},{10,11... | collective-permute-start | bytes 24584 | tf_op jit(solution)/shard_map/ppermute | solution.py:340

commit v2 on v1

--- a/solution.py
+++ b/solution.py
@@ -61,7 +61,7 @@
     return jnp.concatenate([jnp.where(which == f, piece, zero) for f in range(FOLD)], axis=1)
 
 
-def slots_kernel(own_hbm, row_hbm, want_ref, slot_ref, slot_col_ref, own_ref, row_ref, sems):
+def slots_kernel(core_ref, own_hbm, row_hbm, want_ref, slot_ref, slot_col_ref, own_ref, row_ref, sems):
     copies = [
         pltpu.make_async_copy(own_hbm, own_ref, sems.at[0]),
         pltpu.make_async_copy(row_hbm, row_ref, sems.at[1]),
@@ -333,13 +333,17 @@
     wanted, slots, slot_cols = call(
         slots_kernel, 8,
         (sds((OWNERS, LINES), i32), sds((TABLES, IMPS), i32), sds((IMPS, 2 * TABLES), i32)),
-        [HBM, HBM],
+        [SMEM, HBM, HBM],
         [pltpu.VMEM((8, 128), i32), pltpu.VMEM((TABLES, IMPS), i32), pltpu.SemaphoreType.DMA((2,))],
-    )(owner_ids.reshape(8, 128), row_ids.reshape(TABLES, IMPS))
+    )(
+        core,
+        pltpu.with_memory_space_constraint(owner_ids.reshape(8, 128), pltpu.HBM),
+        pltpu.with_memory_space_constraint(row_ids.reshape(TABLES, IMPS), pltpu.HBM),
+    )
     requested = exchange(wanted, TABLE)
     other_ids = lax.ppermute(requested, "dp", swap)
     (served,) = call(
-        serve_kernel, 61,
+        serve_kernel, 24,
         (sds((OWNERS, LINES, EMB), BF),),
         [VMEM, HBM],
         [
@@ -347,7 +351,7 @@
             pltpu.VMEM((TABLES, ROWS, EMB), BF),
             pltpu.SemaphoreType.DMA((TABLES,)),
         ],
-    )(requested, tables)
+    )(requested, pltpu.with_memory_space_constraint(tables, pltpu.HBM))
     returned = exchange(served, TABLE)
     half = sds((1024 + SMALL, EMB), F32)
     pre_grad, keep, send = call(

time: 140 us -> 137 us (0.979)
  blocking collectives: 86.7 us -> 108 us
  waiting for transfers between devices: 18.6 us -> 2.58 us
  starting transfers between devices: 15.3 us -> 9.25 us
  local copies, waits for them, and re-layouts: 1.47 us -> 0.03 us
    all_to_all x4 -> x5, blocking collectives: 86.7 us -> 108 us  [exchange(): return lax.all_to_all(array, axes, split_axis=0, concat_axis=0, tiled=True)]
    all_to_all x1 -> x0, waiting for transfers between devices: 16.1 us -> none  [exchange(): return lax.all_to_all(array, axes, split_axis=0, concat_axis=0, tiled=True)]
    all_to_all x1 -> x0, starting transfers between devices: 6.19 us -> none  [exchange(): return lax.all_to_all(array, axes, split_axis=0, concat_axis=0, tiled=True)]
    pallas_call x1, Pallas kernels: 5.95 us -> 4.33 us  [whole_step(): call(serve_kernel, 24, (sds((OWNERS, LINES, EMB), BF),), [VMEM, HBM], [pl...]
    unnamed x18 -> x12, local copies, waits for them, and re-layouts: 1.47 us -> 0.03 us
  transfers between devices with their start and end apart: 5 -> 4, of which waited for: 3 -> 2; matrix products, arithmetic and copies ran while one was open for 0% -> 0% of each run, Pallas kernels for 5% -> 5%
where the time goes in v2:
time: 137 us
  blocking collectives  108 us (79%)
  Pallas kernels  16.4 us (12%)
  starting transfers between devices  9.25 us (7%)
  waiting for transfers between devices  2.58 us (2%)
    all_to_all x5, blocking collectives, exchange(): return lax.all_to_all(array, axes, split_axis=0, concat_axis=0, tiled=True)  108 us
    pallas_call x1, Pallas kernels, whole_step(): call(place_kernel, 28, (sds((TABLES, ROWS // 2, EMB), F32),), [SMEM] + [V...  5.38 us
    ppermute x1, starting transfers between devices, whole_step(): came = lax.ppermute(send, 'dp', swap)  4.48 us
    pallas_call x1, Pallas kernels, whole_step(): call(serve_kernel, 24, (sds((OWNERS, LINES, EMB), BF),), [VMEM, HBM], [pl...  4.33 us
    ppermute x1, starting transfers between devices, whole_step(): theirs = lax.ppermute(mine, 'dp', swap)  4.26 us
  transfers between devices with their start and end apart: 4, of which 2 were waited for; matrix products, arithmetic and copies ran while one was open for 0% of the time, Pallas kernels for 5%

profile of v2, /device:TPU:1, one launch (start us, length us, event | category | flops | bytes accessed | tf_op | source)
XLA Modules:
  0.0 136.7 jit_solution(1149963060294544017)
XLA Ops:
  0.6 0.0 copy-start
  0.6 0.0 copy-start.2
  0.7 0.0 copy-start.1
  0.7 0.0 copy-start.5
  0.7 0.0 copy-start.4
  0.7 0.0 copy-start.3
  0.7 1.9 %shard_map.128 = (s32[128,16]{1,0:T(8,128)S(1)}, s32[4,256]{1,0:T(4,128)S(1)}, s32[256,8]{1,0:T(8,128)S(1)}) custom-call(s32[1]{0:T(128)} %bitcast.core_ref, s32[8,128]{1,0:T(8,128)} %bitcast.19, s32[4,256]{1,0:T(4,128)} %bitcast.20), custom_call_target="tpu_custom_call" | custom-call | flops 268435456 | bytes 1048576 | tf_op jit(solution)/shard_map/pallas_call | solution.py:333
  2.6 26.7 %all_to_all.31 = s32[128,1,16]{2,1,0:T(1,128)S(1)} all-to-all(s32[128,1,16]{2,1,0:T(1,128)S(1)} %bitcast.16), channel_id=1, replica_groups=mesh['x'=4,'z'=8,'y'=4,'dp'=2] {'x','z','y'}, dimensions={0} | all-to-all | bytes 16384 | tf_op jit(solution)/shard_map/all_to_all | solution.py:324
  29.3 4.3 %shard_map.129 = bf16[128,16,128]{2,1,0:T(8,128)(2,1)S(1)} custom-call(s32[128,16]{1,0:T(8,128)S(1)} %bitcast.13, bf16[4,4096,128]{2,1,0:T(8,128)(2,1)} %far_ref.1), custom_call_target="tpu_custom_call" | custom-call | flops 268435456 | bytes 1048576 | tf_op jit(solution)/shard_map/pallas_call | solution.py:345
  33.6 21.5 %all_to_all.32.ret_ref = bf16[128,16,128]{2,1,0:T(8,128)(2,1)S(1)} all-to-all(bf16[128,16,128]{2,1,0:T(8,128)(2,1)S(1)} %shard_map.129), channel_id=1, replica_groups=mesh['x'=4,'z'=8,'y'=4,'dp'=2] {'x','z','y'}, dimensions={0} | all-to-all | bytes 1048576 | tf_op jit(solution)/shard_map/all_to_all | solution.py:324
  55.1 0.0 copy-done
  55.1 0.0 copy-done.2
  55.1 0.0 copy-done.1
  55.1 0.0 copy-done.5
  55.1 0.0 copy-done.4
  55.1 0.0 copy-done.3
  55.1 2.2 %shard_map.130 = (bf16[256,512]{1,0:T(8,128)(2,1)S(1)}, f32[1040,128]{1,0:T(8,128)S(1)}, f32[1040,128]{1,0:T(8,128)S(1)}) custom-call(s32[1]{0:T(128)} %bitcast.core_ref, bf16[128,16,128]{2,1,0:T(8,128)(2,1)S(1)} %all_to_all.32.ret_ref, s32[256,8]{1,0:T(8,128)S(1)} %get-tuple-element.20.slot_col_ref, s32[1,256]{1,0:T(1,128)S(1)} %copy-done.3, ...), custom_call_target="tpu_custom_call" | custom-call | flops 268435456 | bytes 1048576 | tf_op jit(solution)/shard_map/pallas_call | solution.py:357
  57.3 4.5 %collective-permute-start = (f32[1040,128]{1,0:T(8,128)S(1)}, f32[1040,128]{1,0:T(8,128)S(1)}, u32[]{:S(2)}, u32[]{:S(2)}) collective-permute-start(f32[1040,128]{1,0:T(8,128)S(1)} %get-tuple-element.24), channel_id=1, source_target_pairs={{0,1},{1,0},{2,3},{3,2},{4,5},{5,4},{6,7},{7,6},{8,9},{9,8},{10,11... | collective-permute-start | bytes 1597448 | tf_op jit(solution)/shard_map/ppermute | solution.py:366
  61.8 1.0 shard_map.131.line_ref
  62.9 0.5 collective-permute-done.came_ref
  63.4 0.1 shard_map.132
  63.5 33.9 %all_to_all.33.got_ref = bf16[128,32,128]{2,1,0:T(8,128)(2,1)S(1)} all-to-all(bf16[128,32,128]{2,1,0:T(8,128)(2,1)S(1)} %get-tuple-element.25), channel_id=1, replica_groups=mesh['x'=4,'z'=8,'y'=4,'dp'=2] {'x','z','y'}, dimensions={0} | all-to-all | bytes 2097152 | tf_op jit(solution)/shard_map/all_to_all | solution.py:324
  97.4 0.1 shard_map.133
  97.5 13.4 %all_to_all.34.got_ref = f32[8,24,128]{2,1,0:T(8,128)S(1)} all-to-all(f32[8,24,128]{2,1,0:T(8,128)S(1)} %get-tuple-element.28), channel_id=1, replica_groups=mesh['x'=4,'z'=8,'y'=4,'dp'=2] {'z'}, dimensions={0} | all-to-all | bytes 196608 | tf_op jit(solution)/shard_map/all_to_all | solution.py:324
  110.9 12.3 %all_to_all.35.own_ref = f32[16,80,128]{2,1,0:T(8,128)S(1)} all-to-all(f32[16,80,128]{2,1,0:T(8,128)S(1)} %shard_map.135), channel_id=1, replica_groups=mesh['x'=4,'z'=8,'y'=4,'dp'=2] {'x','y'}, dimensions={0} | all-to-all | bytes 1310720 | tf_op jit(solution)/shard_map/all_to_all | solution.py:324
  123.2 4.3 %collective-permute-start.3 = (f32[16,80,128]{2,1,0:T(8,128)S(1)}, f32[16,80,128]{2,1,0:T(8,128)S(1)}, u32[]{:S(2)}, u32[]{:S(2)}) collective-permute-start(f32[16,80,128]{2,1,0:T(8,128)S(1)} %all_to_all.35.own_ref), channel_id=1, source_target_pairs={{0,1},{1,0},{2,3},{3,2},{4,5},{5,4},{6,7},{7,6},{8,9},{9,8},{10,11... | collective-permute-start | bytes 1966088 | tf_op jit(solution)/shard_map/ppermute | solution.py:396
  127.5 0.0 collective-permute-start.1
  127.5 0.5 collective-permute-start.2
  128.0 2.1 %collective-permute-done.2.other_id_ref = s32[128,16]{1,0:T(8,128)S(1)} collective-permute-done((s32[128,16]{1,0:T(8,128)S(1)}, s32[128,16]{1,0:T(8,128)S(1)}, u32[]{:S(2)}, u32[]{:S(2)}) %collective-permute-start.2) | collective-permute-done | bytes 8224 | tf_op jit(solution)/shard_map/ppermute | solution.py:344
  130.0 0.0 collective-permute-done.1.other_ref
  130.1 5.4 %shard_map.134 = f32[4,2048,128]{2,1,0:T(8,128)} custom-call(s32[1]{0:T(128)} %bitcast.core_ref, bf16[128,16,128]{2,1,0:T(8,128)(2,1)S(1)} %get-tuple-element.27.own_ref, bf16[128,16,128]{2,1,0:T(8,128)(2,1)S(1)} %collective-permute-done.1.other_ref, s32[128,16]{1,0:T(8,128)S(1)} %bitcast.15, s32[128,16]{1,0:T(8,128)S(1)} %collective-permute-done.2.other_id_ref), custom_call_target="tpu_custom_call" | custom-call | flops 268435456 | bytes 1048576 | tf_op jit(solution)/shard_map/pallas_call | solution.py:383
  135.4 0.0 collective-permute-done.3.other_ref
  135.5 1.3 shard_map.136
  (1 shorter events, 0.0 us)
Async XLA Ops:
  0.6 54.5 %copy-start = (f32[512,512]{1,0:T(8,128)S(1)}, f32[512,512]{1,0:T(8,128)}, u32[]{:S(2)}) copy-start(f32[512,512]{1,0:T(8,128)} %w_ref.3) | copy-start | bytes 3145732
  0.6 54.5 %copy-start.2 = (f32[512]{0:T(512)S(1)}, f32[512]{0:T(512)}, u32[]{:S(2)}) copy-start(f32[512]{0:T(512)} %param.17) | copy-start | bytes 6148
  0.7 54.5 %copy-start.1 = (f32[512]{0:T(512)S(1)}, f32[512]{0:T(512)}, u32[]{:S(2)}) copy-start(f32[512]{0:T(512)} %param.16) | copy-start | bytes 6148
  0.7 54.5 %copy-start.5 = (f32[1,256]{1,0:T(1,128)S(1)}, f32[1,256]{1,0:T(1,128)}, u32[]{:S(2)}) copy-start(f32[1,256]{1,0:T(1,128)} %lb_ref.1) | copy-start | bytes 3076
  0.7 54.5 %copy-start.4 = (f32[1,256]{1,0:T(1,128)S(1)}, f32[1,256]{1,0:T(1,128)}, u32[]{:S(2)}) copy-start(f32[1,256]{1,0:T(1,128)} %rel_ref.1) | copy-start | bytes 3076
  0.7 54.5 %copy-start.3 = (s32[1,256]{1,0:T(1,128)S(1)}, s32[1,256]{1,0:T(1,128)}, u32[]{:S(2)}) copy-start(s32[1,256]{1,0:T(1,128)} %ses_ref.1) | copy-start | bytes 3076
  57.3 6.0 %collective-permute-start = (f32[1040,128]{1,0:T(8,128)S(1)}, f32[1040,128]{1,0:T(8,128)S(1)}, u32[]{:S(2)}, u32[]{:S(2)}) collective-permute-start(f32[1040,128]{1,0:T(8,128)S(1)} %get-tuple-element.24), channel_id=1, source_target_pairs={{0,1},{1,0},{2,3},{3,2},{4,5},{5,4},{6,7},{7,6},{8,9},{9,8},{10,11... | collective-permute-start | bytes 1597448 | tf_op jit(solution)/shard_map/ppermute | solution.py:366
  123.2 12.2 %collective-permute-start.3 = (f32[16,80,128]{2,1,0:T(8,128)S(1)}, f32[16,80,128]{2,1,0:T(8,128)S(1)}, u32[]{:S(2)}, u32[]{:S(2)}) collective-permute-start(f32[16,80,128]{2,1,0:T(8,128)S(1)} %all_to_all.35.own_ref), channel_id=1, source_target_pairs={{0,1},{1,0},{2,3},{3,2},{4,5},{5,4},{6,7},{7,6},{8,9},{9,8},{10,11... | collective-permute-start | bytes 1966088 | tf_op jit(solution)/shard_map/ppermute | solution.py:396
  127.5 2.6 %collective-permute-start.1 = (bf16[128,16,128]{2,1,0:T(8,128)(2,1)S(1)}, bf16[128,16,128]{2,1,0:T(8,128)(2,1)S(1)}, u32[]{:S(2)}, u32[]{:S(2)}) collective-permute-start(bf16[128,16,128]{2,1,0:T(8,128)(2,1)S(1)} %get-tuple-element.27.own_ref), channel_id=1, source_target_pairs={{0,1},{1,0},{2,3},{3,2},{4,5},{5,4},{6,7},{7,6},{8,9},{9,8},{10,11... | collective-permute-start | bytes 1572872 | tf_op jit(solution)/shard_map/ppermute | solution.py:381
  127.5 2.6 %collective-permute-start.2 = (s32[128,16]{1,0:T(8,128)S(1)}, s32[128,16]{1,0:T(8,128)S(1)}, u32[]{:S(2)}, u32[]{:S(2)}) collective-permute-start(s32[128,16]{1,0:T(8,128)S(1)} %bitcast.14), channel_id=1, source_target_pairs={{0,1},{1,0},{2,3},{3,2},{4,5},{5,4},{6,7},{7,6},{8,9},{9,8},{10,11... | collective-permute-start | bytes 24584 | tf_op jit(solution)/shard_map/ppermute | solution.py:344

commit v3 on v2

--- a/solution.py
+++ b/solution.py
@@ -165,10 +165,13 @@
     bias_grad = jnp.sum(pre_grad, axis=0, keepdims=True)
     score_w_grad = jnp.sum(score_grad * hidden, axis=0, keepdims=True)
     start = pl.multiple_of(core_ref[0] * 256, 256)
-    for q in range(4):
-        columns = slice(EMB * q, EMB * (q + 1))
-        keep_ref[256 * q : 256 * (q + 1)] = dense_ref[pl.ds(start, 256), columns]
-        send_ref[256 * q : 256 * (q + 1)] = dense_ref[pl.ds(256 - start, 256), columns]
+    for y in range(4):
+        for x in range(4):
+            for z in range(8):
+                k = ((y * 4 + x) * 8 + z) * 8
+                row, columns = 8 * (2 * (4 * x + y) + z // 4), slice(EMB * (z % 4), EMB * (z % 4 + 1))
+                for ref, base in ((keep_ref, start), (send_ref, 256 - start)):
+                    ref[k : k + 8] = dense_ref[pl.ds(pl.multiple_of(base + row, 8), 8), columns]
     small = jnp.concatenate(
         [bias_grad[:, EMB * q : EMB * (q + 1)] for q in range(4)]
         + [score_w_grad[:, EMB * q : EMB * (q + 1)] for q in range(4)]
@@ -200,40 +203,35 @@
         )
 
 
-def pack_kernel(line_ref, keep_ref, came_ref, out_ref, small_ref):
-    out_ref[:, :LINES] = line_ref[...]
-    for x in range(4):
-        for z in range(8):
-            for y in range(4):
-                k = 256 * (z % 4) + 8 * (2 * (4 * x + y) + z // 4)
-                tile = keep_ref[k : k + 8] + came_ref[k : k + 8]
-                high = tile.astype(BF).astype(F32)
-                out_ref[(x * 8 + z) * 4 + y, LINES:] = jnp.concatenate(
-                    [high, tile - high], axis=0
-                ).astype(BF)
+def chip_kernel(at_ref, keep_ref, came_ref, own_ref, one_ref, two_ref, three_ref, small_ref, sum_ref):
+    sum_ref[...] = keep_ref[:1024] + came_ref[:1024]
     small_ref[...] = keep_ref[1024:] + came_ref[1024:]
-
-
-def open_kernel(got_ref, small_ref, line_ref, chunk_ref):
-    line_ref[...] = got_ref[:, :LINES]
-    sums = [jnp.zeros((16, EMB), F32) for _ in range(4)]
-    for k in range(OWNERS):
-        sums[k % 4] = sums[k % 4] + got_ref[k, LINES:].astype(F32)
-    total = (sums[0] + sums[1]) + (sums[2] + sums[3])
-    tile = total[:8] + total[8:]
+    for d, ref in enumerate((own_ref, one_ref, two_ref, three_ref)):
+        ref[...] = sum_ref[pl.ds(pl.multiple_of(((at_ref[0] + d) & 3) * 256, 256), 256), :]
+
+
+def cross_kernel(
+    at_ref, mine_ref, a_ref, b_ref, c_ref, own_ref, one_ref, two_ref, three_ref, sum_ref
+):
+    sum_ref[...] = (mine_ref[...] + a_ref[...]) + (b_ref[...] + c_ref[...])
+    for d, ref in enumerate((own_ref, one_ref, two_ref, three_ref)):
+        ref[...] = sum_ref[pl.ds(pl.multiple_of(((at_ref[0] + d) & 3) * 64, 64), 64), :]
+
+
+def plane_kernel(mine_ref, a_ref, b_ref, c_ref, small_ref, out_ref):
+    total = (mine_ref[...] + a_ref[...]) + (b_ref[...] + c_ref[...])
+    small = small_ref[...]
     for k in range(8):
-        chunk_ref[k, :8] = tile
-        chunk_ref[k, 8:] = small_ref[...]
+        out_ref[k, :64] = total
+        out_ref[k, 64:] = small
 
 
 def column_kernel(got_ref, out_ref):
-    small = got_ref[0, 8:]
+    total = got_ref[0]
     for z in range(1, 8):
-        small = small + got_ref[z, 8:]
+        total = total + got_ref[z]
     for p in range(16):
-        for z in range(8):
-            out_ref[p, 8 * z : 8 * (z + 1)] = got_ref[z, :8]
-        out_ref[p, 64:] = small
+        out_ref[p] = total
 
 
 def place_kernel(
@@ -367,17 +365,28 @@
     (lines,) = call(
         back_kernel, 20, (sds((OWNERS, LINES, EMB), BF),), [VMEM] * 4
     )(pre_grad, slots, slot_cols, w_hidden)
-    message, small = call(
-        pack_kernel, 12,
-        (sds((OWNERS, 2 * LINES, EMB), BF), sds((SMALL, EMB), F32)),
-        [VMEM] * 3,
-    )(lines, keep, came)
-    got = exchange(message, TABLE)
-    incoming, chunks = call(
-        open_kernel, 12,
-        (sds((OWNERS, LINES, EMB), BF), sds((8, 8 + SMALL, EMB), F32)),
-        [VMEM] * 2,
-    )(got, small)
+    incoming = exchange(lines, TABLE)
+
+    def spread(parts, axis):
+        return [
+            lax.ppermute(part, axis, [(i, (i + d) % 4) for i in range(4)])
+            for d, part in enumerate(parts, 1)
+        ]
+
+    quarter, tiles = sds((256, EMB), F32), sds((64, EMB), F32)
+    own, *rest, small = call(
+        chip_kernel, 12, (quarter,) * 4 + (sds((SMALL, EMB), F32),), [SMEM] + [VMEM] * 2,
+        [pltpu.VMEM((1024, EMB), F32)],
+    )(lax.axis_index("y").astype(i32).reshape(1), keep, came)
+    rest = spread(rest, "y")
+    own, *rest = call(
+        cross_kernel, 12, (tiles,) * 4, [SMEM] + [VMEM] * 4,
+        [pltpu.VMEM((256, EMB), F32)],
+    )(lax.axis_index("x").astype(i32).reshape(1), own, *rest)
+    rest = spread(rest, "x")
+    (chunks,) = call(
+        plane_kernel, 12, (sds((8, 64 + SMALL, EMB), F32),), [VMEM] * 5
+    )(own, *rest, small)
     other = lax.ppermute(incoming, "dp", swap)
     column = exchange(chunks, "z")
     (emb_step,) = call(
@@ -391,8 +400,8 @@
         ],
         out_specs=(ANY,),
     )(core, incoming, other, requested, other_ids)
-    (plane,) = call(column_kernel, 12, (sds((16, 64 + SMALL, EMB), F32),), [VMEM])(column)
-    mine = exchange(plane, ("x", "y"))
+    (sums,) = call(column_kernel, 12, (sds((16, 64 + SMALL, EMB), F32),), [VMEM])(column)
+    mine = exchange(sums, ("x", "y"))
     theirs = lax.ppermute(mine, "dp", swap)
     step_hidden, step_bias, step_score, loss = call(
         final_kernel, 12,

time: 137 us -> 146 us (1.066)
  blocking collectives: 108 us -> 61.2 us
  starting transfers between devices: 9.25 us -> 36.4 us
  waiting for transfers between devices: 2.58 us -> 28.9 us
  Pallas kernels: 16.4 us -> 17.9 us
    all_to_all x5 -> x3, blocking collectives: 108 us -> 61.2 us  [exchange(): return lax.all_to_all(array, axes, split_axis=0, concat_axis=0, tiled=True)]
    all_to_all x0 -> x2, waiting for transfers between devices: none -> 18.9 us  [exchange(): return lax.all_to_all(array, axes, split_axis=0, concat_axis=0, tiled=True)]
    all_to_all x0 -> x2, starting transfers between devices: none -> 15.1 us  [exchange(): return lax.all_to_all(array, axes, split_axis=0, concat_axis=0, tiled=True)]
    ppermute x0 -> x6, starting transfers between devices: none -> 7.41 us  [spread(): lax.ppermute(part, axis, [(i, (i + d) % 4) for i in range(4)])]
    ppermute x0 -> x6, waiting for transfers between devices: none -> 6.82 us  [spread(): lax.ppermute(part, axis, [(i, (i + d) % 4) for i in range(4)])]
    ppermute x1, starting transfers between devices: 0.01 us -> 6 us  [whole_step(): other = lax.ppermute(incoming, 'dp', swap)]
  transfers between devices with their start and end apart: 4 -> 12, of which waited for: 2 -> 10; matrix products, arithmetic and copies ran while one was open for 0% -> 0% of each run, Pallas kernels for 5% -> 5%
where the time goes in v3:
time: 146 us; the launch traced here: 145 us
  blocking collectives  61.2 us (42%)
  starting transfers between devices  36.4 us (25%)
  waiting for transfers between devices  28.9 us (20%)
  Pallas kernels  17.9 us (12%)
    all_to_all x3, blocking collectives, exchange(): return lax.all_to_all(array, axes, split_axis=0, concat_axis=0, tiled=True)  61.2 us
    all_to_all x2, waiting for transfers between devices, exchange(): return lax.all_to_all(array, axes, split_axis=0, concat_axis=0, tiled=True)  18.9 us
    all_to_all x2, starting transfers between devices, exchange(): return lax.all_to_all(array, axes, split_axis=0, concat_axis=0, tiled=True)  15.1 us
    ppermute x6, starting transfers between devices, spread(): lax.ppermute(part, axis, [(i, (i + d) % 4) for i in range(4)])  7.41 us
    ppermute x6, waiting for transfers between devices, spread(): lax.ppermute(part, axis, [(i, (i + d) % 4) for i in range(4)])  6.82 us
    ppermute x1, starting transfers between devices, whole_step(): other = lax.ppermute(incoming, 'dp', swap)  6 us
    pallas_call x1, Pallas kernels, whole_step(): call(place_kernel, 28, (sds((TABLES, ROWS // 2, EMB), F32),), [SMEM] + [V...  5.33 us
    ppermute x1, starting transfers between devices, whole_step(): came = lax.ppermute(send, 'dp', swap)  4.47 us
  transfers between devices with their start and end apart: 12, of which 10 were waited for; matrix products, arithmetic and copies ran while one was open for 0% of the time, Pallas kernels for 5%

profile of v3, /device:TPU:1, one launch (start us, length us, event | category | flops | bytes accessed | tf_op | source)
XLA Modules:
  0.0 145.1 jit_solution(16135108395757712011)
XLA Ops:
  0.6 0.0 copy-start
  0.6 0.0 copy-start.2
  0.7 0.0 copy-start.1
  0.7 0.0 copy-start.5
  0.7 0.0 copy-start.4
  0.7 0.0 copy-start.3
  0.7 1.9 %shard_map.128 = (s32[128,16]{1,0:T(8,128)S(1)}, s32[4,256]{1,0:T(4,128)S(1)}, s32[256,8]{1,0:T(8,128)S(1)}) custom-call(s32[1]{0:T(128)} %bitcast.core_ref, s32[8,128]{1,0:T(8,128)} %bitcast.21, s32[4,256]{1,0:T(4,128)} %bitcast.22), custom_call_target="tpu_custom_call" | custom-call | flops 268435456 | bytes 1048576 | tf_op jit(solution)/shard_map/pallas_call | solution.py:331
  2.6 26.7 %all_to_all.31 = s32[128,1,16]{2,1,0:T(1,128)S(1)} all-to-all(s32[128,1,16]{2,1,0:T(1,128)S(1)} %bitcast.18), channel_id=1, replica_groups=mesh['x'=4,'z'=8,'y'=4,'dp'=2] {'x','z','y'}, dimensions={0} | all-to-all | bytes 16384 | tf_op jit(solution)/shard_map/all_to_all | solution.py:322
  29.3 4.3 %shard_map.129 = bf16[128,16,128]{2,1,0:T(8,128)(2,1)S(1)} custom-call(s32[128,16]{1,0:T(8,128)S(1)} %bitcast.15, bf16[4,4096,128]{2,1,0:T(8,128)(2,1)} %far_ref.1), custom_call_target="tpu_custom_call" | custom-call | flops 268435456 | bytes 1048576 | tf_op jit(solution)/shard_map/pallas_call | solution.py:343
  33.6 21.5 %all_to_all.32.ret_ref = bf16[128,16,128]{2,1,0:T(8,128)(2,1)S(1)} all-to-all(bf16[128,16,128]{2,1,0:T(8,128)(2,1)S(1)} %shard_map.129), channel_id=1, replica_groups=mesh['x'=4,'z'=8,'y'=4,'dp'=2] {'x','z','y'}, dimensions={0} | all-to-all | bytes 1048576 | tf_op jit(solution)/shard_map/all_to_all | solution.py:322
  55.1 0.0 copy-done
  55.1 0.0 copy-done.2
  55.1 0.0 copy-done.1
  55.1 0.0 copy-done.5
  55.1 0.0 copy-done.4
  55.1 0.0 copy-done.3
  55.1 2.2 %shard_map.130 = (bf16[256,512]{1,0:T(8,128)(2,1)S(1)}, f32[1040,128]{1,0:T(8,128)S(1)}, f32[1040,128]{1,0:T(8,128)S(1)}) custom-call(s32[1]{0:T(128)} %bitcast.core_ref, bf16[128,16,128]{2,1,0:T(8,128)(2,1)S(1)} %all_to_all.32.ret_ref, s32[256,8]{1,0:T(8,128)S(1)} %get-tuple-element.25.slot_col_ref, s32[1,256]{1,0:T(1,128)S(1)} %copy-done.3, ...), custom_call_target="tpu_custom_call" | custom-call | flops 268435456 | bytes 1048576 | tf_op jit(solution)/shard_map/pallas_call | solution.py:355
  57.4 4.5 %collective-permute-start.2 = (f32[1040,128]{1,0:T(8,128)S(1)}, f32[1040,128]{1,0:T(8,128)S(1)}, u32[]{:S(2)}, u32[]{:S(2)}) collective-permute-start(f32[1040,128]{1,0:T(8,128)S(1)} %get-tuple-element.29), channel_id=1, source_target_pairs={{0,1},{1,0},{2,3},{3,2},{4,5},{5,4},{6,7},{7,6},{8,9},{9,8},{10,11... | collective-permute-start | bytes 1597448 | tf_op jit(solution)/shard_map/ppermute | solution.py:364
  61.8 1.5 %collective-permute-done.2.came_ref = f32[1040,128]{1,0:T(8,128)S(1)} collective-permute-done((f32[1040,128]{1,0:T(8,128)S(1)}, f32[1040,128]{1,0:T(8,128)S(1)}, u32[]{:S(2)}, u32[]{:S(2)}) %collective-permute-start.2) | collective-permute-done | bytes 532512 | tf_op jit(solution)/shard_map/ppermute | solution.py:364
  63.4 0.1 shard_map.133
  63.5 0.4 collective-permute-start.3
  63.8 1.8 %collective-permute-start.4 = (f32[256,128]{1,0:T(8,128)S(1)}, f32[256,128]{1,0:T(8,128)S(1)}, u32[]{:S(2)}, u32[]{:S(2)}) collective-permute-start(f32[256,128]{1,0:T(8,128)S(1)} %get-tuple-element.32), channel_id=1, source_target_pairs={{0,4},{2,6},{4,0},{6,2},{1,5},{3,7},{5,1},{7,3},{8,12},{10,14},{12... | collective-permute-start | bytes 393224 | tf_op jit(solution)/shard_map/ppermute | solution.py:372
  65.6 1.4 collective-permute-start.5
  67.0 3.1 %collective-permute-done.3.a_ref = f32[256,128]{1,0:T(8,128)S(1)} collective-permute-done((f32[256,128]{1,0:T(8,128)S(1)}, f32[256,128]{1,0:T(8,128)S(1)}, u32[]{:S(2)}, u32[]{:S(2)}) %collective-permute-start.3) | collective-permute-done | bytes 131104 | tf_op jit(solution)/shard_map/ppermute | solution.py:372
  70.1 1.6 %collective-permute-done.4.b_ref = f32[256,128]{1,0:T(8,128)S(1)} collective-permute-done((f32[256,128]{1,0:T(8,128)S(1)}, f32[256,128]{1,0:T(8,128)S(1)}, u32[]{:S(2)}, u32[]{:S(2)}) %collective-permute-start.4) | collective-permute-done | bytes 131104 | tf_op jit(solution)/shard_map/ppermute | solution.py:372
  71.7 0.9 collective-permute-done.5.c_ref
  72.6 0.4 collective-permute-start.6
  73.0 1.5 %collective-permute-start.7 = (f32[64,128]{1,0:T(8,128)S(1)}, f32[64,128]{1,0:T(8,128)S(1)}, u32[]{:S(2)}, u32[]{:S(2)}) collective-permute-start(f32[64,128]{1,0:T(8,128)S(1)} %get-tuple-element.36), channel_id=1, source_target_pairs={{0,128},{64,192},{128,0},{192,64},{1,129},{65,193},{129,1},{193,65... | collective-permute-start | bytes 98312 | tf_op jit(solution)/shard_map/ppermute | solution.py:372
  74.5 2.0 %collective-permute-start.8 = (f32[64,128]{1,0:T(8,128)S(1)}, f32[64,128]{1,0:T(8,128)S(1)}, u32[]{:S(2)}, u32[]{:S(2)}) collective-permute-start(f32[64,128]{1,0:T(8,128)S(1)} %get-tuple-element.37), channel_id=1, source_target_pairs={{0,192},{64,0},{128,64},{192,128},{1,193},{65,1},{129,65},{193,129... | collective-permute-start | bytes 98312 | tf_op jit(solution)/shard_map/ppermute | solution.py:372
  76.5 0.3 collective-permute-done.6.a_ref
  76.8 0.4 collective-permute-done.7.b_ref
  77.3 0.5 collective-permute-done.8.c_ref
  77.8 13.0 %all_to_all.33.got_ref = f32[8,80,128]{2,1,0:T(8,128)S(1)} all-to-all(f32[8,80,128]{2,1,0:T(8,128)S(1)} %shard_map.135), channel_id=1, replica_groups=mesh['x'=4,'z'=8,'y'=4,'dp'=2] {'z'}, dimensions={0} | all-to-all | bytes 655360 | tf_op jit(solution)/shard_map/all_to_all | solution.py:322
  90.8 0.9 shard_map.136
  91.6 7.2 %all-to-all-start.4 = ((f32[16,80,128]{2,1,0:T(8,128)}), f32[16,80,128]{2,1,0:T(8,128)S(1)}, u32[]{:S(2)}, u32[]{:S(2)}) async-start(f32[16,80,128]{2,1,0:T(8,128)} %shard_map.136), calls=%async_computation.4 | async-start | bytes 1310720 | tf_op jit(solution)/shard_map/all_to_all | solution.py:322
  98.8 1.8 %shard_map.131 = bf16[128,16,128]{2,1,0:T(8,128)(2,1)} custom-call(bf16[256,512]{1,0:T(8,128)(2,1)S(1)} %get-tuple-element.26.pre_grad_ref, s32[4,256]{1,0:T(4,128)S(1)} %get-tuple-element.27.slot_ref, s32[256,8]{1,0:T(8,128)S(1)} %get-tuple-element.25.slot_col_ref, f32[512,512]{1,0:T(8,128)S(1)} %copy-done), custom_call_target="tpu_custom_call" | custom-call | flops 268435456 | bytes 1048576 | tf_op jit(solution)/shard_map/pallas_call | solution.py:365
  100.6 7.9 %all-to-all-done.4.own_ref = f32[16,80,128]{2,1,0:T(8,128)S(1)} async-done(((f32[16,80,128]{2,1,0:T(8,128)}), f32[16,80,128]{2,1,0:T(8,128)S(1)}, u32[]{:S(2)}, u32[]{:S(2)}) %all-to-all-start.4) | async-done | bytes 655392 | tf_op jit(solution)/shard_map/all_to_all | solution.py:322
  108.6 8.0 %all-to-all-start.2 = ((bf16[128,16,128]{2,1,0:T(8,128)(2,1)}), bf16[128,16,128]{2,1,0:T(8,128)(2,1)S(1)}, u32[]{:S(2)}, u32[]{:S(2)}) async-start(bf16[128,16,128]{2,1,0:T(8,128)(2,1)} %shard_map.131), calls=%async_computation.2 | async-start | bytes 1048576 | tf_op jit(solution)/shard_map/all_to_all | solution.py:322
  116.5 3.3 %collective-permute-start.9 = (f32[16,80,128]{2,1,0:T(8,128)S(1)}, f32[16,80,128]{2,1,0:T(8,128)S(1)}, u32[]{:S(2)}, u32[]{:S(2)}) collective-permute-start(f32[16,80,128]{2,1,0:T(8,128)S(1)} %all-to-all-done.4.own_ref), channel_id=1, source_target_pairs={{0,1},{1,0},{2,3},{3,2},{4,5},{5,4},{6,7},{7,6},{8,9},{9,8},{10,11... | collective-permute-start | bytes 1966088 | tf_op jit(solution)/shard_map/ppermute | solution.py:405
  119.9 11.0 %all-to-all-done.2.own_ref = bf16[128,16,128]{2,1,0:T(8,128)(2,1)S(1)} async-done(((bf16[128,16,128]{2,1,0:T(8,128)(2,1)}), bf16[128,16,128]{2,1,0:T(8,128)(2,1)S(1)}, u32[]{:S(2)}, u32[]{:S(2)}) %all-to-all-start.2) | async-done | bytes 524320 | tf_op jit(solution)/shard_map/all_to_all | solution.py:322
  130.9 6.0 %collective-permute-start = (bf16[128,16,128]{2,1,0:T(8,128)(2,1)S(1)}, bf16[128,16,128]{2,1,0:T(8,128)(2,1)S(1)}, u32[]{:S(2)}, u32[]{:S(2)}) collective-permute-start(bf16[128,16,128]{2,1,0:T(8,128)(2,1)S(1)} %all-to-all-done.2.own_ref), channel_id=1, source_target_pairs={{0,1},{1,0},{2,3},{3,2},{4,5},{5,4},{6,7},{7,6},{8,9},{9,8},{10,11... | collective-permute-start | bytes 1572872 | tf_op jit(solution)/shard_map/ppermute | solution.py:390
  136.9 0.0 collective-permute-start.1
  136.9 1.6 %collective-permute-done.1.other_id_ref = s32[128,16]{1,0:T(8,128)S(1)} collective-permute-done((s32[128,16]{1,0:T(8,128)S(1)}, s32[128,16]{1,0:T(8,128)S(1)}, u32[]{:S(2)}, u32[]{:S(2)}) %collective-permute-start.1) | collective-permute-done | bytes 8224 | tf_op jit(solution)/shard_map/ppermute | solution.py:342
  138.5 0.0 collective-permute-done.other_ref
  138.5 5.3 %shard_map.132 = f32[4,2048,128]{2,1,0:T(8,128)} custom-call(s32[1]{0:T(128)} %bitcast.core_ref, bf16[128,16,128]{2,1,0:T(8,128)(2,1)S(1)} %all-to-all-done.2.own_ref, bf16[128,16,128]{2,1,0:T(8,128)(2,1)S(1)} %collective-permute-done.other_ref, s32[128,16]{1,0:T(8,128)S(1)} %bitcast.17, s32[128,16]{1,0:T(8,128)S(1)} %collective-permute-done.1.other_id_ref), custom_call_target="tpu_custom_call" | custom-call | flops 268435456 | bytes 1048576 | tf_op jit(solution)/shard_map/pallas_call | solution.py:392
  143.8 0.0 collective-permute-done.9.other_ref
  143.9 1.3 shard_map.137
  (2 shorter events, 0.1 us)
Async XLA Ops:
  0.6 54.5 %copy-start = (f32[512,512]{1,0:T(8,128)S(1)}, f32[512,512]{1,0:T(8,128)}, u32[]{:S(2)}) copy-start(f32[512,512]{1,0:T(8,128)} %w_ref.3) | copy-start | bytes 3145732
  0.6 54.5 %copy-start.2 = (f32[512]{0:T(512)S(1)}, f32[512]{0:T(512)}, u32[]{:S(2)}) copy-start(f32[512]{0:T(512)} %param.17) | copy-start | bytes 6148
  0.7 54.5 %copy-start.1 = (f32[512]{0:T(512)S(1)}, f32[512]{0:T(512)}, u32[]{:S(2)}) copy-start(f32[512]{0:T(512)} %param.16) | copy-start | bytes 6148
  0.7 54.5 %copy-start.5 = (f32[1,256]{1,0:T(1,128)S(1)}, f32[1,256]{1,0:T(1,128)}, u32[]{:S(2)}) copy-start(f32[1,256]{1,0:T(1,128)} %lb_ref.1) | copy-start | bytes 3076
  0.7 54.5 %copy-start.4 = (f32[1,256]{1,0:T(1,128)S(1)}, f32[1,256]{1,0:T(1,128)}, u32[]{:S(2)}) copy-start(f32[1,256]{1,0:T(1,128)} %rel_ref.1) | copy-start | bytes 3076
  0.7 54.5 %copy-start.3 = (s32[1,256]{1,0:T(1,128)S(1)}, s32[1,256]{1,0:T(1,128)}, u32[]{:S(2)}) copy-start(s32[1,256]{1,0:T(1,128)} %ses_ref.1) | copy-start | bytes 3076
  57.4 6.0 %collective-permute-start.2 = (f32[1040,128]{1,0:T(8,128)S(1)}, f32[1040,128]{1,0:T(8,128)S(1)}, u32[]{:S(2)}, u32[]{:S(2)}) collective-permute-start(f32[1040,128]{1,0:T(8,128)S(1)} %get-tuple-element.29), channel_id=1, source_target_pairs={{0,1},{1,0},{2,3},{3,2},{4,5},{5,4},{6,7},{7,6},{8,9},{9,8},{10,11... | collective-permute-start | bytes 1597448 | tf_op jit(solution)/shard_map/ppermute | solution.py:364
  63.5 6.6 %collective-permute-start.3 = (f32[256,128]{1,0:T(8,128)S(1)}, f32[256,128]{1,0:T(8,128)S(1)}, u32[]{:S(2)}, u32[]{:S(2)}) collective-permute-start(f32[256,128]{1,0:T(8,128)S(1)} %get-tuple-element.31), channel_id=1, source_target_pairs={{0,2},{2,4},{4,6},{6,0},{1,3},{3,5},{5,7},{7,1},{8,10},{10,12},{12... | collective-permute-start | bytes 393224 | tf_op jit(solution)/shard_map/ppermute | solution.py:372
  63.8 7.8 %collective-permute-start.4 = (f32[256,128]{1,0:T(8,128)S(1)}, f32[256,128]{1,0:T(8,128)S(1)}, u32[]{:S(2)}, u32[]{:S(2)}) collective-permute-start(f32[256,128]{1,0:T(8,128)S(1)} %get-tuple-element.32), channel_id=1, source_target_pairs={{0,4},{2,6},{4,0},{6,2},{1,5},{3,7},{5,1},{7,3},{8,12},{10,14},{12... | collective-permute-start | bytes 393224 | tf_op jit(solution)/shard_map/ppermute | solution.py:372
  65.6 7.0 %collective-permute-start.5 = (f32[256,128]{1,0:T(8,128)S(1)}, f32[256,128]{1,0:T(8,128)S(1)}, u32[]{:S(2)}, u32[]{:S(2)}) collective-permute-start(f32[256,128]{1,0:T(8,128)S(1)} %get-tuple-element.33), channel_id=1, source_target_pairs={{0,6},{2,0},{4,2},{6,4},{1,7},{3,1},{5,3},{7,5},{8,14},{10,8},{12,... | collective-permute-start | bytes 393224 | tf_op jit(solution)/shard_map/ppermute | solution.py:372
  72.6 4.2 %collective-permute-start.6 = (f32[64,128]{1,0:T(8,128)S(1)}, f32[64,128]{1,0:T(8,128)S(1)}, u32[]{:S(2)}, u32[]{:S(2)}) collective-permute-start(f32[64,128]{1,0:T(8,128)S(1)} %get-tuple-element.35), channel_id=1, source_target_pairs={{0,64},{64,128},{128,192},{192,0},{1,65},{65,129},{129,193},{193,1... | collective-permute-start | bytes 98312 | tf_op jit(solution)/shard_map/ppermute | solution.py:372
  73.0 4.3 %collective-permute-start.7 = (f32[64,128]{1,0:T(8,128)S(1)}, f32[64,128]{1,0:T(8,128)S(1)}, u32[]{:S(2)}, u32[]{:S(2)}) collective-permute-start(f32[64,128]{1,0:T(8,128)S(1)} %get-tuple-element.36), channel_id=1, source_target_pairs={{0,128},{64,192},{128,0},{192,64},{1,129},{65,193},{129,1},{193,65... | collective-permute-start | bytes 98312 | tf_op jit(solution)/shard_map/ppermute | solution.py:372
  74.5 3.2 %collective-permute-start.8 = (f32[64,128]{1,0:T(8,128)S(1)}, f32[64,128]{1,0:T(8,128)S(1)}, u32[]{:S(2)}, u32[]{:S(2)}) collective-permute-start(f32[64,128]{1,0:T(8,128)S(1)} %get-tuple-element.37), channel_id=1, source_target_pairs={{0,192},{64,0},{128,64},{192,128},{1,193},{65,1},{129,65},{193,129... | collective-permute-start | bytes 98312 | tf_op jit(solution)/shard_map/ppermute | solution.py:372
  91.6 16.9 %all-to-all-start.4 = ((f32[16,80,128]{2,1,0:T(8,128)}), f32[16,80,128]{2,1,0:T(8,128)S(1)}, u32[]{:S(2)}, u32[]{:S(2)}) async-start(f32[16,80,128]{2,1,0:T(8,128)} %shard_map.136), calls=%async_computation.4 | async-start | bytes 1310720 | tf_op jit(solution)/shard_map/all_to_all | solution.py:322
  108.6 22.3 %all-to-all-start.2 = ((bf16[128,16,128]{2,1,0:T(8,128)(2,1)}), bf16[128,16,128]{2,1,0:T(8,128)(2,1)S(1)}, u32[]{:S(2)}, u32[]{:S(2)}) async-start(bf16[128,16,128]{2,1,0:T(8,128)(2,1)} %shard_map.131), calls=%async_computation.2 | async-start | bytes 1048576 | tf_op jit(solution)/shard_map/all_to_all | solution.py:322
  116.5 27.3 %collective-permute-start.9 = (f32[16,80,128]{2,1,0:T(8,128)S(1)}, f32[16,80,128]{2,1,0:T(8,128)S(1)}, u32[]{:S(2)}, u32[]{:S(2)}) collective-permute-start(f32[16,80,128]{2,1,0:T(8,128)S(1)} %all-to-all-done.4.own_ref), channel_id=1, source_target_pairs={{0,1},{1,0},{2,3},{3,2},{4,5},{5,4},{6,7},{7,6},{8,9},{9,8},{10,11... | collective-permute-start | bytes 1966088 | tf_op jit(solution)/shard_map/ppermute | solution.py:405
  130.9 7.6 %collective-permute-start = (bf16[128,16,128]{2,1,0:T(8,128)(2,1)S(1)}, bf16[128,16,128]{2,1,0:T(8,128)(2,1)S(1)}, u32[]{:S(2)}, u32[]{:S(2)}) collective-permute-start(bf16[128,16,128]{2,1,0:T(8,128)(2,1)S(1)} %all-to-all-done.2.own_ref), channel_id=1, source_target_pairs={{0,1},{1,0},{2,3},{3,2},{4,5},{5,4},{6,7},{7,6},{8,9},{9,8},{10,11... | collective-permute-start | bytes 1572872 | tf_op jit(solution)/shard_map/ppermute | solution.py:390
  136.9 1.6 %collective-permute-start.1 = (s32[128,16]{1,0:T(8,128)S(1)}, s32[128,16]{1,0:T(8,128)S(1)}, u32[]{:S(2)}, u32[]{:S(2)}) collective-permute-start(s32[128,16]{1,0:T(8,128)S(1)} %bitcast.16), channel_id=1, source_target_pairs={{0,1},{1,0},{2,3},{3,2},{4,5},{5,4},{6,7},{7,6},{8,9},{9,8},{10,11... | collective-permute-start | bytes 24584 | tf_op jit(solution)/shard_map/ppermute | solution.py:342

commit v4 on v2

--- a/solution.py
+++ b/solution.py
@@ -18,7 +18,7 @@
 ROWS = 4096
 HID = 512
 FOLD = 4
-SMALL = 16
+SMALL = 8
 VMEM = pl.BlockSpec(memory_space=pltpu.VMEM)
 ANY = pl.BlockSpec(memory_space=pl.ANY)
 BF = jnp.bfloat16
@@ -169,15 +169,15 @@
         columns = slice(EMB * q, EMB * (q + 1))
         keep_ref[256 * q : 256 * (q + 1)] = dense_ref[pl.ds(start, 256), columns]
         send_ref[256 * q : 256 * (q + 1)] = dense_ref[pl.ds(256 - start, 256), columns]
-    small = jnp.concatenate(
-        [bias_grad[:, EMB * q : EMB * (q + 1)] for q in range(4)]
-        + [score_w_grad[:, EMB * q : EMB * (q + 1)] for q in range(4)]
-        + [jnp.broadcast_to(loss, (1, EMB))]
-        + [jnp.zeros((7, EMB), F32)],
-        axis=0,
-    )
-    keep_ref[1024:] = small
-    send_ref[1024:] = small
+    def rows_of(line, last):
+        parts = [line[:, EMB * q : EMB * (q + 1)] for q in range(4)]
+        return jnp.concatenate(parts + [last] + [jnp.zeros((3, EMB), F32)], axis=0)
+
+    first_core = jnp.broadcast_to(core_ref[0], (8, EMB)) == 0
+    for_zero = rows_of(bias_grad, jnp.broadcast_to(loss, (1, EMB)))
+    for_one = rows_of(score_w_grad, jnp.zeros((1, EMB), F32))
+    keep_ref[1024:] = jnp.where(first_core, for_zero, for_one)
+    send_ref[1024:] = jnp.where(first_core, for_one, for_zero)
 
 
 def back_kernel(pre_grad_ref, slot_ref, slot_col_ref, w_ref, out_ref):
@@ -214,8 +214,11 @@
     small_ref[...] = keep_ref[1024:] + came_ref[1024:]
 
 
-def open_kernel(got_ref, small_ref, line_ref, chunk_ref):
-    line_ref[...] = got_ref[:, :LINES]
+def open_kernel(got_ref, small_ref, id_ref, line_ref, chunk_ref):
+    line_ref[:OWNERS] = got_ref[:, :LINES]
+    ids = jnp.transpose(id_ref[...])
+    line_ref[OWNERS] = (ids >> 6).astype(F32).astype(BF)
+    line_ref[OWNERS + 1] = (ids & 63).astype(F32).astype(BF)
     sums = [jnp.zeros((16, EMB), F32) for _ in range(4)]
     for k in range(OWNERS):
         sums[k % 4] = sums[k % 4] + got_ref[k, LINES:].astype(F32)
@@ -237,14 +240,17 @@
 
 
 def place_kernel(
-    core_ref, own_ref, other_ref, own_id_ref, other_id_ref, out_ref, wide_ref, buf_ref, sems
+    core_ref, own_ref, other_ref, out_ref, wide_ref, buf_ref, sems
 ):
     core = core_ref[0]
     lines = OWNERS * LINES
-    wide_ref[:lines] = own_ref[...].reshape(lines, EMB).astype(F32)
-    wide_ref[lines:] = other_ref[...].reshape(lines, EMB).astype(F32)
-    cols = [own_id_ref[...], other_id_ref[...]]
-    rows = [jnp.transpose(c) for c in cols]
+    wide_ref[:lines] = own_ref[:OWNERS].reshape(lines, EMB).astype(F32)
+    wide_ref[lines:] = other_ref[:OWNERS].reshape(lines, EMB).astype(F32)
+    rows = [
+        ref[OWNERS].astype(F32).astype(jnp.int32) * 64 + ref[OWNERS + 1].astype(F32).astype(jnp.int32)
+        for ref in (own_ref, other_ref)
+    ]
+    cols = [jnp.transpose(r) for r in rows]
     part = ROWS // 2 // FOLD
     copies = []
     for t in range(TABLES):
@@ -271,22 +277,33 @@
         copy.wait()
 
 
-def final_kernel(core_ref, own_ref, other_ref, w_ref, b_ref, s_ref, loss_ref):
+def squares_of(ref):
+    sums = [jnp.zeros((8, EMB), F32) for _ in range(4)]
+    for p in range(16):
+        for z in range(8):
+            tile = ref[p, 8 * z : 8 * (z + 1)]
+            sums[z % 4] = sums[z % 4] + tile * tile
+    small = ref[0, 64:]
+    for p in range(1, 16):
+        small = small + ref[p, 64:]
+    return (sums[0] + sums[1]) + (sums[2] + sums[3]), small
+
+
+def square_kernel(own_ref, main_ref, small_ref):
+    main_ref[...], small_ref[...] = squares_of(own_ref)
+
+
+def final_kernel(
+    core_ref, own_ref, other_ref, own_main_ref, own_small_ref, w_ref, b_ref, s_ref, loss_ref
+):
     start = core_ref[0] * 256
-    small = own_ref[0, 64:]
-    for p in range(1, 16):
-        small = small + own_ref[p, 64:]
-    kept = small[0:8]
-    square = jnp.sum(kept * kept, axis=0, keepdims=True)
-    halves = []
-    for ref in (own_ref, other_ref):
-        sums = [jnp.zeros((8, EMB), F32) for _ in range(4)]
-        for p in range(16):
-            for z in range(8):
-                tile = ref[p, 8 * z : 8 * (z + 1)]
-                sums[z % 4] = sums[z % 4] + tile * tile
-        halves.append((sums[0] + sums[1]) + (sums[2] + sums[3]))
-    main = halves[0] + halves[1]
+    other_main, other_small = squares_of(other_ref)
+    own_small = own_small_ref[...]
+    first_core = jnp.broadcast_to(core_ref[0], (8, EMB)) == 0
+    bias = jnp.where(first_core, own_small, other_small)
+    score = jnp.where(first_core, other_small, own_small)
+    square = jnp.sum(bias[0:4] * bias[0:4] + score[0:4] * score[0:4], axis=0, keepdims=True)
+    main = own_main_ref[...] + other_main
     square = jnp.sum(square + jnp.sum(main, axis=0, keepdims=True), axis=1, keepdims=True)
     factor = 1.0 / jnp.sqrt(square * (1.0 / (HID * HID + 2 * HID)) + 1e-06)
     for p in range(16):
@@ -299,9 +316,9 @@
             w_ref[pl.ds(pl.multiple_of(256 - start + row, 8), 8), columns] = (
                 other_ref[p, 8 * z : 8 * (z + 1)] * factor
             )
-    b_ref[...] = small[0:4] * factor
-    s_ref[...] = small[4:8] * factor
-    loss_ref[...] = small[8:9] * (1.0 / 512)
+    b_ref[...] = bias[0:4] * factor
+    s_ref[...] = score[0:4] * factor
+    loss_ref[...] = bias[4:5] * (1.0 / 512)
 
 
 def sds(shape, dtype):
@@ -341,7 +358,6 @@
         pltpu.with_memory_space_constraint(row_ids.reshape(TABLES, IMPS), pltpu.HBM),
     )
     requested = exchange(wanted, TABLE)
-    other_ids = lax.ppermute(requested, "dp", swap)
     (served,) = call(
         serve_kernel, 24,
         (sds((OWNERS, LINES, EMB), BF),),
@@ -375,30 +391,32 @@
     got = exchange(message, TABLE)
     incoming, chunks = call(
         open_kernel, 12,
-        (sds((OWNERS, LINES, EMB), BF), sds((8, 8 + SMALL, EMB), F32)),
-        [VMEM] * 2,
-    )(got, small)
+        (sds((OWNERS + 2, LINES, EMB), BF), sds((8, 8 + SMALL, EMB), F32)),
+        [VMEM] * 3,
+    )(got, small, requested)
     other = lax.ppermute(incoming, "dp", swap)
     column = exchange(chunks, "z")
     (emb_step,) = call(
         place_kernel, 28,
         (sds((TABLES, ROWS // 2, EMB), F32),),
-        [SMEM] + [VMEM] * 4,
+        [SMEM] + [VMEM] * 2,
         [
             pltpu.VMEM((2 * OWNERS * LINES, EMB), F32),
             pltpu.VMEM((TABLES, ROWS // 2, EMB), F32),
             pltpu.SemaphoreType.DMA((TABLES,)),
         ],
         out_specs=(ANY,),
-    )(core, incoming, other, requested, other_ids)
+    )(core, incoming, other)
     (plane,) = call(column_kernel, 12, (sds((16, 64 + SMALL, EMB), F32),), [VMEM])(column)
     mine = exchange(plane, ("x", "y"))
     theirs = lax.ppermute(mine, "dp", swap)
+    tile = sds((8, EMB), F32)
+    own_main, own_small = call(square_kernel, 8, (tile, tile), [VMEM])(mine)
     step_hidden, step_bias, step_score, loss = call(
         final_kernel, 12,
         (sds((HID, HID), F32), sds((4, 128), F32), sds((4, 128), F32), sds((1, 128), F32)),
-        [SMEM] + [VMEM] * 2,
-    )(core, mine, theirs)
+        [SMEM] + [VMEM] * 4,
+    )(core, mine, theirs, own_main, own_small)
     return emb_step, step_hidden, step_bias.reshape(HID), step_score.reshape(HID), loss[0, 0]
 
 

time: 137 us -> 136 us (level)
    ppermute x1, waiting for transfers between devices: 0.01 us -> 2.39 us  [whole_step(): other = lax.ppermute(incoming, 'dp', swap)]
    ppermute x1 -> x0, waiting for transfers between devices: 2.06 us -> none  [whole_step(): other_ids = lax.ppermute(requested, 'dp', swap)]
  transfers between devices with their start and end apart: 4 -> 3, of which waited for: 2 -> 2; matrix products, arithmetic and copies ran while one was open for 0% -> 0% of each run, Pallas kernels for 5% -> 5%
where the time goes in v4:
time: 136 us
  blocking collectives  107 us (79%)
  Pallas kernels  16.4 us (12%)
  starting transfers between devices  8.75 us (6%)
  waiting for transfers between devices  2.9 us (2%)
    all_to_all x5, blocking collectives, exchange(): return lax.all_to_all(array, axes, split_axis=0, concat_axis=0, tiled=True)  107 us
    pallas_call x1, Pallas kernels, whole_step(): call(place_kernel, 28, (sds((TABLES, ROWS // 2, EMB), F32),), [SMEM] + [V...  5.34 us
    ppermute x1, starting transfers between devices, whole_step(): came = lax.ppermute(send, 'dp', swap)  4.48 us
    pallas_call x1, Pallas kernels, whole_step(): call(serve_kernel, 24, (sds((OWNERS, LINES, EMB), BF),), [VMEM, HBM], [pl...  4.33 us
    ppermute x1, starting transfers between devices, whole_step(): theirs = lax.ppermute(mine, 'dp', swap)  4.26 us
  transfers between devices with their start and end apart: 3, of which 2 were waited for; matrix products, arithmetic and copies ran while one was open for 0% of the time, Pallas kernels for 5%

profile of v4, /device:TPU:1, one launch (start us, length us, event | category | flops | bytes accessed | tf_op | source)
XLA Modules:
  0.0 136.0 jit_solution(11431800643834817713)
XLA Ops:
  0.6 0.0 copy-start
  0.6 0.0 copy-start.2
  0.7 0.0 copy-start.1
  0.7 0.0 copy-start.5
  0.7 0.0 copy-start.4
  0.7 0.0 copy-start.3
  0.7 1.9 %shard_map.128 = (s32[128,16]{1,0:T(8,128)S(1)}, s32[4,256]{1,0:T(4,128)S(1)}, s32[256,8]{1,0:T(8,128)S(1)}) custom-call(s32[1]{0:T(128)} %bitcast.core_ref, s32[8,128]{1,0:T(8,128)} %bitcast.18, s32[4,256]{1,0:T(4,128)} %bitcast.19), custom_call_target="tpu_custom_call" | custom-call | flops 268435456 | bytes 1048576 | tf_op jit(solution)/shard_map/pallas_call | solution.py:350
  2.6 26.7 %all_to_all.31 = s32[128,1,16]{2,1,0:T(1,128)S(1)} all-to-all(s32[128,1,16]{2,1,0:T(1,128)S(1)} %bitcast.15), channel_id=1, replica_groups=mesh['x'=4,'z'=8,'y'=4,'dp'=2] {'x','z','y'}, dimensions={0} | all-to-all | bytes 16384 | tf_op jit(solution)/shard_map/all_to_all | solution.py:341
  29.3 4.3 %shard_map.129 = bf16[128,16,128]{2,1,0:T(8,128)(2,1)S(1)} custom-call(s32[128,16]{1,0:T(8,128)S(1)} %bitcast.13, bf16[4,4096,128]{2,1,0:T(8,128)(2,1)} %far_ref.1), custom_call_target="tpu_custom_call" | custom-call | flops 268435456 | bytes 1048576 | tf_op jit(solution)/shard_map/pallas_call | solution.py:361
  33.6 21.5 %all_to_all.32.ret_ref = bf16[128,16,128]{2,1,0:T(8,128)(2,1)S(1)} all-to-all(bf16[128,16,128]{2,1,0:T(8,128)(2,1)S(1)} %shard_map.129), channel_id=1, replica_groups=mesh['x'=4,'z'=8,'y'=4,'dp'=2] {'x','z','y'}, dimensions={0} | all-to-all | bytes 1048576 | tf_op jit(solution)/shard_map/all_to_all | solution.py:341
  55.1 0.0 copy-done
  55.1 0.0 copy-done.2
  55.1 0.0 copy-done.1
  55.1 0.0 copy-done.5
  55.1 0.0 copy-done.4
  55.1 0.0 copy-done.3
  55.1 2.2 %shard_map.130 = (bf16[256,512]{1,0:T(8,128)(2,1)S(1)}, f32[1032,128]{1,0:T(8,128)S(1)}, f32[1032,128]{1,0:T(8,128)S(1)}) custom-call(s32[1]{0:T(128)} %bitcast.core_ref, bf16[128,16,128]{2,1,0:T(8,128)(2,1)S(1)} %all_to_all.32.ret_ref, s32[256,8]{1,0:T(8,128)S(1)} %get-tuple-element.22.slot_col_ref, s32[1,256]{1,0:T(1,128)S(1)} %copy-done.3, ...), custom_call_target="tpu_custom_call" | custom-call | flops 268435456 | bytes 1048576 | tf_op jit(solution)/shard_map/pallas_call | solution.py:373
  57.3 4.5 %collective-permute-start = (f32[1032,128]{1,0:T(8,128)S(1)}, f32[1032,128]{1,0:T(8,128)S(1)}, u32[]{:S(2)}, u32[]{:S(2)}) collective-permute-start(f32[1032,128]{1,0:T(8,128)S(1)} %get-tuple-element.26), channel_id=1, source_target_pairs={{0,1},{1,0},{2,3},{3,2},{4,5},{5,4},{6,7},{7,6},{8,9},{9,8},{10,11... | collective-permute-start | bytes 1585160 | tf_op jit(solution)/shard_map/ppermute | solution.py:382
  61.8 1.0 shard_map.131.line_ref
  62.8 0.5 collective-permute-done.came_ref
  63.4 0.1 shard_map.132
  63.5 33.9 %all_to_all.33.got_ref = bf16[128,32,128]{2,1,0:T(8,128)(2,1)S(1)} all-to-all(bf16[128,32,128]{2,1,0:T(8,128)(2,1)S(1)} %get-tuple-element.27), channel_id=1, replica_groups=mesh['x'=4,'z'=8,'y'=4,'dp'=2] {'x','z','y'}, dimensions={0} | all-to-all | bytes 2097152 | tf_op jit(solution)/shard_map/all_to_all | solution.py:341
  97.4 0.1 shard_map.133
  97.5 13.0 %all_to_all.34.got_ref = f32[8,16,128]{2,1,0:T(8,128)S(1)} all-to-all(f32[8,16,128]{2,1,0:T(8,128)S(1)} %get-tuple-element.30), channel_id=1, replica_groups=mesh['x'=4,'z'=8,'y'=4,'dp'=2] {'z'}, dimensions={0} | all-to-all | bytes 131072 | tf_op jit(solution)/shard_map/all_to_all | solution.py:341
  110.6 12.1 %all_to_all.35.own_ref = f32[16,72,128]{2,1,0:T(8,128)S(1)} all-to-all(f32[16,72,128]{2,1,0:T(8,128)S(1)} %shard_map.135), channel_id=1, replica_groups=mesh['x'=4,'z'=8,'y'=4,'dp'=2] {'x','y'}, dimensions={0} | all-to-all | bytes 1179648 | tf_op jit(solution)/shard_map/all_to_all | solution.py:341
  122.6 4.3 %collective-permute-start.2 = (f32[16,72,128]{2,1,0:T(8,128)S(1)}, f32[16,72,128]{2,1,0:T(8,128)S(1)}, u32[]{:S(2)}, u32[]{:S(2)}) collective-permute-start(f32[16,72,128]{2,1,0:T(8,128)S(1)} %all_to_all.35.own_ref), channel_id=1, source_target_pairs={{0,1},{1,0},{2,3},{3,2},{4,5},{5,4},{6,7},{7,6},{8,9},{9,8},{10,11... | collective-permute-start | bytes 1769480 | tf_op jit(solution)/shard_map/ppermute | solution.py:412
  126.9 0.0 collective-permute-start.1
  126.9 2.4 %collective-permute-done.1.other_ref = bf16[130,16,128]{2,1,0:T(8,128)(2,1)S(1)} collective-permute-done((bf16[130,16,128]{2,1,0:T(8,128)(2,1)S(1)}, bf16[130,16,128]{2,1,0:T(8,128)(2,1)S(1)}, u32[]{:S(2)}, u32[]{:S(2)}) %collective-permute-start.1) | collective-permute-done | bytes 532512 | tf_op jit(solution)/shard_map/ppermute | solution.py:397
  129.3 5.3 %shard_map.134 = f32[4,2048,128]{2,1,0:T(8,128)} custom-call(s32[1]{0:T(128)} %bitcast.core_ref, bf16[130,16,128]{2,1,0:T(8,128)(2,1)S(1)} %get-tuple-element.29.own_ref, bf16[130,16,128]{2,1,0:T(8,128)(2,1)S(1)} %collective-permute-done.1.other_ref), custom_call_target="tpu_custom_call" | custom-call | flops 268435456 | bytes 1048576 | tf_op jit(solution)/shard_map/pallas_call | solution.py:399
  134.6 0.1 shard_map.136
  134.7 0.0 collective-permute-done.2.other_ref
  134.7 1.3 shard_map.137
  (1 shorter events, 0.0 us)
Async XLA Ops:
  0.6 54.5 %copy-start = (f32[512,512]{1,0:T(8,128)S(1)}, f32[512,512]{1,0:T(8,128)}, u32[]{:S(2)}) copy-start(f32[512,512]{1,0:T(8,128)} %w_ref.3) | copy-start | bytes 3145732
  0.6 54.5 %copy-start.2 = (f32[512]{0:T(512)S(1)}, f32[512]{0:T(512)}, u32[]{:S(2)}) copy-start(f32[512]{0:T(512)} %param.17) | copy-start | bytes 6148
  0.7 54.5 %copy-start.1 = (f32[512]{0:T(512)S(1)}, f32[512]{0:T(512)}, u32[]{:S(2)}) copy-start(f32[512]{0:T(512)} %param.16) | copy-start | bytes 6148
  0.7 54.5 %copy-start.5 = (f32[1,256]{1,0:T(1,128)S(1)}, f32[1,256]{1,0:T(1,128)}, u32[]{:S(2)}) copy-start(f32[1,256]{1,0:T(1,128)} %lb_ref.1) | copy-start | bytes 3076
  0.7 54.5 %copy-start.4 = (f32[1,256]{1,0:T(1,128)S(1)}, f32[1,256]{1,0:T(1,128)}, u32[]{:S(2)}) copy-start(f32[1,256]{1,0:T(1,128)} %rel_ref.1) | copy-start | bytes 3076
  0.7 54.5 %copy-start.3 = (s32[1,256]{1,0:T(1,128)S(1)}, s32[1,256]{1,0:T(1,128)}, u32[]{:S(2)}) copy-start(s32[1,256]{1,0:T(1,128)} %ses_ref.1) | copy-start | bytes 3076
  57.3 6.0 %collective-permute-start = (f32[1032,128]{1,0:T(8,128)S(1)}, f32[1032,128]{1,0:T(8,128)S(1)}, u32[]{:S(2)}, u32[]{:S(2)}) collective-permute-start(f32[1032,128]{1,0:T(8,128)S(1)} %get-tuple-element.26), channel_id=1, source_target_pairs={{0,1},{1,0},{2,3},{3,2},{4,5},{5,4},{6,7},{7,6},{8,9},{9,8},{10,11... | collective-permute-start | bytes 1585160 | tf_op jit(solution)/shard_map/ppermute | solution.py:382
  122.6 12.1 %collective-permute-start.2 = (f32[16,72,128]{2,1,0:T(8,128)S(1)}, f32[16,72,128]{2,1,0:T(8,128)S(1)}, u32[]{:S(2)}, u32[]{:S(2)}) collective-permute-start(f32[16,72,128]{2,1,0:T(8,128)S(1)} %all_to_all.35.own_ref), channel_id=1, source_target_pairs={{0,1},{1,0},{2,3},{3,2},{4,5},{5,4},{6,7},{7,6},{8,9},{9,8},{10,11... | collective-permute-start | bytes 1769480 | tf_op jit(solution)/shard_map/ppermute | solution.py:412
  126.9 2.4 %collective-permute-start.1 = (bf16[130,16,128]{2,1,0:T(8,128)(2,1)S(1)}, bf16[130,16,128]{2,1,0:T(8,128)(2,1)S(1)}, u32[]{:S(2)}, u32[]{:S(2)}) collective-permute-start(bf16[130,16,128]{2,1,0:T(8,128)(2,1)S(1)} %get-tuple-element.29.own_ref), channel_id=1, source_target_pairs={{0,1},{1,0},{2,3},{3,2},{4,5},{5,4},{6,7},{7,6},{8,9},{9,8},{10,11... | collective-permute-start | bytes 1597448 | tf_op jit(solution)/shard_map/ppermute | solution.py:397

commit v5 on v4

--- a/solution.py
+++ b/solution.py
@@ -98,13 +98,14 @@
 
 def serve_kernel(req_ref, far_ref, out_ref, wide_ref, tab_ref, sems):
     copies = [pltpu.make_async_copy(far_ref.at[t], tab_ref.at[t], sems.at[t]) for t in range(TABLES)]
-    for copy in copies:
-        copy.start()
+    copies[0].start()
     req = req_ref[...]
     part = ROWS // FOLD
     for t in range(TABLES):
         rows = [req[:, CAP * t + r : CAP * t + r + 1] for r in range(CAP)]
         hot = jnp.concatenate([hot_rows(row & 127, (row >> 7) & 7, 8) for row in rows], axis=0)
+        if t + 1 < TABLES:
+            copies[t + 1].start()
         copies[t].wait()
         table = jnp.concatenate(
             [tab_ref[t, f * part : (f + 1) * part, :] for f in range(FOLD)], axis=1
@@ -169,6 +170,7 @@
         columns = slice(EMB * q, EMB * (q + 1))
         keep_ref[256 * q : 256 * (q + 1)] = dense_ref[pl.ds(start, 256), columns]
         send_ref[256 * q : 256 * (q + 1)] = dense_ref[pl.ds(256 - start, 256), columns]
+
     def rows_of(line, last):
         parts = [line[:, EMB * q : EMB * (q + 1)] for q in range(4)]
         return jnp.concatenate(parts + [last] + [jnp.zeros((3, EMB), F32)], axis=0)
@@ -205,38 +207,64 @@
     for x in range(4):
         for z in range(8):
             for y in range(4):
-                k = 256 * (z % 4) + 8 * (2 * (4 * x + y) + z // 4)
-                tile = keep_ref[k : k + 8] + came_ref[k : k + 8]
-                high = tile.astype(BF).astype(F32)
+                k = 256 * (z % 4) + 16 * (4 * x + y) + 4 * (z // 4)
+                half = keep_ref[k : k + 4] + came_ref[k : k + 4]
+                high = half.astype(BF).astype(F32)
                 out_ref[(x * 8 + z) * 4 + y, LINES:] = jnp.concatenate(
-                    [high, tile - high], axis=0
+                    [high, half - high], axis=0
                 ).astype(BF)
     small_ref[...] = keep_ref[1024:] + came_ref[1024:]
 
 
-def open_kernel(got_ref, small_ref, id_ref, line_ref, chunk_ref):
+def chip_kernel(at_ref, keep_ref, came_ref, own_ref, one_ref, two_ref, three_ref, sum_ref):
+    for y in range(4):
+        for x in range(4):
+            for q in range(4):
+                k, to = 256 * q + 16 * (4 * x + y) + 8, 8 * ((y * 4 + x) * 4 + q)
+                sum_ref[to : to + 8] = keep_ref[k : k + 8] + came_ref[k : k + 8]
+    for d, ref in enumerate((own_ref, one_ref, two_ref, three_ref)):
+        ref[...] = sum_ref[pl.ds(pl.multiple_of(((at_ref[0] + d) & 3) * 128, 128), 128), :]
+
+
+def cross_kernel(
+    at_ref, mine_ref, a_ref, b_ref, c_ref, own_ref, one_ref, two_ref, three_ref, sum_ref
+):
+    sum_ref[...] = (mine_ref[...] + a_ref[...]) + (b_ref[...] + c_ref[...])
+    for d, ref in enumerate((own_ref, one_ref, two_ref, three_ref)):
+        ref[...] = sum_ref[pl.ds(pl.multiple_of(((at_ref[0] + d) & 3) * 32, 32), 32), :]
+
+
+def plane_kernel(mine_ref, a_ref, b_ref, c_ref, out_ref):
+    out_ref[...] = (mine_ref[...] + a_ref[...]) + (b_ref[...] + c_ref[...])
+
+
+def open_kernel(got_ref, small_ref, plane_ref, id_ref, line_ref, chunk_ref):
     line_ref[:OWNERS] = got_ref[:, :LINES]
     ids = jnp.transpose(id_ref[...])
     line_ref[OWNERS] = (ids >> 6).astype(F32).astype(BF)
     line_ref[OWNERS + 1] = (ids & 63).astype(F32).astype(BF)
-    sums = [jnp.zeros((16, EMB), F32) for _ in range(4)]
+    sums = [jnp.zeros((8, EMB), F32) for _ in range(4)]
     for k in range(OWNERS):
         sums[k % 4] = sums[k % 4] + got_ref[k, LINES:].astype(F32)
     total = (sums[0] + sums[1]) + (sums[2] + sums[3])
-    tile = total[:8] + total[8:]
+    half = total[:4] + total[4:]
+    last = jnp.concatenate([half, jnp.zeros((4, EMB), F32)], axis=0)
     for k in range(8):
-        chunk_ref[k, :8] = tile
-        chunk_ref[k, 8:] = small_ref[...]
+        chunk_ref[k, :32] = plane_ref[...]
+        chunk_ref[k, 32:40] = small_ref[...]
+        chunk_ref[k, 40:] = last
 
 
 def column_kernel(got_ref, out_ref):
-    small = got_ref[0, 8:]
+    total = got_ref[0, :40]
     for z in range(1, 8):
-        small = small + got_ref[z, 8:]
+        total = total + got_ref[z, :40]
+    tiles = [
+        jnp.concatenate([got_ref[q, 40:44], got_ref[q + 4, 40:44]], axis=0) for q in range(4)
+    ]
+    column = jnp.concatenate(tiles + [total], axis=0)
     for p in range(16):
-        for z in range(8):
-            out_ref[p, 8 * z : 8 * (z + 1)] = got_ref[z, :8]
-        out_ref[p, 64:] = small
+        out_ref[p] = column
 
 
 def place_kernel(
@@ -385,15 +413,34 @@
     )(pre_grad, slots, slot_cols, w_hidden)
     message, small = call(
         pack_kernel, 12,
-        (sds((OWNERS, 2 * LINES, EMB), BF), sds((SMALL, EMB), F32)),
+        (sds((OWNERS, LINES + 8, EMB), BF), sds((SMALL, EMB), F32)),
         [VMEM] * 3,
     )(lines, keep, came)
     got = exchange(message, TABLE)
+
+    def spread(parts, axis):
+        return [
+            lax.ppermute(part, axis, [(i, (i + d) % 4) for i in range(4)])
+            for d, part in enumerate(parts, 1)
+        ]
+
+    quarter, tiles = sds((128, EMB), F32), sds((32, EMB), F32)
+    own, *rest = call(
+        chip_kernel, 8, (quarter,) * 4, [SMEM] + [VMEM] * 2,
+        [pltpu.VMEM((512, EMB), F32)],
+    )(lax.axis_index("y").astype(i32).reshape(1), keep, came)
+    rest = spread(rest, "y")
+    own, *rest = call(
+        cross_kernel, 8, (tiles,) * 4, [SMEM] + [VMEM] * 4,
+        [pltpu.VMEM((128, EMB), F32)],
+    )(lax.axis_index("x").astype(i32).reshape(1), own, *rest)
+    rest = spread(rest, "x")
+    (plane,) = call(plane_kernel, 8, (tiles,), [VMEM] * 4)(own, *rest)
     incoming, chunks = call(
         open_kernel, 12,
-        (sds((OWNERS + 2, LINES, EMB), BF), sds((8, 8 + SMALL, EMB), F32)),
-        [VMEM] * 3,
-    )(got, small, requested)
+        (sds((OWNERS + 2, LINES, EMB), BF), sds((8, 48, EMB), F32)),
+        [VMEM] * 4,
+    )(got, small, plane, requested)
     other = lax.ppermute(incoming, "dp", swap)
     column = exchange(chunks, "z")
     (emb_step,) = call(
@@ -407,8 +454,8 @@
         ],
         out_specs=(ANY,),
     )(core, incoming, other)
-    (plane,) = call(column_kernel, 12, (sds((16, 64 + SMALL, EMB), F32),), [VMEM])(column)
-    mine = exchange(plane, ("x", "y"))
+    (sums,) = call(column_kernel, 12, (sds((16, 64 + SMALL, EMB), F32),), [VMEM])(column)
+    mine = exchange(sums, ("x", "y"))
     theirs = lax.ppermute(mine, "dp", swap)
     tile = sds((8, EMB), F32)
     own_main, own_small = call(square_kernel, 8, (tile, tile), [VMEM])(mine)

time: 136 us -> 133 us (0.978)
  blocking collectives: 107 us -> 74.1 us
  starting transfers between devices: 8.75 us -> 24.6 us
  waiting for transfers between devices: 2.9 us -> 16 us
    all_to_all x5 -> x4, blocking collectives: 107 us -> 74.1 us  [exchange(): return lax.all_to_all(array, axes, split_axis=0, concat_axis=0, tiled=True)]
    ppermute x0 -> x6, starting transfers between devices: none -> 8.96 us  [spread(): lax.ppermute(part, axis, [(i, (i + d) % 4) for i in range(4)])]
    ppermute x0 -> x6, waiting for transfers between devices: none -> 6.97 us  [spread(): lax.ppermute(part, axis, [(i, (i + d) % 4) for i in range(4)])]
    all_to_all x0 -> x1, starting transfers between devices: none -> 6.64 us  [exchange(): return lax.all_to_all(array, axes, split_axis=0, concat_axis=0, tiled=True)]
    all_to_all x0 -> x1, waiting for transfers between devices: none -> 6.11 us  [exchange(): return lax.all_to_all(array, axes, split_axis=0, concat_axis=0, tiled=True)]
  transfers between devices with their start and end apart: 3 -> 10, of which waited for: 2 -> 8; matrix products, arithmetic and copies ran while one was open for 0% -> 0% of each run, Pallas kernels for 5% -> 5%
where the time goes in v5:
time: 133 us
  blocking collectives  74.1 us (56%)
  starting transfers between devices  24.6 us (18%)
  Pallas kernels  17.4 us (13%)
  waiting for transfers between devices  16 us (12%)
    all_to_all x4, blocking collectives, exchange(): return lax.all_to_all(array, axes, split_axis=0, concat_axis=0, tiled=True)  74.1 us
    ppermute x6, starting transfers between devices, spread(): lax.ppermute(part, axis, [(i, (i + d) % 4) for i in range(4)])  8.96 us
    ppermute x6, waiting for transfers between devices, spread(): lax.ppermute(part, axis, [(i, (i + d) % 4) for i in range(4)])  6.97 us
    all_to_all x1, starting transfers between devices, exchange(): return lax.all_to_all(array, axes, split_axis=0, concat_axis=0, tiled=True)  6.64 us
    all_to_all x1, waiting for transfers between devices, exchange(): return lax.all_to_all(array, axes, split_axis=0, concat_axis=0, tiled=True)  6.11 us
    pallas_call x1, Pallas kernels, whole_step(): call(place_kernel, 28, (sds((TABLES, ROWS // 2, EMB), F32),), [SMEM] + [V...  5.35 us
    ppermute x1, starting transfers between devices, whole_step(): theirs = lax.ppermute(mine, 'dp', swap)  4.51 us
    ppermute x1, starting transfers between devices, whole_step(): came = lax.ppermute(send, 'dp', swap)  4.48 us
  transfers between devices with their start and end apart: 10, of which 8 were waited for; matrix products, arithmetic and copies ran while one was open for 0% of the time, Pallas kernels for 5%

profile of v5, /device:TPU:1, one launch (start us, length us, event | category | flops | bytes accessed | tf_op | source)
XLA Modules:
  0.0 133.0 jit_solution(5397657170708838353)
XLA Ops:
  0.6 0.0 copy-start
  0.6 0.0 copy-start.2
  0.7 0.0 copy-start.1
  0.7 0.0 copy-start.5
  0.7 0.0 copy-start.4
  0.7 0.0 copy-start.3
  0.7 1.9 %shard_map.128 = (s32[128,16]{1,0:T(8,128)S(1)}, s32[4,256]{1,0:T(4,128)S(1)}, s32[256,8]{1,0:T(8,128)S(1)}) custom-call(s32[1]{0:T(128)} %bitcast.core_ref, s32[8,128]{1,0:T(8,128)} %bitcast.20, s32[4,256]{1,0:T(4,128)} %bitcast.21), custom_call_target="tpu_custom_call" | custom-call | flops 268435456 | bytes 1048576 | tf_op jit(solution)/shard_map/pallas_call | solution.py:378
  2.6 26.7 %all_to_all.31 = s32[128,1,16]{2,1,0:T(1,128)S(1)} all-to-all(s32[128,1,16]{2,1,0:T(1,128)S(1)} %bitcast.17), channel_id=1, replica_groups=mesh['x'=4,'z'=8,'y'=4,'dp'=2] {'x','z','y'}, dimensions={0} | all-to-all | bytes 16384 | tf_op jit(solution)/shard_map/all_to_all | solution.py:369
  29.3 4.5 %shard_map.129 = bf16[128,16,128]{2,1,0:T(8,128)(2,1)S(1)} custom-call(s32[128,16]{1,0:T(8,128)S(1)} %bitcast.15, bf16[4,4096,128]{2,1,0:T(8,128)(2,1)} %far_ref.1), custom_call_target="tpu_custom_call" | custom-call | flops 268435456 | bytes 1048576 | tf_op jit(solution)/shard_map/pallas_call | solution.py:389
  33.8 21.5 %all_to_all.32.ret_ref = bf16[128,16,128]{2,1,0:T(8,128)(2,1)S(1)} all-to-all(bf16[128,16,128]{2,1,0:T(8,128)(2,1)S(1)} %shard_map.129), channel_id=1, replica_groups=mesh['x'=4,'z'=8,'y'=4,'dp'=2] {'x','z','y'}, dimensions={0} | all-to-all | bytes 1048576 | tf_op jit(solution)/shard_map/all_to_all | solution.py:369
  55.2 0.0 copy-done
  55.2 0.0 copy-done.2
  55.2 0.0 copy-done.1
  55.2 0.0 copy-done.5
  55.2 0.0 copy-done.4
  55.3 0.0 copy-done.3
  55.3 2.2 %shard_map.130 = (bf16[256,512]{1,0:T(8,128)(2,1)S(1)}, f32[1032,128]{1,0:T(8,128)S(1)}, f32[1032,128]{1,0:T(8,128)S(1)}) custom-call(s32[1]{0:T(128)} %bitcast.core_ref, bf16[128,16,128]{2,1,0:T(8,128)(2,1)S(1)} %all_to_all.32.ret_ref, s32[256,8]{1,0:T(8,128)S(1)} %get-tuple-element.30.slot_col_ref, s32[1,256]{1,0:T(1,128)S(1)} %copy-done.3, ...), custom_call_target="tpu_custom_call" | custom-call | flops 268435456 | bytes 1048576 | tf_op jit(solution)/shard_map/pallas_call | solution.py:401
  57.5 4.5 %collective-permute-start = (f32[1032,128]{1,0:T(8,128)S(1)}, f32[1032,128]{1,0:T(8,128)S(1)}, u32[]{:S(2)}, u32[]{:S(2)}) collective-permute-start(f32[1032,128]{1,0:T(8,128)S(1)} %get-tuple-element.34), channel_id=1, source_target_pairs={{0,1},{1,0},{2,3},{3,2},{4,5},{5,4},{6,7},{7,6},{8,9},{9,8},{10,11... | collective-permute-start | bytes 1585160 | tf_op jit(solution)/shard_map/ppermute | solution.py:410
  61.9 1.0 shard_map.131.line_ref
  63.0 0.5 collective-permute-done.came_ref
  63.5 1.0 shard_map.132
  64.5 6.6 %all-to-all-start.2 = ((bf16[128,24,128]{2,1,0:T(8,128)(2,1)}), bf16[128,24,128]{2,1,0:T(8,128)(2,1)S(1)}, u32[]{:S(2)}, u32[]{:S(2)}) async-start(bf16[128,24,128]{2,1,0:T(8,128)(2,1)} %get-tuple-element.35), calls=%async_computation.2 | async-start | bytes 1572864 | tf_op jit(solution)/shard_map/all_to_all | solution.py:369
  71.2 0.1 shard_map.133
  71.2 0.7 collective-permute-start.1
  71.9 2.4 %collective-permute-start.2 = (f32[128,128]{1,0:T(8,128)S(1)}, f32[128,128]{1,0:T(8,128)S(1)}, u32[]{:S(2)}, u32[]{:S(2)}) collective-permute-start(f32[128,128]{1,0:T(8,128)S(1)} %get-tuple-element.39), channel_id=1, source_target_pairs={{0,4},{2,6},{4,0},{6,2},{1,5},{3,7},{5,1},{7,3},{8,12},{10,14},{12... | collective-permute-start | bytes 196616 | tf_op jit(solution)/shard_map/ppermute | solution.py:423
  74.3 1.2 collective-permute-start.3
  75.5 0.7 collective-permute-done.1.a_ref
  76.2 2.6 %collective-permute-done.2.b_ref = f32[128,128]{1,0:T(8,128)S(1)} collective-permute-done((f32[128,128]{1,0:T(8,128)S(1)}, f32[128,128]{1,0:T(8,128)S(1)}, u32[]{:S(2)}, u32[]{:S(2)}) %collective-permute-start.2) | collective-permute-done | bytes 65568 | tf_op jit(solution)/shard_map/ppermute | solution.py:423
  78.9 1.0 collective-permute-done.3.c_ref
  79.9 1.1 collective-permute-start.4
  81.0 3.0 %collective-permute-start.5 = (f32[32,128]{1,0:T(8,128)S(1)}, f32[32,128]{1,0:T(8,128)S(1)}, u32[]{:S(2)}, u32[]{:S(2)}) collective-permute-start(f32[32,128]{1,0:T(8,128)S(1)} %get-tuple-element.43), channel_id=1, source_target_pairs={{0,128},{64,192},{128,0},{192,64},{1,129},{65,193},{129,1},{193,65... | collective-permute-start | bytes 49160 | tf_op jit(solution)/shard_map/ppermute | solution.py:423
  83.9 0.6 collective-permute-start.6
  84.6 0.0 collective-permute-done.4.a_ref
  84.6 1.4 %collective-permute-done.5.b_ref = f32[32,128]{1,0:T(8,128)S(1)} collective-permute-done((f32[32,128]{1,0:T(8,128)S(1)}, f32[32,128]{1,0:T(8,128)S(1)}, u32[]{:S(2)}, u32[]{:S(2)}) %collective-permute-start.5) | collective-permute-done | bytes 16416 | tf_op jit(solution)/shard_map/ppermute | solution.py:423
  86.0 1.2 collective-permute-done.6.c_ref
  87.2 6.1 %all-to-all-done.2.got_ref = bf16[128,24,128]{2,1,0:T(8,128)(2,1)S(1)} async-done(((bf16[128,24,128]{2,1,0:T(8,128)(2,1)}), bf16[128,24,128]{2,1,0:T(8,128)(2,1)S(1)}, u32[]{:S(2)}, u32[]{:S(2)}) %all-to-all-start.2) | async-done | bytes 786464 | tf_op jit(solution)/shard_map/all_to_all | solution.py:369
  93.3 0.1 shard_map.136
  93.4 13.9 %all_to_all.33.got_ref = f32[8,48,128]{2,1,0:T(8,128)S(1)} all-to-all(f32[8,48,128]{2,1,0:T(8,128)S(1)} %get-tuple-element.46), channel_id=1, replica_groups=mesh['x'=4,'z'=8,'y'=4,'dp'=2] {'z'}, dimensions={0} | all-to-all | bytes 393216 | tf_op jit(solution)/shard_map/all_to_all | solution.py:369
  107.3 12.1 %all_to_all.34.own_ref = f32[16,72,128]{2,1,0:T(8,128)S(1)} all-to-all(f32[16,72,128]{2,1,0:T(8,128)S(1)} %shard_map.138), channel_id=1, replica_groups=mesh['x'=4,'z'=8,'y'=4,'dp'=2] {'x','y'}, dimensions={0} | all-to-all | bytes 1179648 | tf_op jit(solution)/shard_map/all_to_all | solution.py:369
  119.4 4.5 %collective-permute-start.8 = (f32[16,72,128]{2,1,0:T(8,128)S(1)}, f32[16,72,128]{2,1,0:T(8,128)S(1)}, u32[]{:S(2)}, u32[]{:S(2)}) collective-permute-start(f32[16,72,128]{2,1,0:T(8,128)S(1)} %all_to_all.34.own_ref), channel_id=1, source_target_pairs={{0,1},{1,0},{2,3},{3,2},{4,5},{5,4},{6,7},{7,6},{8,9},{9,8},{10,11... | collective-permute-start | bytes 1769480 | tf_op jit(solution)/shard_map/ppermute | solution.py:459
  123.9 0.0 collective-permute-start.7
  123.9 2.4 %collective-permute-done.7.other_ref = bf16[130,16,128]{2,1,0:T(8,128)(2,1)S(1)} collective-permute-done((bf16[130,16,128]{2,1,0:T(8,128)(2,1)S(1)}, bf16[130,16,128]{2,1,0:T(8,128)(2,1)S(1)}, u32[]{:S(2)}, u32[]{:S(2)}) %collective-permute-start.7) | collective-permute-done | bytes 532512 | tf_op jit(solution)/shard_map/ppermute | solution.py:444
  126.3 5.3 %shard_map.137 = f32[4,2048,128]{2,1,0:T(8,128)} custom-call(s32[1]{0:T(128)} %bitcast.core_ref, bf16[130,16,128]{2,1,0:T(8,128)(2,1)S(1)} %get-tuple-element.45.own_ref, bf16[130,16,128]{2,1,0:T(8,128)(2,1)S(1)} %collective-permute-done.7.other_ref), custom_call_target="tpu_custom_call" | custom-call | flops 268435456 | bytes 1048576 | tf_op jit(solution)/shard_map/pallas_call | solution.py:446
  131.7 0.1 shard_map.139
  131.7 0.0 collective-permute-done.8.other_ref
  131.7 1.3 shard_map.140
  (3 shorter events, 0.1 us)
Async XLA Ops:
  0.6 54.6 %copy-start = (f32[512,512]{1,0:T(8,128)S(1)}, f32[512,512]{1,0:T(8,128)}, u32[]{:S(2)}) copy-start(f32[512,512]{1,0:T(8,128)} %w_ref.3) | copy-start | bytes 3145732
  0.6 54.6 %copy-start.2 = (f32[512]{0:T(512)S(1)}, f32[512]{0:T(512)}, u32[]{:S(2)}) copy-start(f32[512]{0:T(512)} %param.17) | copy-start | bytes 6148
  0.7 54.6 %copy-start.1 = (f32[512]{0:T(512)S(1)}, f32[512]{0:T(512)}, u32[]{:S(2)}) copy-start(f32[512]{0:T(512)} %param.16) | copy-start | bytes 6148
  0.7 54.6 %copy-start.5 = (f32[1,256]{1,0:T(1,128)S(1)}, f32[1,256]{1,0:T(1,128)}, u32[]{:S(2)}) copy-start(f32[1,256]{1,0:T(1,128)} %lb_ref.1) | copy-start | bytes 3076
  0.7 54.6 %copy-start.4 = (f32[1,256]{1,0:T(1,128)S(1)}, f32[1,256]{1,0:T(1,128)}, u32[]{:S(2)}) copy-start(f32[1,256]{1,0:T(1,128)} %rel_ref.1) | copy-start | bytes 3076
  0.7 54.6 %copy-start.3 = (s32[1,256]{1,0:T(1,128)S(1)}, s32[1,256]{1,0:T(1,128)}, u32[]{:S(2)}) copy-start(s32[1,256]{1,0:T(1,128)} %ses_ref.1) | copy-start | bytes 3076
  57.5 6.0 %collective-permute-start = (f32[1032,128]{1,0:T(8,128)S(1)}, f32[1032,128]{1,0:T(8,128)S(1)}, u32[]{:S(2)}, u32[]{:S(2)}) collective-permute-start(f32[1032,128]{1,0:T(8,128)S(1)} %get-tuple-element.34), channel_id=1, source_target_pairs={{0,1},{1,0},{2,3},{3,2},{4,5},{5,4},{6,7},{7,6},{8,9},{9,8},{10,11... | collective-permute-start | bytes 1585160 | tf_op jit(solution)/shard_map/ppermute | solution.py:410
  64.5 28.8 %all-to-all-start.2 = ((bf16[128,24,128]{2,1,0:T(8,128)(2,1)}), bf16[128,24,128]{2,1,0:T(8,128)(2,1)S(1)}, u32[]{:S(2)}, u32[]{:S(2)}) async-start(bf16[128,24,128]{2,1,0:T(8,128)(2,1)} %get-tuple-element.35), calls=%async_computation.2 | async-start | bytes 1572864 | tf_op jit(solution)/shard_map/all_to_all | solution.py:369
  71.2 5.0 %collective-permute-start.1 = (f32[128,128]{1,0:T(8,128)S(1)}, f32[128,128]{1,0:T(8,128)S(1)}, u32[]{:S(2)}, u32[]{:S(2)}) collective-permute-start(f32[128,128]{1,0:T(8,128)S(1)} %get-tuple-element.38), channel_id=1, source_target_pairs={{0,2},{2,4},{4,6},{6,0},{1,3},{3,5},{5,7},{7,1},{8,10},{10,12},{12... | collective-permute-start | bytes 196616 | tf_op jit(solution)/shard_map/ppermute | solution.py:423
  71.9 7.0 %collective-permute-start.2 = (f32[128,128]{1,0:T(8,128)S(1)}, f32[128,128]{1,0:T(8,128)S(1)}, u32[]{:S(2)}, u32[]{:S(2)}) collective-permute-start(f32[128,128]{1,0:T(8,128)S(1)} %get-tuple-element.39), channel_id=1, source_target_pairs={{0,4},{2,6},{4,0},{6,2},{1,5},{3,7},{5,1},{7,3},{8,12},{10,14},{12... | collective-permute-start | bytes 196616 | tf_op jit(solution)/shard_map/ppermute | solution.py:423
  74.3 5.5 %collective-permute-start.3 = (f32[128,128]{1,0:T(8,128)S(1)}, f32[128,128]{1,0:T(8,128)S(1)}, u32[]{:S(2)}, u32[]{:S(2)}) collective-permute-start(f32[128,128]{1,0:T(8,128)S(1)} %get-tuple-element.40), channel_id=1, source_target_pairs={{0,6},{2,0},{4,2},{6,4},{1,7},{3,1},{5,3},{7,5},{8,14},{10,8},{12,... | collective-permute-start | bytes 196616 | tf_op jit(solution)/shard_map/ppermute | solution.py:423
  79.9 4.7 %collective-permute-start.4 = (f32[32,128]{1,0:T(8,128)S(1)}, f32[32,128]{1,0:T(8,128)S(1)}, u32[]{:S(2)}, u32[]{:S(2)}) collective-permute-start(f32[32,128]{1,0:T(8,128)S(1)} %get-tuple-element.42), channel_id=1, source_target_pairs={{0,64},{64,128},{128,192},{192,0},{1,65},{65,129},{129,193},{193,1... | collective-permute-start | bytes 49160 | tf_op jit(solution)/shard_map/ppermute | solution.py:423
  81.0 5.0 %collective-permute-start.5 = (f32[32,128]{1,0:T(8,128)S(1)}, f32[32,128]{1,0:T(8,128)S(1)}, u32[]{:S(2)}, u32[]{:S(2)}) collective-permute-start(f32[32,128]{1,0:T(8,128)S(1)} %get-tuple-element.43), channel_id=1, source_target_pairs={{0,128},{64,192},{128,0},{192,64},{1,129},{65,193},{129,1},{193,65... | collective-permute-start | bytes 49160 | tf_op jit(solution)/shard_map/ppermute | solution.py:423
  83.9 3.3 %collective-permute-start.6 = (f32[32,128]{1,0:T(8,128)S(1)}, f32[32,128]{1,0:T(8,128)S(1)}, u32[]{:S(2)}, u32[]{:S(2)}) collective-permute-start(f32[32,128]{1,0:T(8,128)S(1)} %get-tuple-element.44), channel_id=1, source_target_pairs={{0,192},{64,0},{128,64},{192,128},{1,193},{65,1},{129,65},{193,129... | collective-permute-start | bytes 49160 | tf_op jit(solution)/shard_map/ppermute | solution.py:423
  119.4 12.3 %collective-permute-start.8 = (f32[16,72,128]{2,1,0:T(8,128)S(1)}, f32[16,72,128]{2,1,0:T(8,128)S(1)}, u32[]{:S(2)}, u32[]{:S(2)}) collective-permute-start(f32[16,72,128]{2,1,0:T(8,128)S(1)} %all_to_all.34.own_ref), channel_id=1, source_target_pairs={{0,1},{1,0},{2,3},{3,2},{4,5},{5,4},{6,7},{7,6},{8,9},{9,8},{10,11... | collective-permute-start | bytes 1769480 | tf_op jit(solution)/shard_map/ppermute | solution.py:459
  123.9 2.4 %collective-permute-start.7 = (bf16[130,16,128]{2,1,0:T(8,128)(2,1)S(1)}, bf16[130,16,128]{2,1,0:T(8,128)(2,1)S(1)}, u32[]{:S(2)}, u32[]{:S(2)}) collective-permute-start(bf16[130,16,128]{2,1,0:T(8,128)(2,1)S(1)} %get-tuple-element.45.own_ref), channel_id=1, source_target_pairs={{0,1},{1,0},{2,3},{3,2},{4,5},{5,4},{6,7},{7,6},{8,9},{9,8},{10,11... | collective-permute-start | bytes 1597448 | tf_op jit(solution)/shard_map/ppermute | solution.py:444

commit v6 on v5

--- a/solution.py
+++ b/solution.py
@@ -98,14 +98,13 @@
 
 def serve_kernel(req_ref, far_ref, out_ref, wide_ref, tab_ref, sems):
     copies = [pltpu.make_async_copy(far_ref.at[t], tab_ref.at[t], sems.at[t]) for t in range(TABLES)]
-    copies[0].start()
+    for copy in copies:
+        copy.start()
     req = req_ref[...]
     part = ROWS // FOLD
     for t in range(TABLES):
         rows = [req[:, CAP * t + r : CAP * t + r + 1] for r in range(CAP)]
         hot = jnp.concatenate([hot_rows(row & 127, (row >> 7) & 7, 8) for row in rows], axis=0)
-        if t + 1 < TABLES:
-            copies[t + 1].start()
         copies[t].wait()
         table = jnp.concatenate(
             [tab_ref[t, f * part : (f + 1) * part, :] for f in range(FOLD)], axis=1
@@ -238,11 +237,14 @@
     out_ref[...] = (mine_ref[...] + a_ref[...]) + (b_ref[...] + c_ref[...])
 
 
-def open_kernel(got_ref, small_ref, plane_ref, id_ref, line_ref, chunk_ref):
+def lines_kernel(got_ref, id_ref, line_ref):
     line_ref[:OWNERS] = got_ref[:, :LINES]
     ids = jnp.transpose(id_ref[...])
     line_ref[OWNERS] = (ids >> 6).astype(F32).astype(BF)
     line_ref[OWNERS + 1] = (ids & 63).astype(F32).astype(BF)
+
+
+def open_kernel(got_ref, small_ref, plane_ref, chunk_ref):
     sums = [jnp.zeros((8, EMB), F32) for _ in range(4)]
     for k in range(OWNERS):
         sums[k % 4] = sums[k % 4] + got_ref[k, LINES:].astype(F32)
@@ -436,11 +438,10 @@
     )(lax.axis_index("x").astype(i32).reshape(1), own, *rest)
     rest = spread(rest, "x")
     (plane,) = call(plane_kernel, 8, (tiles,), [VMEM] * 4)(own, *rest)
-    incoming, chunks = call(
-        open_kernel, 12,
-        (sds((OWNERS + 2, LINES, EMB), BF), sds((8, 48, EMB), F32)),
-        [VMEM] * 4,
-    )(got, small, plane, requested)
+    (chunks,) = call(open_kernel, 12, (sds((8, 48, EMB), F32),), [VMEM] * 3)(got, small, plane)
+    (incoming,) = call(
+        lines_kernel, 12, (sds((OWNERS + 2, LINES, EMB), BF),), [VMEM] * 2
+    )(got, requested)
     other = lax.ppermute(incoming, "dp", swap)
     column = exchange(chunks, "z")
     (emb_step,) = call(

time: 133 us -> 133 us (level)
  no operation moved by 1% of the time
where the time goes in v6:
time: 133 us
  blocking collectives  74.2 us (56%)
  starting transfers between devices  24.6 us (18%)
  Pallas kernels  17.4 us (13%)
  waiting for transfers between devices  15.8 us (12%)
    all_to_all x4, blocking collectives, exchange(): return lax.all_to_all(array, axes, split_axis=0, concat_axis=0, tiled=True)  74.2 us
    ppermute x6, starting transfers between devices, spread(): lax.ppermute(part, axis, [(i, (i + d) % 4) for i in range(4)])  8.96 us
    ppermute x6, waiting for transfers between devices, spread(): lax.ppermute(part, axis, [(i, (i + d) % 4) for i in range(4)])  6.97 us
    all_to_all x1, starting transfers between devices, exchange(): return lax.all_to_all(array, axes, split_axis=0, concat_axis=0, tiled=True)  6.64 us
    all_to_all x1, waiting for transfers between devices, exchange(): return lax.all_to_all(array, axes, split_axis=0, concat_axis=0, tiled=True)  6.11 us
    pallas_call x1, Pallas kernels, whole_step(): call(place_kernel, 28, (sds((TABLES, ROWS // 2, EMB), F32),), [SMEM] + [V...  5.35 us
    ppermute x1, starting transfers between devices, whole_step(): theirs = lax.ppermute(mine, 'dp', swap)  4.51 us
    ppermute x1, starting transfers between devices, whole_step(): came = lax.ppermute(send, 'dp', swap)  4.47 us
  transfers between devices with their start and end apart: 10, of which 8 were waited for; matrix products, arithmetic and copies ran while one was open for 0% of the time, Pallas kernels for 5%

profile of v6, /device:TPU:1, one launch (start us, length us, event | category | flops | bytes accessed | tf_op | source)
XLA Modules:
  0.0 132.8 jit_solution(9560851476805083636)
XLA Ops:
  0.6 0.0 copy-start
  0.6 0.0 copy-start.2
  0.7 0.0 copy-start.1
  0.7 0.0 copy-start.5
  0.7 0.0 copy-start.4
  0.7 0.0 copy-start.3
  0.7 1.9 %shard_map.128 = (s32[128,16]{1,0:T(8,128)S(1)}, s32[4,256]{1,0:T(4,128)S(1)}, s32[256,8]{1,0:T(8,128)S(1)}) custom-call(s32[1]{0:T(128)} %bitcast.core_ref, s32[8,128]{1,0:T(8,128)} %bitcast.20, s32[4,256]{1,0:T(4,128)} %bitcast.21), custom_call_target="tpu_custom_call" | custom-call | flops 268435456 | bytes 1048576 | tf_op jit(solution)/shard_map/pallas_call | solution.py:380
  2.6 26.7 %all_to_all.31 = s32[128,1,16]{2,1,0:T(1,128)S(1)} all-to-all(s32[128,1,16]{2,1,0:T(1,128)S(1)} %bitcast.17), channel_id=1, replica_groups=mesh['x'=4,'z'=8,'y'=4,'dp'=2] {'x','z','y'}, dimensions={0} | all-to-all | bytes 16384 | tf_op jit(solution)/shard_map/all_to_all | solution.py:371
  29.3 4.3 %shard_map.129 = bf16[128,16,128]{2,1,0:T(8,128)(2,1)S(1)} custom-call(s32[128,16]{1,0:T(8,128)S(1)} %bitcast.15, bf16[4,4096,128]{2,1,0:T(8,128)(2,1)} %far_ref.1), custom_call_target="tpu_custom_call" | custom-call | flops 268435456 | bytes 1048576 | tf_op jit(solution)/shard_map/pallas_call | solution.py:391
  33.6 21.5 %all_to_all.32.ret_ref = bf16[128,16,128]{2,1,0:T(8,128)(2,1)S(1)} all-to-all(bf16[128,16,128]{2,1,0:T(8,128)(2,1)S(1)} %shard_map.129), channel_id=1, replica_groups=mesh['x'=4,'z'=8,'y'=4,'dp'=2] {'x','z','y'}, dimensions={0} | all-to-all | bytes 1048576 | tf_op jit(solution)/shard_map/all_to_all | solution.py:371
  55.1 0.0 copy-done
  55.1 0.0 copy-done.2
  55.1 0.0 copy-done.1
  55.1 0.0 copy-done.5
  55.1 0.0 copy-done.4
  55.1 0.0 copy-done.3
  55.1 2.2 %shard_map.130 = (bf16[256,512]{1,0:T(8,128)(2,1)S(1)}, f32[1032,128]{1,0:T(8,128)S(1)}, f32[1032,128]{1,0:T(8,128)S(1)}) custom-call(s32[1]{0:T(128)} %bitcast.core_ref, bf16[128,16,128]{2,1,0:T(8,128)(2,1)S(1)} %all_to_all.32.ret_ref, s32[256,8]{1,0:T(8,128)S(1)} %get-tuple-element.28.slot_col_ref, s32[1,256]{1,0:T(1,128)S(1)} %copy-done.3, ...), custom_call_target="tpu_custom_call" | custom-call | flops 268435456 | bytes 1048576 | tf_op jit(solution)/shard_map/pallas_call | solution.py:403
  57.3 4.5 %collective-permute-start = (f32[1032,128]{1,0:T(8,128)S(1)}, f32[1032,128]{1,0:T(8,128)S(1)}, u32[]{:S(2)}, u32[]{:S(2)}) collective-permute-start(f32[1032,128]{1,0:T(8,128)S(1)} %get-tuple-element.32), channel_id=1, source_target_pairs={{0,1},{1,0},{2,3},{3,2},{4,5},{5,4},{6,7},{7,6},{8,9},{9,8},{10,11... | collective-permute-start | bytes 1585160 | tf_op jit(solution)/shard_map/ppermute | solution.py:412
  61.8 1.0 shard_map.131.line_ref
  62.8 0.5 collective-permute-done.came_ref
  63.4 1.0 shard_map.132
  64.4 6.6 %all-to-all-start.2 = ((bf16[128,24,128]{2,1,0:T(8,128)(2,1)}), bf16[128,24,128]{2,1,0:T(8,128)(2,1)S(1)}, u32[]{:S(2)}, u32[]{:S(2)}) async-start(bf16[128,24,128]{2,1,0:T(8,128)(2,1)} %get-tuple-element.33), calls=%async_computation.2 | async-start | bytes 1572864 | tf_op jit(solution)/shard_map/all_to_all | solution.py:371
  71.1 0.1 shard_map.135
  71.1 0.7 collective-permute-start.2
  71.8 2.4 %collective-permute-start.3 = (f32[128,128]{1,0:T(8,128)S(1)}, f32[128,128]{1,0:T(8,128)S(1)}, u32[]{:S(2)}, u32[]{:S(2)}) collective-permute-start(f32[128,128]{1,0:T(8,128)S(1)} %get-tuple-element.37), channel_id=1, source_target_pairs={{0,4},{2,6},{4,0},{6,2},{1,5},{3,7},{5,1},{7,3},{8,12},{10,14},{12... | collective-permute-start | bytes 196616 | tf_op jit(solution)/shard_map/ppermute | solution.py:425
  74.2 1.2 collective-permute-start.4
  75.3 0.7 collective-permute-done.2.a_ref
  76.1 2.6 %collective-permute-done.3.b_ref = f32[128,128]{1,0:T(8,128)S(1)} collective-permute-done((f32[128,128]{1,0:T(8,128)S(1)}, f32[128,128]{1,0:T(8,128)S(1)}, u32[]{:S(2)}, u32[]{:S(2)}) %collective-permute-start.3) | collective-permute-done | bytes 65568 | tf_op jit(solution)/shard_map/ppermute | solution.py:425
  78.7 1.0 collective-permute-done.4.c_ref
  79.7 1.1 collective-permute-start.5
  80.8 3.0 %collective-permute-start.6 = (f32[32,128]{1,0:T(8,128)S(1)}, f32[32,128]{1,0:T(8,128)S(1)}, u32[]{:S(2)}, u32[]{:S(2)}) collective-permute-start(f32[32,128]{1,0:T(8,128)S(1)} %get-tuple-element.41), channel_id=1, source_target_pairs={{0,128},{64,192},{128,0},{192,64},{1,129},{65,193},{129,1},{193,65... | collective-permute-start | bytes 49160 | tf_op jit(solution)/shard_map/ppermute | solution.py:425
  83.8 0.6 collective-permute-start.7
  84.5 0.0 collective-permute-done.5.a_ref
  84.5 1.4 %collective-permute-done.6.b_ref = f32[32,128]{1,0:T(8,128)S(1)} collective-permute-done((f32[32,128]{1,0:T(8,128)S(1)}, f32[32,128]{1,0:T(8,128)S(1)}, u32[]{:S(2)}, u32[]{:S(2)}) %collective-permute-start.6) | collective-permute-done | bytes 16416 | tf_op jit(solution)/shard_map/ppermute | solution.py:425
  85.8 1.2 collective-permute-done.7.c_ref
  87.1 6.1 %all-to-all-done.2.got_ref = bf16[128,24,128]{2,1,0:T(8,128)(2,1)S(1)} async-done(((bf16[128,24,128]{2,1,0:T(8,128)(2,1)}), bf16[128,24,128]{2,1,0:T(8,128)(2,1)S(1)}, u32[]{:S(2)}, u32[]{:S(2)}) %all-to-all-start.2) | async-done | bytes 786464 | tf_op jit(solution)/shard_map/all_to_all | solution.py:371
  93.2 13.9 %all_to_all.33.got_ref = f32[8,48,128]{2,1,0:T(8,128)S(1)} all-to-all(f32[8,48,128]{2,1,0:T(8,128)S(1)} %shard_map.138), channel_id=1, replica_groups=mesh['x'=4,'z'=8,'y'=4,'dp'=2] {'z'}, dimensions={0} | all-to-all | bytes 393216 | tf_op jit(solution)/shard_map/all_to_all | solution.py:371
  107.2 12.1 %all_to_all.34.own_ref = f32[16,72,128]{2,1,0:T(8,128)S(1)} all-to-all(f32[16,72,128]{2,1,0:T(8,128)S(1)} %shard_map.139), channel_id=1, replica_groups=mesh['x'=4,'z'=8,'y'=4,'dp'=2] {'x','y'}, dimensions={0} | all-to-all | bytes 1179648 | tf_op jit(solution)/shard_map/all_to_all | solution.py:371
  119.3 4.5 %collective-permute-start.8 = (f32[16,72,128]{2,1,0:T(8,128)S(1)}, f32[16,72,128]{2,1,0:T(8,128)S(1)}, u32[]{:S(2)}, u32[]{:S(2)}) collective-permute-start(f32[16,72,128]{2,1,0:T(8,128)S(1)} %all_to_all.34.own_ref), channel_id=1, source_target_pairs={{0,1},{1,0},{2,3},{3,2},{4,5},{5,4},{6,7},{7,6},{8,9},{9,8},{10,11... | collective-permute-start | bytes 1769480 | tf_op jit(solution)/shard_map/ppermute | solution.py:460
  123.8 0.1 shard_map.133.own_ref
  123.8 0.1 collective-permute-start.1
  123.9 2.2 %collective-permute-done.1.other_ref = bf16[130,16,128]{2,1,0:T(8,128)(2,1)S(1)} collective-permute-done((bf16[130,16,128]{2,1,0:T(8,128)(2,1)S(1)}, bf16[130,16,128]{2,1,0:T(8,128)(2,1)S(1)}, u32[]{:S(2)}, u32[]{:S(2)}) %collective-permute-start.1) | collective-permute-done | bytes 532512 | tf_op jit(solution)/shard_map/ppermute | solution.py:445
  126.2 5.3 %shard_map.134 = f32[4,2048,128]{2,1,0:T(8,128)} custom-call(s32[1]{0:T(128)} %bitcast.core_ref, bf16[130,16,128]{2,1,0:T(8,128)(2,1)S(1)} %shard_map.133.own_ref, bf16[130,16,128]{2,1,0:T(8,128)(2,1)S(1)} %collective-permute-done.1.other_ref), custom_call_target="tpu_custom_call" | custom-call | flops 268435456 | bytes 1048576 | tf_op jit(solution)/shard_map/pallas_call | solution.py:447
  131.5 0.1 shard_map.140
  131.6 0.0 collective-permute-done.8.other_ref
  131.6 1.3 shard_map.141
  (4 shorter events, 0.1 us)
Async XLA Ops:
  0.6 54.5 %copy-start = (f32[512,512]{1,0:T(8,128)S(1)}, f32[512,512]{1,0:T(8,128)}, u32[]{:S(2)}) copy-start(f32[512,512]{1,0:T(8,128)} %w_ref.3) | copy-start | bytes 3145732
  0.6 54.5 %copy-start.2 = (f32[512]{0:T(512)S(1)}, f32[512]{0:T(512)}, u32[]{:S(2)}) copy-start(f32[512]{0:T(512)} %param.17) | copy-start | bytes 6148
  0.7 54.5 %copy-start.1 = (f32[512]{0:T(512)S(1)}, f32[512]{0:T(512)}, u32[]{:S(2)}) copy-start(f32[512]{0:T(512)} %param.16) | copy-start | bytes 6148
  0.7 54.5 %copy-start.5 = (f32[1,256]{1,0:T(1,128)S(1)}, f32[1,256]{1,0:T(1,128)}, u32[]{:S(2)}) copy-start(f32[1,256]{1,0:T(1,128)} %lb_ref.1) | copy-start | bytes 3076
  0.7 54.5 %copy-start.4 = (f32[1,256]{1,0:T(1,128)S(1)}, f32[1,256]{1,0:T(1,128)}, u32[]{:S(2)}) copy-start(f32[1,256]{1,0:T(1,128)} %rel_ref.1) | copy-start | bytes 3076
  0.7 54.5 %copy-start.3 = (s32[1,256]{1,0:T(1,128)S(1)}, s32[1,256]{1,0:T(1,128)}, u32[]{:S(2)}) copy-start(s32[1,256]{1,0:T(1,128)} %ses_ref.1) | copy-start | bytes 3076
  57.3 6.0 %collective-permute-start = (f32[1032,128]{1,0:T(8,128)S(1)}, f32[1032,128]{1,0:T(8,128)S(1)}, u32[]{:S(2)}, u32[]{:S(2)}) collective-permute-start(f32[1032,128]{1,0:T(8,128)S(1)} %get-tuple-element.32), channel_id=1, source_target_pairs={{0,1},{1,0},{2,3},{3,2},{4,5},{5,4},{6,7},{7,6},{8,9},{9,8},{10,11... | collective-permute-start | bytes 1585160 | tf_op jit(solution)/shard_map/ppermute | solution.py:412
  64.4 28.8 %all-to-all-start.2 = ((bf16[128,24,128]{2,1,0:T(8,128)(2,1)}), bf16[128,24,128]{2,1,0:T(8,128)(2,1)S(1)}, u32[]{:S(2)}, u32[]{:S(2)}) async-start(bf16[128,24,128]{2,1,0:T(8,128)(2,1)} %get-tuple-element.33), calls=%async_computation.2 | async-start | bytes 1572864 | tf_op jit(solution)/shard_map/all_to_all | solution.py:371
  71.1 5.0 %collective-permute-start.2 = (f32[128,128]{1,0:T(8,128)S(1)}, f32[128,128]{1,0:T(8,128)S(1)}, u32[]{:S(2)}, u32[]{:S(2)}) collective-permute-start(f32[128,128]{1,0:T(8,128)S(1)} %get-tuple-element.36), channel_id=1, source_target_pairs={{0,2},{2,4},{4,6},{6,0},{1,3},{3,5},{5,7},{7,1},{8,10},{10,12},{12... | collective-permute-start | bytes 196616 | tf_op jit(solution)/shard_map/ppermute | solution.py:425
  71.8 7.0 %collective-permute-start.3 = (f32[128,128]{1,0:T(8,128)S(1)}, f32[128,128]{1,0:T(8,128)S(1)}, u32[]{:S(2)}, u32[]{:S(2)}) collective-permute-start(f32[128,128]{1,0:T(8,128)S(1)} %get-tuple-element.37), channel_id=1, source_target_pairs={{0,4},{2,6},{4,0},{6,2},{1,5},{3,7},{5,1},{7,3},{8,12},{10,14},{12... | collective-permute-start | bytes 196616 | tf_op jit(solution)/shard_map/ppermute | solution.py:425
  74.2 5.5 %collective-permute-start.4 = (f32[128,128]{1,0:T(8,128)S(1)}, f32[128,128]{1,0:T(8,128)S(1)}, u32[]{:S(2)}, u32[]{:S(2)}) collective-permute-start(f32[128,128]{1,0:T(8,128)S(1)} %get-tuple-element.38), channel_id=1, source_target_pairs={{0,6},{2,0},{4,2},{6,4},{1,7},{3,1},{5,3},{7,5},{8,14},{10,8},{12,... | collective-permute-start | bytes 196616 | tf_op jit(solution)/shard_map/ppermute | solution.py:425
  79.7 4.7 %collective-permute-start.5 = (f32[32,128]{1,0:T(8,128)S(1)}, f32[32,128]{1,0:T(8,128)S(1)}, u32[]{:S(2)}, u32[]{:S(2)}) collective-permute-start(f32[32,128]{1,0:T(8,128)S(1)} %get-tuple-element.40), channel_id=1, source_target_pairs={{0,64},{64,128},{128,192},{192,0},{1,65},{65,129},{129,193},{193,1... | collective-permute-start | bytes 49160 | tf_op jit(solution)/shard_map/ppermute | solution.py:425
  80.8 5.0 %collective-permute-start.6 = (f32[32,128]{1,0:T(8,128)S(1)}, f32[32,128]{1,0:T(8,128)S(1)}, u32[]{:S(2)}, u32[]{:S(2)}) collective-permute-start(f32[32,128]{1,0:T(8,128)S(1)} %get-tuple-element.41), channel_id=1, source_target_pairs={{0,128},{64,192},{128,0},{192,64},{1,129},{65,193},{129,1},{193,65... | collective-permute-start | bytes 49160 | tf_op jit(solution)/shard_map/ppermute | solution.py:425
  83.8 3.3 %collective-permute-start.7 = (f32[32,128]{1,0:T(8,128)S(1)}, f32[32,128]{1,0:T(8,128)S(1)}, u32[]{:S(2)}, u32[]{:S(2)}) collective-permute-start(f32[32,128]{1,0:T(8,128)S(1)} %get-tuple-element.42), channel_id=1, source_target_pairs={{0,192},{64,0},{128,64},{192,128},{1,193},{65,1},{129,65},{193,129... | collective-permute-start | bytes 49160 | tf_op jit(solution)/shard_map/ppermute | solution.py:425
  119.3 12.3 %collective-permute-start.8 = (f32[16,72,128]{2,1,0:T(8,128)S(1)}, f32[16,72,128]{2,1,0:T(8,128)S(1)}, u32[]{:S(2)}, u32[]{:S(2)}) collective-permute-start(f32[16,72,128]{2,1,0:T(8,128)S(1)} %all_to_all.34.own_ref), channel_id=1, source_target_pairs={{0,1},{1,0},{2,3},{3,2},{4,5},{5,4},{6,7},{7,6},{8,9},{9,8},{10,11... | collective-permute-start | bytes 1769480 | tf_op jit(solution)/shard_map/ppermute | solution.py:460
  123.8 2.3 %collective-permute-start.1 = (bf16[130,16,128]{2,1,0:T(8,128)(2,1)S(1)}, bf16[130,16,128]{2,1,0:T(8,128)(2,1)S(1)}, u32[]{:S(2)}, u32[]{:S(2)}) collective-permute-start(bf16[130,16,128]{2,1,0:T(8,128)(2,1)S(1)} %shard_map.133.own_ref), channel_id=1, source_target_pairs={{0,1},{1,0},{2,3},{3,2},{4,5},{5,4},{6,7},{7,6},{8,9},{9,8},{10,11... | collective-permute-start | bytes 1597448 | tf_op jit(solution)/shard_map/ppermute | solution.py:445

commit v7 on v6

--- a/solution.py
+++ b/solution.py
@@ -201,18 +201,23 @@
         )
 
 
-def pack_kernel(line_ref, keep_ref, came_ref, out_ref, small_ref):
-    out_ref[:, :LINES] = line_ref[...]
+def pack_kernel(line_ref, keep_ref, came_ref, out_ref, small_ref, half_ref, sems):
+    copies = [
+        pltpu.make_async_copy(line_ref, out_ref.at[:, :LINES], sems.at[0]),
+        pltpu.make_async_copy(half_ref, out_ref.at[:, LINES:], sems.at[1]),
+    ]
+    copies[0].start()
     for x in range(4):
         for z in range(8):
             for y in range(4):
                 k = 256 * (z % 4) + 16 * (4 * x + y) + 4 * (z // 4)
                 half = keep_ref[k : k + 4] + came_ref[k : k + 4]
                 high = half.astype(BF).astype(F32)
-                out_ref[(x * 8 + z) * 4 + y, LINES:] = jnp.concatenate(
-                    [high, half - high], axis=0
-                ).astype(BF)
+                half_ref[(x * 8 + z) * 4 + y] = jnp.concatenate([high, half - high], axis=0).astype(BF)
+    copies[1].start()
     small_ref[...] = keep_ref[1024:] + came_ref[1024:]
+    for copy in copies:
+        copy.wait()
 
 
 def chip_kernel(at_ref, keep_ref, came_ref, own_ref, one_ref, two_ref, three_ref, sum_ref):
@@ -257,16 +262,19 @@
         chunk_ref[k, 40:] = last
 
 
-def column_kernel(got_ref, out_ref):
+def column_kernel(got_ref, out_ref, column_ref, sems):
     total = got_ref[0, :40]
     for z in range(1, 8):
         total = total + got_ref[z, :40]
     tiles = [
         jnp.concatenate([got_ref[q, 40:44], got_ref[q + 4, 40:44]], axis=0) for q in range(4)
     ]
-    column = jnp.concatenate(tiles + [total], axis=0)
-    for p in range(16):
-        out_ref[p] = column
+    column_ref[...] = jnp.concatenate(tiles + [total], axis=0)
+    copies = [pltpu.make_async_copy(column_ref, out_ref.at[p], sems.at[p]) for p in range(16)]
+    for copy in copies:
+        copy.start()
+    for copy in copies:
+        copy.wait()
 
 
 def place_kernel(
@@ -417,6 +425,8 @@
         pack_kernel, 12,
         (sds((OWNERS, LINES + 8, EMB), BF), sds((SMALL, EMB), F32)),
         [VMEM] * 3,
+        [pltpu.VMEM((OWNERS, 8, EMB), BF), pltpu.SemaphoreType.DMA((2,))],
+        out_specs=(HBM, VMEM),
     )(lines, keep, came)
     got = exchange(message, TABLE)
 
@@ -455,7 +465,11 @@
         ],
         out_specs=(ANY,),
     )(core, incoming, other)
-    (sums,) = call(column_kernel, 12, (sds((16, 64 + SMALL, EMB), F32),), [VMEM])(column)
+    (sums,) = call(
+        column_kernel, 12, (sds((16, 64 + SMALL, EMB), F32),), [VMEM],
+        [pltpu.VMEM((64 + SMALL, EMB), F32), pltpu.SemaphoreType.DMA((16,))],
+        out_specs=(HBM,),
+    )(column)
     mine = exchange(sums, ("x", "y"))
     theirs = lax.ppermute(mine, "dp", swap)
     tile = sds((8, EMB), F32)

time: 133 us -> 134 us (level)
  no operation moved by 1% of the time
where the time goes in v7:
time: 134 us
  blocking collectives  74.2 us (55%)
  starting transfers between devices  24.7 us (18%)
  Pallas kernels  18.1 us (14%)
  waiting for transfers between devices  15.8 us (12%)
    all_to_all x4, blocking collectives, exchange(): return lax.all_to_all(array, axes, split_axis=0, concat_axis=0, tiled=True)  74.2 us
    ppermute x6, starting transfers between devices, spread(): lax.ppermute(part, axis, [(i, (i + d) % 4) for i in range(4)])  8.96 us
    ppermute x6, waiting for transfers between devices, spread(): lax.ppermute(part, axis, [(i, (i + d) % 4) for i in range(4)])  6.97 us
    all_to_all x1, starting transfers between devices, exchange(): return lax.all_to_all(array, axes, split_axis=0, concat_axis=0, tiled=True)  6.66 us
    all_to_all x1, waiting for transfers between devices, exchange(): return lax.all_to_all(array, axes, split_axis=0, concat_axis=0, tiled=True)  6.11 us
    pallas_call x1, Pallas kernels, whole_step(): call(place_kernel, 28, (sds((TABLES, ROWS // 2, EMB), F32),), [SMEM] + [V...  5.35 us
    ppermute x1, starting transfers between devices, whole_step(): theirs = lax.ppermute(mine, 'dp', swap)  4.51 us
    ppermute x1, starting transfers between devices, whole_step(): came = lax.ppermute(send, 'dp', swap)  4.47 us
  transfers between devices with their start and end apart: 10, of which 8 were waited for; matrix products, arithmetic and copies ran while one was open for 0% of the time, Pallas kernels for 5%

profile of v7, /device:TPU:1, one launch (start us, length us, event | category | flops | bytes accessed | tf_op | source)
XLA Modules:
  0.0 133.6 jit_solution(14075721875952841918)
XLA Ops:
  0.6 0.0 copy-start
  0.6 0.0 copy-start.2
  0.7 0.0 copy-start.1
  0.7 0.0 copy-start.5
  0.7 0.0 copy-start.4
  0.7 0.0 copy-start.3
  0.7 1.9 %shard_map.128 = (s32[128,16]{1,0:T(8,128)S(1)}, s32[4,256]{1,0:T(4,128)S(1)}, s32[256,8]{1,0:T(8,128)S(1)}) custom-call(s32[1]{0:T(128)} %bitcast.core_ref, s32[8,128]{1,0:T(8,128)} %bitcast.20, s32[4,256]{1,0:T(4,128)} %bitcast.21), custom_call_target="tpu_custom_call" | custom-call | flops 268435456 | bytes 1048576 | tf_op jit(solution)/shard_map/pallas_call | solution.py:388
  2.6 26.7 %all_to_all.31 = s32[128,1,16]{2,1,0:T(1,128)S(1)} all-to-all(s32[128,1,16]{2,1,0:T(1,128)S(1)} %bitcast.17), channel_id=1, replica_groups=mesh['x'=4,'z'=8,'y'=4,'dp'=2] {'x','z','y'}, dimensions={0} | all-to-all | bytes 16384 | tf_op jit(solution)/shard_map/all_to_all | solution.py:379
  29.3 4.3 %shard_map.129 = bf16[128,16,128]{2,1,0:T(8,128)(2,1)S(1)} custom-call(s32[128,16]{1,0:T(8,128)S(1)} %bitcast.15, bf16[4,4096,128]{2,1,0:T(8,128)(2,1)} %far_ref.1), custom_call_target="tpu_custom_call" | custom-call | flops 268435456 | bytes 1048576 | tf_op jit(solution)/shard_map/pallas_call | solution.py:399
  33.6 21.5 %all_to_all.32.ret_ref = bf16[128,16,128]{2,1,0:T(8,128)(2,1)S(1)} all-to-all(bf16[128,16,128]{2,1,0:T(8,128)(2,1)S(1)} %shard_map.129), channel_id=1, replica_groups=mesh['x'=4,'z'=8,'y'=4,'dp'=2] {'x','z','y'}, dimensions={0} | all-to-all | bytes 1048576 | tf_op jit(solution)/shard_map/all_to_all | solution.py:379
  55.1 0.0 copy-done
  55.1 0.0 copy-done.2
  55.1 0.0 copy-done.1
  55.1 0.0 copy-done.5
  55.1 0.0 copy-done.4
  55.1 0.0 copy-done.3
  55.1 2.2 %shard_map.130 = (bf16[256,512]{1,0:T(8,128)(2,1)S(1)}, f32[1032,128]{1,0:T(8,128)S(1)}, f32[1032,128]{1,0:T(8,128)S(1)}) custom-call(s32[1]{0:T(128)} %bitcast.core_ref, bf16[128,16,128]{2,1,0:T(8,128)(2,1)S(1)} %all_to_all.32.ret_ref, s32[256,8]{1,0:T(8,128)S(1)} %get-tuple-element.28.slot_col_ref, s32[1,256]{1,0:T(1,128)S(1)} %copy-done.3, ...), custom_call_target="tpu_custom_call" | custom-call | flops 268435456 | bytes 1048576 | tf_op jit(solution)/shard_map/pallas_call | solution.py:411
  57.3 4.5 %collective-permute-start = (f32[1032,128]{1,0:T(8,128)S(1)}, f32[1032,128]{1,0:T(8,128)S(1)}, u32[]{:S(2)}, u32[]{:S(2)}) collective-permute-start(f32[1032,128]{1,0:T(8,128)S(1)} %get-tuple-element.32), channel_id=1, source_target_pairs={{0,1},{1,0},{2,3},{3,2},{4,5},{5,4},{6,7},{7,6},{8,9},{9,8},{10,11... | collective-permute-start | bytes 1585160 | tf_op jit(solution)/shard_map/ppermute | solution.py:420
  61.8 1.0 shard_map.131.line_ref
  62.8 0.5 collective-permute-done.came_ref
  63.4 0.9 shard_map.132
  64.3 6.7 %all-to-all-start.2 = ((bf16[128,24,128]{2,1,0:T(8,128)(2,1)}), bf16[128,24,128]{2,1,0:T(8,128)(2,1)S(1)}, u32[]{:S(2)}, u32[]{:S(2)}) async-start(bf16[128,24,128]{2,1,0:T(8,128)(2,1)} %get-tuple-element.33), calls=%async_computation.2 | async-start | bytes 1572864 | tf_op jit(solution)/shard_map/all_to_all | solution.py:379
  70.9 0.1 shard_map.135
  71.0 0.7 collective-permute-start.2
  71.6 2.4 %collective-permute-start.3 = (f32[128,128]{1,0:T(8,128)S(1)}, f32[128,128]{1,0:T(8,128)S(1)}, u32[]{:S(2)}, u32[]{:S(2)}) collective-permute-start(f32[128,128]{1,0:T(8,128)S(1)} %get-tuple-element.37), channel_id=1, source_target_pairs={{0,4},{2,6},{4,0},{6,2},{1,5},{3,7},{5,1},{7,3},{8,12},{10,14},{12... | collective-permute-start | bytes 196616 | tf_op jit(solution)/shard_map/ppermute | solution.py:435
  74.0 1.2 collective-permute-start.4
  75.2 0.7 collective-permute-done.2.a_ref
  76.0 2.6 %collective-permute-done.3.b_ref = f32[128,128]{1,0:T(8,128)S(1)} collective-permute-done((f32[128,128]{1,0:T(8,128)S(1)}, f32[128,128]{1,0:T(8,128)S(1)}, u32[]{:S(2)}, u32[]{:S(2)}) %collective-permute-start.3) | collective-permute-done | bytes 65568 | tf_op jit(solution)/shard_map/ppermute | solution.py:435
  78.6 1.0 collective-permute-done.4.c_ref
  79.6 1.1 collective-permute-start.5
  80.7 3.0 %collective-permute-start.6 = (f32[32,128]{1,0:T(8,128)S(1)}, f32[32,128]{1,0:T(8,128)S(1)}, u32[]{:S(2)}, u32[]{:S(2)}) collective-permute-start(f32[32,128]{1,0:T(8,128)S(1)} %get-tuple-element.41), channel_id=1, source_target_pairs={{0,128},{64,192},{128,0},{192,64},{1,129},{65,193},{129,1},{193,65... | collective-permute-start | bytes 49160 | tf_op jit(solution)/shard_map/ppermute | solution.py:435
  83.7 0.6 collective-permute-start.7
  84.3 0.0 collective-permute-done.5.a_ref
  84.3 1.4 %collective-permute-done.6.b_ref = f32[32,128]{1,0:T(8,128)S(1)} collective-permute-done((f32[32,128]{1,0:T(8,128)S(1)}, f32[32,128]{1,0:T(8,128)S(1)}, u32[]{:S(2)}, u32[]{:S(2)}) %collective-permute-start.6) | collective-permute-done | bytes 16416 | tf_op jit(solution)/shard_map/ppermute | solution.py:435
  85.7 1.2 collective-permute-done.7.c_ref
  87.0 6.1 %all-to-all-done.2.got_ref = bf16[128,24,128]{2,1,0:T(8,128)(2,1)S(1)} async-done(((bf16[128,24,128]{2,1,0:T(8,128)(2,1)}), bf16[128,24,128]{2,1,0:T(8,128)(2,1)S(1)}, u32[]{:S(2)}, u32[]{:S(2)}) %all-to-all-start.2) | async-done | bytes 786464 | tf_op jit(solution)/shard_map/all_to_all | solution.py:379
  93.1 13.9 %all_to_all.33.got_ref = f32[8,48,128]{2,1,0:T(8,128)S(1)} all-to-all(f32[8,48,128]{2,1,0:T(8,128)S(1)} %shard_map.138), channel_id=1, replica_groups=mesh['x'=4,'z'=8,'y'=4,'dp'=2] {'z'}, dimensions={0} | all-to-all | bytes 393216 | tf_op jit(solution)/shard_map/all_to_all | solution.py:379
  107.0 0.9 shard_map.139
  108.0 12.1 %all_to_all.34.own_ref = f32[16,72,128]{2,1,0:T(8,128)S(1)} all-to-all(f32[16,72,128]{2,1,0:T(8,128)S(1)} %shard_map.139), channel_id=1, replica_groups=mesh['x'=4,'z'=8,'y'=4,'dp'=2] {'x','y'}, dimensions={0} | all-to-all | bytes 1179648 | tf_op jit(solution)/shard_map/all_to_all | solution.py:379
  120.0 4.5 %collective-permute-start.8 = (f32[16,72,128]{2,1,0:T(8,128)S(1)}, f32[16,72,128]{2,1,0:T(8,128)S(1)}, u32[]{:S(2)}, u32[]{:S(2)}) collective-permute-start(f32[16,72,128]{2,1,0:T(8,128)S(1)} %all_to_all.34.own_ref), channel_id=1, source_target_pairs={{0,1},{1,0},{2,3},{3,2},{4,5},{5,4},{6,7},{7,6},{8,9},{9,8},{10,11... | collective-permute-start | bytes 1769480 | tf_op jit(solution)/shard_map/ppermute | solution.py:474
  124.5 0.1 shard_map.133.own_ref
  124.6 0.1 collective-permute-start.1
  124.7 2.2 %collective-permute-done.1.other_ref = bf16[130,16,128]{2,1,0:T(8,128)(2,1)S(1)} collective-permute-done((bf16[130,16,128]{2,1,0:T(8,128)(2,1)S(1)}, bf16[130,16,128]{2,1,0:T(8,128)(2,1)S(1)}, u32[]{:S(2)}, u32[]{:S(2)}) %collective-permute-start.1) | collective-permute-done | bytes 532512 | tf_op jit(solution)/shard_map/ppermute | solution.py:455
  126.9 5.3 %shard_map.134 = f32[4,2048,128]{2,1,0:T(8,128)} custom-call(s32[1]{0:T(128)} %bitcast.core_ref, bf16[130,16,128]{2,1,0:T(8,128)(2,1)S(1)} %shard_map.133.own_ref, bf16[130,16,128]{2,1,0:T(8,128)(2,1)S(1)} %collective-permute-done.1.other_ref), custom_call_target="tpu_custom_call" | custom-call | flops 268435456 | bytes 1048576 | tf_op jit(solution)/shard_map/pallas_call | solution.py:457
  132.3 0.1 shard_map.140
  132.3 0.0 collective-permute-done.8.other_ref
  132.4 1.3 shard_map.141
  (3 shorter events, 0.1 us)
Async XLA Ops:
  0.6 54.5 %copy-start = (f32[512,512]{1,0:T(8,128)S(1)}, f32[512,512]{1,0:T(8,128)}, u32[]{:S(2)}) copy-start(f32[512,512]{1,0:T(8,128)} %w_ref.3) | copy-start | bytes 3145732
  0.6 54.5 %copy-start.2 = (f32[512]{0:T(512)S(1)}, f32[512]{0:T(512)}, u32[]{:S(2)}) copy-start(f32[512]{0:T(512)} %param.17) | copy-start | bytes 6148
  0.7 54.5 %copy-start.1 = (f32[512]{0:T(512)S(1)}, f32[512]{0:T(512)}, u32[]{:S(2)}) copy-start(f32[512]{0:T(512)} %param.16) | copy-start | bytes 6148
  0.7 54.5 %copy-start.5 = (f32[1,256]{1,0:T(1,128)S(1)}, f32[1,256]{1,0:T(1,128)}, u32[]{:S(2)}) copy-start(f32[1,256]{1,0:T(1,128)} %lb_ref.1) | copy-start | bytes 3076
  0.7 54.5 %copy-start.4 = (f32[1,256]{1,0:T(1,128)S(1)}, f32[1,256]{1,0:T(1,128)}, u32[]{:S(2)}) copy-start(f32[1,256]{1,0:T(1,128)} %rel_ref.1) | copy-start | bytes 3076
  0.7 54.5 %copy-start.3 = (s32[1,256]{1,0:T(1,128)S(1)}, s32[1,256]{1,0:T(1,128)}, u32[]{:S(2)}) copy-start(s32[1,256]{1,0:T(1,128)} %ses_ref.1) | copy-start | bytes 3076
  57.3 6.0 %collective-permute-start = (f32[1032,128]{1,0:T(8,128)S(1)}, f32[1032,128]{1,0:T(8,128)S(1)}, u32[]{:S(2)}, u32[]{:S(2)}) collective-permute-start(f32[1032,128]{1,0:T(8,128)S(1)} %get-tuple-element.32), channel_id=1, source_target_pairs={{0,1},{1,0},{2,3},{3,2},{4,5},{5,4},{6,7},{7,6},{8,9},{9,8},{10,11... | collective-permute-start | bytes 1585160 | tf_op jit(solution)/shard_map/ppermute | solution.py:420
  64.3 28.8 %all-to-all-start.2 = ((bf16[128,24,128]{2,1,0:T(8,128)(2,1)}), bf16[128,24,128]{2,1,0:T(8,128)(2,1)S(1)}, u32[]{:S(2)}, u32[]{:S(2)}) async-start(bf16[128,24,128]{2,1,0:T(8,128)(2,1)} %get-tuple-element.33), calls=%async_computation.2 | async-start | bytes 1572864 | tf_op jit(solution)/shard_map/all_to_all | solution.py:379
  71.0 5.0 %collective-permute-start.2 = (f32[128,128]{1,0:T(8,128)S(1)}, f32[128,128]{1,0:T(8,128)S(1)}, u32[]{:S(2)}, u32[]{:S(2)}) collective-permute-start(f32[128,128]{1,0:T(8,128)S(1)} %get-tuple-element.36), channel_id=1, source_target_pairs={{0,2},{2,4},{4,6},{6,0},{1,3},{3,5},{5,7},{7,1},{8,10},{10,12},{12... | collective-permute-start | bytes 196616 | tf_op jit(solution)/shard_map/ppermute | solution.py:435
  71.6 7.0 %collective-permute-start.3 = (f32[128,128]{1,0:T(8,128)S(1)}, f32[128,128]{1,0:T(8,128)S(1)}, u32[]{:S(2)}, u32[]{:S(2)}) collective-permute-start(f32[128,128]{1,0:T(8,128)S(1)} %get-tuple-element.37), channel_id=1, source_target_pairs={{0,4},{2,6},{4,0},{6,2},{1,5},{3,7},{5,1},{7,3},{8,12},{10,14},{12... | collective-permute-start | bytes 196616 | tf_op jit(solution)/shard_map/ppermute | solution.py:435
  74.0 5.5 %collective-permute-start.4 = (f32[128,128]{1,0:T(8,128)S(1)}, f32[128,128]{1,0:T(8,128)S(1)}, u32[]{:S(2)}, u32[]{:S(2)}) collective-permute-start(f32[128,128]{1,0:T(8,128)S(1)} %get-tuple-element.38), channel_id=1, source_target_pairs={{0,6},{2,0},{4,2},{6,4},{1,7},{3,1},{5,3},{7,5},{8,14},{10,8},{12,... | collective-permute-start | bytes 196616 | tf_op jit(solution)/shard_map/ppermute | solution.py:435
  79.6 4.7 %collective-permute-start.5 = (f32[32,128]{1,0:T(8,128)S(1)}, f32[32,128]{1,0:T(8,128)S(1)}, u32[]{:S(2)}, u32[]{:S(2)}) collective-permute-start(f32[32,128]{1,0:T(8,128)S(1)} %get-tuple-element.40), channel_id=1, source_target_pairs={{0,64},{64,128},{128,192},{192,0},{1,65},{65,129},{129,193},{193,1... | collective-permute-start | bytes 49160 | tf_op jit(solution)/shard_map/ppermute | solution.py:435
  80.7 5.0 %collective-permute-start.6 = (f32[32,128]{1,0:T(8,128)S(1)}, f32[32,128]{1,0:T(8,128)S(1)}, u32[]{:S(2)}, u32[]{:S(2)}) collective-permute-start(f32[32,128]{1,0:T(8,128)S(1)} %get-tuple-element.41), channel_id=1, source_target_pairs={{0,128},{64,192},{128,0},{192,64},{1,129},{65,193},{129,1},{193,65... | collective-permute-start | bytes 49160 | tf_op jit(solution)/shard_map/ppermute | solution.py:435
  83.7 3.3 %collective-permute-start.7 = (f32[32,128]{1,0:T(8,128)S(1)}, f32[32,128]{1,0:T(8,128)S(1)}, u32[]{:S(2)}, u32[]{:S(2)}) collective-permute-start(f32[32,128]{1,0:T(8,128)S(1)} %get-tuple-element.42), channel_id=1, source_target_pairs={{0,192},{64,0},{128,64},{192,128},{1,193},{65,1},{129,65},{193,129... | collective-permute-start | bytes 49160 | tf_op jit(solution)/shard_map/ppermute | solution.py:435
  120.0 12.3 %collective-permute-start.8 = (f32[16,72,128]{2,1,0:T(8,128)S(1)}, f32[16,72,128]{2,1,0:T(8,128)S(1)}, u32[]{:S(2)}, u32[]{:S(2)}) collective-permute-start(f32[16,72,128]{2,1,0:T(8,128)S(1)} %all_to_all.34.own_ref), channel_id=1, source_target_pairs={{0,1},{1,0},{2,3},{3,2},{4,5},{5,4},{6,7},{7,6},{8,9},{9,8},{10,11... | collective-permute-start | bytes 1769480 | tf_op jit(solution)/shard_map/ppermute | solution.py:474
  124.6 2.3 %collective-permute-start.1 = (bf16[130,16,128]{2,1,0:T(8,128)(2,1)S(1)}, bf16[130,16,128]{2,1,0:T(8,128)(2,1)S(1)}, u32[]{:S(2)}, u32[]{:S(2)}) collective-permute-start(bf16[130,16,128]{2,1,0:T(8,128)(2,1)S(1)} %shard_map.133.own_ref), channel_id=1, source_target_pairs={{0,1},{1,0},{2,3},{3,2},{4,5},{5,4},{6,7},{7,6},{8,9},{9,8},{10,11... | collective-permute-start | bytes 1597448 | tf_op jit(solution)/shard_map/ppermute | solution.py:455
